TPU v7x, 32 devices: a whole 2x2x4 slice. The times are simulated.
32 devices in a mesh: rep: 4 (over z), own: 8 (over y, x, core).
Axes of the slice: x: 2, y: 2, z: 4, core: 2. Of those that a mesh axis runs over, the one named last changes fastest.
Arguments:
- grads: float32 [16, 576, 1024], P('rep', 'own'), may hold values from -60 to 60
- momentum: bfloat16 [32, 576, 1024], P(('rep', 'own')), may hold values from -6 to 6
- owner_table: int32 [4, 8], replicated, may hold values from 0 to 7, each once within a row
Outputs:
- new_momentum: bfloat16 [32, 576, 1024], P(('rep', 'own'))
- updates: bfloat16 [16, 576, 1024], P(None, 'own')
Inputs may be any that keep to these rules, and one draw needn't show every extreme that they name: Each row of owner_table is a permutation of 0 to 7; entries of 4 or more mark empty slots.
All inputs are finite; a program needn't handle non-finite values.
Results may differ from a plain program's by a relative error of at most 0.01.
Values may be sent and summed in bfloat16 or wider, within the bound.
No kernel may reach another device: no remote copies, remote signals or barrier semaphores. Data moves between devices by JAX's collectives and lax.ppermute only.
A program may use at most 128 MiB of HBM per device.

v0:
```python
import math

import jax
import jax.numpy as jnp
from jax import lax
from jax.sharding import PartitionSpec as P

ITERS = 2


DECAY = 0.95
COEF_A = 3.4445
COEF_B = -4.775
COEF_C = 2.0315
EPSILON = 1e-07


def orthogonalize(blend):
    total = jnp.sqrt(jnp.sum(blend * blend))
    iterate = (blend / (total + EPSILON)).astype(jnp.bfloat16)
    factor = 0.2 * math.sqrt(max(blend.shape[0], blend.shape[1]))
    result = None
    for turn in range(ITERS):
        gram = jnp.dot(iterate, iterate.T, preferred_element_type=jnp.float32).astype(jnp.bfloat16)
        square = jnp.dot(gram, gram, preferred_element_type=jnp.float32)
        poly = (COEF_B * gram.astype(jnp.float32) + COEF_C * square).astype(jnp.bfloat16)
        mixed = COEF_A * iterate.astype(jnp.float32) + jnp.dot(
            poly, iterate, preferred_element_type=jnp.float32
        )
        if turn + 1 < ITERS:
            iterate = mixed.astype(jnp.bfloat16)
        else:
            result = (factor * mixed).astype(jnp.bfloat16)
    return result


def body(grads, momentum, owner_table):
    group = lax.axis_index("rep")
    slot_matrix = lax.dynamic_index_in_dim(owner_table, group, 0, keepdims=False)
    matrix_count, shard_rows, columns = grads.shape
    is_live = slot_matrix < matrix_count
    clamped = jnp.minimum(slot_matrix, matrix_count - 1)
    half_grads = grads.astype(jnp.bfloat16)
    outgoing = jnp.take(half_grads, clamped, axis=0) * is_live[:, None, None].astype(jnp.bfloat16)
    incoming = lax.all_to_all(outgoing, "own", split_axis=0, concat_axis=1, tiled=True)
    gradient = incoming[0].astype(jnp.float32)
    moment = DECAY * momentum[0].astype(jnp.float32) + gradient
    new_momentum = moment.astype(jnp.bfloat16)[None]
    update = orthogonalize(gradient + DECAY * moment)
    returned = lax.all_to_all(update[None], "own", split_axis=1, concat_axis=0, tiled=True)
    holders = jnp.argsort(slot_matrix)[:matrix_count]
    grouped = jnp.take(returned, holders, axis=0)
    updates = lax.all_gather(grouped, "rep", axis=0, tiled=True)
    return (new_momentum, updates)


def solution(mesh):
    in_specs = (P("rep", "own", None), P(("rep", "own"), None, None), P())
    out_specs = (P(("rep", "own"), None, None), P(None, "own", None))
    return jax.shard_map(body, mesh=mesh, in_specs=in_specs, out_specs=out_specs, check_vma=False)
```

profile of v0, /device:TPU:0, one launch (start us, length us, event | category | flops | bytes accessed | tf_op | source)
XLA Modules:
  0.0 138.9 jit_solution(14850939103805925869)
XLA Ops:
  7.2 0.7 compare_convert_fusion
  7.9 0.7 fusion.10
  8.6 1.4 convert_element_type.90
  9.9 0.6 gather_fusion
  10.6 0.2 select_multiply_fusion
  10.8 21.7 %all_to_all.21 = bf16[8,72,1024]{2,1,0:T(8,128)(2,1)S(1)} all-to-all(bf16[8,72,1024]{2,1,0:T(8,128)(2,1)S(1)} %select_multiply_fusion), channel_id=1, replica_groups=mesh['rep'=4,'own'=8] {'own'}, dimensions={0} | all-to-all | bytes 2359296 | tf_op jit(solution)/shard_map/all_to_all | solution.py:45
  32.5 0.0 copy-start
  32.5 0.3 convert_element_type.111
  32.8 1.0 copy-done
  33.8 1.5 %convert_multiply_fusion = (f32[1,576,1024]{2,1,0:T(8,128)S(1)}, bf16[1,576,1024]{2,1,0:T(8,128)(2,1)}) fusion(bf16[1,576,1024]{2,1,0:T(8,128)(2,1)S(1)} %copy-done, f32[1,576,1024]{2,1,0:T(8,128)S(1)} %bitcast.46), kind=kLoop, calls=%fused_computation.13 | loop fusion | flops 2359296 | bytes 7077888 | tf_op jit(solution)/shard_map/mul | solution.py:47
  35.3 1.2 multiply_reduce_fusion
  37.2 0.5 divide_convert_fusion
  37.7 0.0 copy-start.1
  37.7 1.1 convolution_convert_fusion.1
  38.8 0.1 copy-done.1
  39.0 0.6 fusion.4
  39.6 1.7 %add_convert_fusion = bf16[576,1024]{1,0:T(8,128)(2,1)S(1)} fusion(bf16[576,1024]{1,0:T(8,128)(2,1)S(1)} %fusion.4, bf16[576,576]{1,0:T(8,128)(2,1)S(1)} %convolution_convert_fusion.1), kind=kOutput, calls=%fused_computation.9 | convolution fusion | flops 1065701376 | bytes 3022848 | tf_op jit(solution)/shard_map/dot_general | solution.py:27
  41.3 1.1 convolution_convert_fusion
  42.4 1.7 %fusion.5 = bf16[1,576,1024]{2,1,0:T(8,128)(2,1)S(1)} fusion(bf16[576,1024]{1,0:T(8,128)(2,1)S(1)} %add_convert_fusion, bf16[576,576]{1,0:T(8,128)(2,1)S(1)} %convolution_convert_fusion), kind=kOutput, calls=%fused_computation.17 | convolution fusion | flops 1066291200 | bytes 3022848 | tf_op jit(solution)/shard_map/dot_general | solution.py:27
  44.1 1.8 %copy.9 = bf16[1,576,1024]{2,0,1:T(2,128)(2,1)S(1)} copy(bf16[1,576,1024]{2,1,0:T(8,128)(2,1)S(1)} %fusion.5) | data formatting | bytes 2359296 | tf_op jit(solution)/shard_map/broadcast_in_dim | solution.py:50
  46.0 0.5 broadcast.140
  46.5 7.7 %reduce.3 = bf16[576,1024]{1,0:T(8,128)(2,1)S(1)} reduce(bf16[576,1,1024]{2,1,0:T(2,128)(2,1)S(1)} %bitcast.47, bf16[]{:T(256)} %broadcast.140), dimensions={1}, to_apply=%bitcast.43.reduce_sub_computation | reduce | bytes 2359298
  54.2 1.6 %reshape.107 = bf16[8,2,36864]{2,1,0:T(2,128)(2,1)} reshape(bf16[576,1024]{1,0:T(8,128)(2,1)S(1)} %reduce.3) | data formatting | bytes 2359296
  55.8 3.6 %all-to-all-start.1 = ((bf16[8,2,36864]{2,1,0:T(2,128)(2,1)}), bf16[8,2,36864]{2,1,0:T(2,128)(2,1)S(1)}, u32[]{:S(2)}, u32[]{:S(2)}) async-start(bf16[8,2,36864]{2,1,0:T(2,128)(2,1)} %reshape.107), calls=%async_computation.1 | async-start | bytes 2359296 | tf_op jit(solution)/shard_map/all_to_all | solution.py:50
  59.4 0.0 all-gather.2.cloned.1.call-start
  59.4 1.0 sort.17
  60.5 15.6 %all-to-all-done.1 = bf16[8,2,36864]{2,1,0:T(2,128)(2,1)S(1)} async-done(((bf16[8,2,36864]{2,1,0:T(2,128)(2,1)}), bf16[8,2,36864]{2,1,0:T(2,128)(2,1)S(1)}, u32[]{:S(2)}, u32[]{:S(2)}) %all-to-all-start.1) | async-done | bytes 1179680 | tf_op jit(solution)/shard_map/all_to_all | solution.py:50
  76.1 1.1 reshape.108
  77.2 0.4 copy.7
  77.7 0.6 gather_fusion.1
  78.3 0.9 broadcast_select_fusion
  79.2 0.0 all-gather.2.cloned.1.call-update
  79.2 49.5 %all-gather.2.cloned.1.call-done = bf16[16,72,1024]{2,1,0:T(8,128)(2,1)} async-done(((bf16[4,72,1024]{2,1,0:T(8,128)(2,1)}), bf16[16,72,1024]{2,1,0:T(8,128)(2,1)}) %all-gather.2.cloned.1.call-update) | async-done | bytes 2359312 | tf_op jit(solution)/shard_map/all_gather | solution.py:53
  128.8 3.3 %copy.11 = bf16[16,72,1024]{2,1,0:T(8,128)(2,1)} copy(bf16[16,72,1024]{2,1,0:T(8,128)(2,1)} %all-gather.2.cloned.1.call-done) | data formatting | bytes 4718592
  (5 shorter events, 0.0 us)
Async XLA Ops:
  32.5 1.3 copy-start
  37.7 1.3 copy-start.1
  55.8 20.3 %all-to-all-start.1 = ((bf16[8,2,36864]{2,1,0:T(2,128)(2,1)}), bf16[8,2,36864]{2,1,0:T(2,128)(2,1)S(1)}, u32[]{:S(2)}, u32[]{:S(2)}) async-start(bf16[8,2,36864]{2,1,0:T(2,128)(2,1)} %reshape.107), calls=%async_computation.1 | async-start | bytes 2359296 | tf_op jit(solution)/shard_map/all_to_all | solution.py:50
  59.4 69.4 %all-gather.2.cloned.1.call-start = ((), (), s32[]{:S(2)}) async-start(), calls=%async_computation.2 | async-start | bytes 2949120 | tf_op jit(solution)/shard_map/all_gather | solution.py:53
Sparse Core Ops, SparseCore 0:
  79.4 49.3 all-gather.1
where the time goes:
time: 139 us
  waiting for transfers between devices  65.1 us (47%)
  blocking collectives  21.7 us (16%)
  other arithmetic  16.7 us (12%)
  between operations  14.9 us (11%)
  local copies, waits for them, and re-layouts  11.1 us (8%)
  matrix products  5.68 us (4%)
  starting transfers between devices  3.61 us (3%)
    all_gather x1, waiting for transfers between devices, body(): updates = lax.all_gather(grouped, 'rep', axis=0, tiled=True)  49.5 us
    all_to_all x1, blocking collectives, body(): lax.all_to_all(outgoing, 'own', split_axis=0, concat_axis=1, tiled=True)  21.7 us
    all_to_all x1, waiting for transfers between devices, body(): lax.all_to_all(update[None], 'own', split_axis=1, concat_axis=0, tiled=True)  15.6 us
    unnamed x9, local copies, waits for them, and re-layouts  8.11 us
    unnamed x1, other arithmetic  7.72 us
    all_to_all x1, starting transfers between devices, body(): lax.all_to_all(update[None], 'own', split_axis=1, concat_axis=0, tiled=True)  3.56 us
    dot_general x2, matrix products, orthogonalize(): jnp.dot(poly, iterate, preferred_element_type=jnp.float32)  3.45 us
  transfers between devices with their start and end apart: 2, of which 2 were waited for; matrix products, arithmetic and copies ran while one was open for 1% of the time, Pallas kernels for 0%

commit v1 on v0

--- a/solution.py
+++ b/solution.py
@@ -1,18 +1,39 @@
+import functools
 import math
 
 import jax
 import jax.numpy as jnp
 from jax import lax
+from jax.experimental import pallas as pl
+from jax.experimental.pallas import tpu as pltpu
 from jax.sharding import PartitionSpec as P
 
+
 ITERS = 2
-
+CHUNKS = 2
 
 DECAY = 0.95
 COEF_A = 3.4445
 COEF_B = -4.775
 COEF_C = 2.0315
 EPSILON = 1e-07
+
+
+VMEM = pl.BlockSpec(memory_space=pltpu.VMEM)
+SMEM = pl.BlockSpec(memory_space=pltpu.SMEM)
+ANY = pl.BlockSpec(memory_space=pl.ANY)
+
+
+def limit(mib):
+    return pltpu.CompilerParams(vmem_limit_bytes=mib * 2**20)
+
+
+def near(x):
+    return pltpu.with_memory_space_constraint(x, pltpu.VMEM)
+
+
+def far(x):
+    return pltpu.with_memory_space_constraint(x, pltpu.HBM)
 
 
 def orthogonalize(blend):
@@ -34,10 +55,10 @@
     return result
 
 
-def body(grads, momentum, owner_table):
+def general_body(grads, momentum, owner_table):
     group = lax.axis_index("rep")
     slot_matrix = lax.dynamic_index_in_dim(owner_table, group, 0, keepdims=False)
-    matrix_count, shard_rows, columns = grads.shape
+    matrix_count, _, _ = grads.shape
     is_live = slot_matrix < matrix_count
     clamped = jnp.minimum(slot_matrix, matrix_count - 1)
     half_grads = grads.astype(jnp.bfloat16)
@@ -54,7 +75,274 @@
     return (new_momentum, updates)
 
 
+def send_order(own):
+    if own == 8:
+        return [6, 7, 2, 4, 3, 5, 1]
+    return list(range(own - 1, 0, -1))
+
+
+def partner(kind, z, reps):
+    other = z ^ 1 if kind == 0 else z + 1 if z % 2 else z - 1
+    return other if 0 <= other < reps else None
+
+
+def line_pairs(kind, reps, own):
+    pairs = []
+    for z in range(reps):
+        other = partner(kind, z, reps)
+        for o in range(own):
+            pairs.append((z * own + o, (z if other is None else other) * own + (o ^ (other is None))))
+    return pairs
+
+
+def source_of(stream, step, z):
+    return z + step * (1 - 2 * ((z + stream + step + 1) % 2))
+
+
+def line_steps(reps):
+    return [
+        (stream, step)
+        for step in range(1, reps)
+        for stream in (0, 1)
+        if any(0 <= source_of(stream, step, z) < reps for z in range(reps))
+    ]
+
+
+def pack_kernel(table_hbm, grads_hbm, *refs):
+    *outs, table, grads, table_sem, sems = refs
+    group, me = lax.axis_index("rep"), lax.axis_index("own")
+    count = grads.shape[0]
+    flights = [pltpu.make_async_copy(table_hbm, table, table_sem)]
+    flights += [pltpu.make_async_copy(grads_hbm.at[k], grads.at[k], sems.at[k]) for k in range(count)]
+    for flight in flights:
+        flight.start()
+    for flight in flights:
+        flight.wait()
+    for d, out in enumerate(outs):
+        matrix = table[group, me ^ d]
+
+        @pl.when(matrix < count)
+        def _():
+            out[...] = grads[jnp.minimum(matrix, count - 1)].astype(jnp.bfloat16)
+
+        @pl.when(matrix >= count)
+        def _():
+            out[...] = jnp.zeros(out.shape, out.dtype)
+
+
+def mix_block(me, d, at, block, momentum, staged, stage_at, new_momentum, sem, blend):
+    rows, columns = block.shape
+    gradient = block[...].astype(jnp.float32)
+    moment = DECAY * momentum[me ^ d].astype(jnp.float32) + gradient
+    staged[stage_at] = moment.astype(jnp.bfloat16)
+    flight = pltpu.make_async_copy(staged.at[stage_at], new_momentum.at[me ^ d], sem)
+    flight.start()
+    mix = gradient + DECAY * moment
+    blend[at * rows : (at + 1) * rows, :] = mix.astype(jnp.bfloat16)
+    return jnp.sum((mix * mix).reshape(rows // 8, 8, columns), axis=0), flight
+
+
+def mix_kernel(order, *refs):
+    blocks, momentum = refs[: len(order)], refs[len(order)]
+    new_momentum, blend, squares = refs[len(order) + 1 : len(order) + 4]
+    staged, sems = refs[-2:]
+    me = lax.axis_index("own")
+    total, flights = jnp.zeros(squares.shape, jnp.float32), []
+    for i, d in enumerate(order):
+        part, flight = mix_block(me, d, i, blocks[i], momentum, staged, i, new_momentum, sems.at[i], blend)
+        total += part
+        flights.append(flight)
+    squares[...] = total
+    for flight in flights:
+        flight.wait()
+
+
+def update_kernel(order, first, chunks, *refs):
+    late = order[first:]
+    blocks, refs = refs[: len(late)], refs[len(late) :]
+    momentum, squares = refs[0], refs[3]
+    new_momentum, blend = refs[4:6]
+    outs = refs[6 : 6 + len(order) * chunks]
+    iterate, staged, sems = refs[-3:]
+    me = lax.axis_index("own")
+    rows, columns = blocks[0].shape
+    width = columns // chunks
+    sums, flights = squares[...], []
+    for i, d in enumerate(late):
+        part, flight = mix_block(me, d, first + i, blocks[i], momentum, staged, i, new_momentum, sems.at[i], blend)
+        sums += part
+        flights.append(flight)
+    scale = 1.0 / (jnp.sqrt(jnp.sum(sums, keepdims=True)) + EPSILON)
+    factor = 0.2 * math.sqrt(max(rows * len(order), columns))
+    for turn in range(ITERS):
+        y = blend[...] if turn == 0 else iterate[...]
+        gram32 = lax.dot_general(y, y, (((1,), (1,)), ((), ())), preferred_element_type=jnp.float32)
+        if turn == 0:
+            gram32 = gram32 * (scale * scale)
+        gram = gram32.astype(jnp.bfloat16)
+        square = jnp.dot(gram, gram, preferred_element_type=jnp.float32)
+        poly = (COEF_B * gram.astype(jnp.float32) + COEF_C * square).astype(jnp.bfloat16)
+        final = turn + 1 == ITERS
+        for c in range(chunks):
+            part = y[:, c * width : (c + 1) * width]
+            mixed = COEF_A * part.astype(jnp.float32) + jnp.dot(poly, part, preferred_element_type=jnp.float32)
+            if turn == 0:
+                mixed = mixed * scale
+            if final:
+                scaled = (factor * mixed).astype(jnp.bfloat16)
+                for i, d in enumerate(order):
+                    outs[c * len(order) + d][...] = scaled[i * rows : (i + 1) * rows, :]
+            else:
+                iterate[:, c * width : (c + 1) * width] = mixed.astype(jnp.bfloat16)
+    for flight in flights:
+        flight.wait()
+
+
+def group_kernel(own, table, *refs):
+    parts, out = refs[:own], refs[own]
+    group, me = lax.axis_index("rep"), lax.axis_index("own")
+    for d in range(own):
+        matrix = table[group, me ^ d]
+
+        @pl.when(matrix < out.shape[0])
+        def _():
+            out[matrix] = parts[d][...]
+
+
+def place_kernel(reps, where, *refs):
+    parts, out, sems = refs[: len(where)], refs[-2], refs[-1]
+    group = lax.axis_index("rep")
+    count, _, width = parts[0].shape
+    flights = []
+    for i, (c, stream, step) in enumerate(where):
+        source = group + step * (1 - 2 * lax.rem(group + stream + step + 1, 2))
+        here = (source >= 0) & (source < reps)
+        at = jnp.clip(source, 0, reps - 1) * count
+        to = out.at[pl.ds(at, count), :, pl.ds(c * width, width)]
+        flights.append((here, pltpu.make_async_copy(parts[i], to, sems.at[i])))
+    for here, copy in flights:
+        pl.when(here)(copy.start)
+    for here, copy in flights:
+        pl.when(here)(copy.wait)
+
+
+def place(reps, where, parts, shape, out):
+    aliases = {} if out is None else {len(where): 0}
+    return pl.pallas_call(
+        functools.partial(place_kernel, reps, where),
+        in_specs=[VMEM] * len(where) + [ANY] * len(aliases),
+        out_specs=ANY,
+        out_shape=jax.ShapeDtypeStruct(shape, jnp.bfloat16),
+        input_output_aliases=aliases,
+        scratch_shapes=[pltpu.SemaphoreType.DMA((len(where),))],
+        compiler_params=limit(4),
+    )(*map(near, parts), *([] if out is None else [out]))
+
+
+def chunked_body(own, reps, grads, momentum, owner_table):
+    count, rows, columns = grads.shape
+    width = columns // CHUNKS
+    half = jnp.bfloat16
+    order = send_order(own)
+    arrival = [0, order[-1]] + order[:-1]
+    first = own // 2
+
+    def swap(x, d):
+        return lax.ppermute(x, "own", [(i, i ^ d) for i in range(own)])
+
+    outgoing = pl.pallas_call(
+        pack_kernel,
+        in_specs=[ANY, ANY],
+        out_specs=[VMEM] * own,
+        out_shape=[pltpu.VMEM((rows, columns), half)] * own,
+        scratch_shapes=[
+            pltpu.SMEM(owner_table.shape, jnp.int32),
+            pltpu.VMEM(grads.shape, grads.dtype),
+            pltpu.SemaphoreType.DMA(()),
+            pltpu.SemaphoreType.DMA((count,)),
+        ],
+        compiler_params=limit(8),
+        name="pack",
+    )(far(owner_table), far(grads))
+    incoming = {0: outgoing[0]}
+    for d in order:
+        incoming[d] = swap(outgoing[d], d)
+    slots = near(momentum.reshape(own, rows, columns))
+    new_momentum, blend, squares = pl.pallas_call(
+        functools.partial(mix_kernel, arrival[:first]),
+        in_specs=[VMEM] * (first + 1),
+        out_specs=[ANY, VMEM, VMEM],
+        out_shape=[
+            jax.ShapeDtypeStruct((own, rows, columns), half),
+            pltpu.VMEM((own * rows, columns), half),
+            pltpu.VMEM((8, columns), jnp.float32),
+        ],
+        scratch_shapes=[pltpu.VMEM((first, rows, columns), half), pltpu.SemaphoreType.DMA((first,))],
+        compiler_params=limit(8),
+        name="mix",
+    )(*[near(incoming[d]) for d in arrival[:first]], slots)
+    late = own - first
+    new_momentum, _, *parts = pl.pallas_call(
+        functools.partial(update_kernel, arrival, first, CHUNKS),
+        in_specs=[VMEM] * (late + 1) + [ANY, VMEM, VMEM],
+        out_specs=[ANY] + [VMEM] * (1 + own * CHUNKS),
+        out_shape=[
+            jax.ShapeDtypeStruct((own, rows, columns), half),
+            pltpu.VMEM((own * rows, columns), half),
+        ]
+        + [pltpu.VMEM((rows, width), half)] * (own * CHUNKS),
+        input_output_aliases={late + 1: 0, late + 2: 1},
+        scratch_shapes=[
+            pltpu.VMEM((own * rows, columns), half),
+            pltpu.VMEM((late, rows, columns), half),
+            pltpu.SemaphoreType.DMA((late,)),
+        ],
+        compiler_params=limit(24),
+        name="update",
+    )(*[near(incoming[d]) for d in arrival[first:]], slots, new_momentum, near(blend), near(squares))
+    held = {}
+    for c in range(CHUNKS):
+        back = [parts[c * own]] + [None] * (own - 1)
+        for d in order:
+            back[d] = swap(parts[c * own + d], d)
+        held[c, 0, 0] = pl.pallas_call(
+            functools.partial(group_kernel, own),
+            in_specs=[SMEM] + [VMEM] * own,
+            out_specs=VMEM,
+            out_shape=pltpu.VMEM((count, rows, width), half),
+            compiler_params=limit(4),
+        )(owner_table, *map(near, back))
+    pairs = [line_pairs(kind, reps, own) for kind in (0, 1)]
+    steps = line_steps(reps)
+    for stream, step in steps:
+        for c in range(CHUNKS):
+            behind = held[c, 0, 0] if step == 1 else held[c, stream, step - 1]
+            held[c, stream, step] = lax.ppermute(behind, ("rep", "own"), pairs[(stream + step + 1) % 2])
+    shape = (reps * count, rows, columns)
+    last = [key for key in held if key[1:] == steps[-1]]
+    soon = [key for key in held if key not in last]
+    updates = place(reps, soon, [held[key] for key in soon], shape, None)
+    updates = place(reps, last, [held[key] for key in last], shape, updates)
+    return (new_momentum.reshape(1, own * rows, columns), updates)
+
+
 def solution(mesh):
     in_specs = (P("rep", "own", None), P(("rep", "own"), None, None), P())
     out_specs = (P(("rep", "own"), None, None), P(None, "own", None))
-    return jax.shard_map(body, mesh=mesh, in_specs=in_specs, out_specs=out_specs, check_vma=False)
+    own, reps = mesh.shape["own"], mesh.shape["rep"]
+
+    def step(grads, momentum, owner_table):
+        _, total_rows, columns = grads.shape
+        tiled = total_rows % (8 * own) == 0 and columns % (128 * CHUNKS) == 0
+        if not tiled or own & (own - 1) or not 4 <= own <= 8 or reps < 2:
+            return jax.shard_map(general_body, mesh=mesh, in_specs=in_specs, out_specs=out_specs, check_vma=False)(
+                grads, momentum, owner_table
+            )
+
+        def body(*args):
+            return chunked_body(own, reps, *args)
+
+        mapped = jax.shard_map(body, mesh=mesh, in_specs=in_specs, out_specs=out_specs, check_vma=False)
+        return mapped(grads, momentum, owner_table)
+
+    return step

time: 139 us -> 89 us (0.64)
  starting transfers between devices: 3.61 us -> 49.6 us
  waiting for transfers between devices: 65.1 us -> 26 us
  blocking collectives: 21.7 us -> 0 us
  other arithmetic: 16.7 us -> 0 us
  between operations: 14.9 us -> 0.72 us
  Pallas kernels: 0 us -> 12.5 us
  local copies, waits for them, and re-layouts: 11.1 us -> 0.01 us
  matrix products: 5.68 us -> 0 us
    ppermute x0 -> x31, starting transfers between devices: none -> 49.6 us  [the longest x10 27.4 us: chunked_body(): lax.ppermute(behind, ('rep', 'own'), pairs[(stream + step + 1) % 2])]
    all_gather x1 -> x0, waiting for transfers between devices: 49.5 us -> none  [body(): updates = lax.all_gather(grouped, 'rep', axis=0, tiled=True)]
    ppermute x0 -> x31, waiting for transfers between devices: none -> 26 us  [the longest x21 13.6 us: swap(): return lax.ppermute(x, 'own', [(i, i ^ d) for i in range(own)])]
    all_to_all x1 -> x0, blocking collectives: 21.7 us -> none  [body(): lax.all_to_all(outgoing, 'own', split_axis=0, concat_axis=1, tiled=True)]
    all_to_all x1 -> x0, waiting for transfers between devices: 15.6 us -> none  [body(): lax.all_to_all(update[None], 'own', split_axis=1, concat_axis=0, tiled=True)]
    pallas_call x0 -> x7, Pallas kernels: none -> 12.5 us  [the longest x1 6.54 us: chunked_body(): pl.pallas_call(functools.partial(update_kernel, arrival, first, CHUNKS),...]
    unnamed x9 -> x4, local copies, waits for them, and re-layouts: 8.11 us -> 0.01 us
    unnamed x1 -> x0, other arithmetic: 7.72 us -> none
  transfers between devices with their start and end apart: 2 -> 31, of which waited for: 2 -> 13; matrix products, arithmetic and copies ran while one was open for 1% -> 0% of each run, Pallas kernels for 0% -> 4%
where the time goes in v1:
time: 89 us; the launch traced here: 88.8 us
  starting transfers between devices  49.6 us (56%)
  waiting for transfers between devices  26 us (29%)
  Pallas kernels  12.5 us (14%)
    ppermute x10, starting transfers between devices, chunked_body(): lax.ppermute(behind, ('rep', 'own'), pairs[(stream + step + 1) % 2])  27.4 us
    ppermute x21, starting transfers between devices, swap(): return lax.ppermute(x, 'own', [(i, i ^ d) for i in range(own)])  22.2 us
    ppermute x21, waiting for transfers between devices, swap(): return lax.ppermute(x, 'own', [(i, i ^ d) for i in range(own)])  13.6 us
    ppermute x10, waiting for transfers between devices, chunked_body(): lax.ppermute(behind, ('rep', 'own'), pairs[(stream + step + 1) % 2])  12.4 us
    pallas_call x1, Pallas kernels, chunked_body(): pl.pallas_call(functools.partial(update_kernel, arrival, first, CHUNKS),...  6.54 us
    pallas_call x2, Pallas kernels, place(): pl.pallas_call(functools.partial(place_kernel, reps, where), in_specs=[VM...  2.11 us
  transfers between devices with their start and end apart: 31, of which 13 were waited for; matrix products, arithmetic and copies ran while one was open for 0% of the time, Pallas kernels for 4%

profile of v1, /device:TPU:0, one launch (start us, length us, event | category | flops | bytes accessed | tf_op | source)
XLA Modules:
  0.0 88.8 jit_solution(15342994011379866377)
XLA Ops:
  0.6 1.6 %pack.1 = (bf16[72,1024]{1,0:T(8,128)(2,1)S(1)}, bf16[72,1024]{1,0:T(8,128)(2,1)S(1)}, bf16[72,1024]{1,0:T(8,128)(2,1)S(1)}, bf16[72,1024]{1,0:T(8,128)(2,1)S(1)...) custom-call(s32[4,8]{1,0:T(4,128)} %table.3, ...), custom_call_target="tpu_custom_call" | custom-call | tf_op jit(solution)/shard_map/pack/pallas_call | solution.py:253
  2.2 0.6 collective-permute-start.4
  2.8 3.5 %collective-permute-start.5 = (bf16[72,1024]{1,0:T(8,128)(2,1)S(1)}, bf16[72,1024]{1,0:T(8,128)(2,1)S(1)}, u32[]{:S(2)}, u32[]{:S(2)}) collective-permute-start(bf16[72,1024]{1,0:T(8,128)(2,1)S(1)} %get-tuple-element.36), channel_id=1, source_target_pairs={{0,6},{1,7},{2,4},{3,5},{4,2},{5,3},{6,0},{7,1},{8,14},{9,15},{10,... | collective-permute-start | bytes 442376 | tf_op jit(solution)/shard_map/ppermute | solution.py:251
  6.3 0.0 collective-permute-start.6
  6.3 1.7 %collective-permute-start = (bf16[72,1024]{1,0:T(8,128)(2,1)S(1)}, bf16[72,1024]{1,0:T(8,128)(2,1)S(1)}, u32[]{:S(2)}, u32[]{:S(2)}) collective-permute-start(bf16[72,1024]{1,0:T(8,128)(2,1)S(1)} %get-tuple-element.30), channel_id=1, source_target_pairs={{0,2},{1,3},{2,0},{3,1},{4,6},{5,7},{6,4},{7,5},{8,10},{9,11},{10,... | collective-permute-start | bytes 442376 | tf_op jit(solution)/shard_map/ppermute | solution.py:251
  8.0 1.5 %collective-permute-start.1 = (bf16[72,1024]{1,0:T(8,128)(2,1)S(1)}, bf16[72,1024]{1,0:T(8,128)(2,1)S(1)}, u32[]{:S(2)}, u32[]{:S(2)}) collective-permute-start(bf16[72,1024]{1,0:T(8,128)(2,1)S(1)} %get-tuple-element.31), channel_id=1, source_target_pairs={{0,4},{1,5},{2,6},{3,7},{4,0},{5,1},{6,2},{7,3},{8,12},{9,13},{10,... | collective-permute-start | bytes 442376 | tf_op jit(solution)/shard_map/ppermute | solution.py:251
  9.5 0.0 collective-permute-done.4.refs_1_
  9.5 0.0 collective-permute-start.2
  9.5 1.5 %collective-permute-done.5.refs_2_ = bf16[72,1024]{1,0:T(8,128)(2,1)S(1)} collective-permute-done((bf16[72,1024]{1,0:T(8,128)(2,1)S(1)}, bf16[72,1024]{1,0:T(8,128)(2,1)S(1)}, u32[]{:S(2)}, u32[]{:S(2)}) %collective-permute-start.5) | collective-permute-done | bytes 147488 | tf_op jit(solution)/shard_map/ppermute | solution.py:251
  11.0 0.6 collective-permute-start.3
  11.6 2.1 %collective-permute-done.6.refs_3_ = bf16[72,1024]{1,0:T(8,128)(2,1)S(1)} collective-permute-done((bf16[72,1024]{1,0:T(8,128)(2,1)S(1)}, bf16[72,1024]{1,0:T(8,128)(2,1)S(1)}, u32[]{:S(2)}, u32[]{:S(2)}) %collective-permute-start.6) | collective-permute-done | bytes 147488 | tf_op jit(solution)/shard_map/ppermute | solution.py:251
  13.7 0.9 %mix.1 = (bf16[8,72,1024]{2,1,0:T(8,128)(2,1)}, bf16[576,1024]{1,0:T(8,128)(2,1)S(1)}, f32[8,1024]{1,0:T(8,128)S(1)}) custom-call(bf16[72,1024]{1,0:T(8,128)(2,1)S(1)} %get-tuple-element.34.refs_0_, bf16[72,1024]{1,0:T(8,128)(2,1)S(1)} %collective-permute-done.4.refs_1_, bf16[72,1024]{1,0:T(8,128)(2,1)S(1)} %collective-permute-done.5.refs_2_, ...), custom_call_target="tpu_custom_call" | custom-call | tf_op jit(solution)/shard_map/mix/pallas_call | solution.py:271
  14.6 3.2 %collective-permute-done.refs_0_ = bf16[72,1024]{1,0:T(8,128)(2,1)S(1)} collective-permute-done((bf16[72,1024]{1,0:T(8,128)(2,1)S(1)}, bf16[72,1024]{1,0:T(8,128)(2,1)S(1)}, u32[]{:S(2)}, u32[]{:S(2)}) %collective-permute-start) | collective-permute-done | bytes 147488 | tf_op jit(solution)/shard_map/ppermute | solution.py:251
  17.9 0.0 collective-permute-done.1.refs_1_
  17.9 2.1 %collective-permute-done.2.refs_2_ = bf16[72,1024]{1,0:T(8,128)(2,1)S(1)} collective-permute-done((bf16[72,1024]{1,0:T(8,128)(2,1)S(1)}, bf16[72,1024]{1,0:T(8,128)(2,1)S(1)}, u32[]{:S(2)}, u32[]{:S(2)}) %collective-permute-start.2) | collective-permute-done | bytes 147488 | tf_op jit(solution)/shard_map/ppermute | solution.py:251
  20.0 0.2 collective-permute-done.3.refs_3_
  20.1 6.5 %update.1 = (bf16[8,72,1024]{2,1,0:T(8,128)(2,1)}, bf16[576,1024]{1,0:T(8,128)(2,1)S(1)}, bf16[72,512]{1,0:T(8,128)(2,1)S(1)}, bf16[72,512]{1,0:T(8,128)(2,1)S(1...) custom-call(bf16[72,1024]{1,0:T(8,128)(2,1)S(1)} %collective-permute, ...), custom_call_target="tpu_custom_call", output_to_operand_aliasing={{0}: (5, {}), {1}: (6, {})} | custom-call | tf_op jit(solution)/shard_map/update/pallas_call | solution.py:285
  26.7 0.3 collective-permute-start.17
  26.9 1.6 %collective-permute-start.18 = (bf16[72,512]{1,0:T(8,128)(2,1)S(1)}, bf16[72,512]{1,0:T(8,128)(2,1)S(1)}, u32[]{:S(2)}, u32[]{:S(2)}) collective-permute-start(bf16[72,512]{1,0:T(8,128)(2,1)S(1)} %get-tuple-element.52), channel_id=1, source_target_pairs={{0,2},{1,3},{2,0},{3,1},{4,6},{5,7},{6,4},{7,5},{8,10},{9,11},{10,... | collective-permute-start | bytes 221192 | tf_op jit(solution)/shard_map/ppermute | solution.py:251
  28.5 0.1 collective-permute-start.19
  28.6 1.7 %collective-permute-start.20 = (bf16[72,512]{1,0:T(8,128)(2,1)S(1)}, bf16[72,512]{1,0:T(8,128)(2,1)S(1)}, u32[]{:S(2)}, u32[]{:S(2)}) collective-permute-start(bf16[72,512]{1,0:T(8,128)(2,1)S(1)} %get-tuple-element.54), channel_id=1, source_target_pairs={{0,4},{1,5},{2,6},{3,7},{4,0},{5,1},{6,2},{7,3},{8,12},{9,13},{10,... | collective-permute-start | bytes 221192 | tf_op jit(solution)/shard_map/ppermute | solution.py:251
  30.3 0.1 collective-permute-start.21
  30.4 0.0 collective-permute-done.17.refs_1_
  30.4 2.6 %collective-permute-start.22 = (bf16[72,512]{1,0:T(8,128)(2,1)S(1)}, bf16[72,512]{1,0:T(8,128)(2,1)S(1)}, u32[]{:S(2)}, u32[]{:S(2)}) collective-permute-start(bf16[72,512]{1,0:T(8,128)(2,1)S(1)} %get-tuple-element.56), channel_id=1, source_target_pairs={{0,6},{1,7},{2,4},{3,5},{4,2},{5,3},{6,0},{7,1},{8,14},{9,15},{10,... | collective-permute-start | bytes 221192 | tf_op jit(solution)/shard_map/ppermute | solution.py:251
  33.0 0.2 collective-permute-start.23
  33.2 0.0 collective-permute-done.19.refs_3_
  33.2 1.5 %collective-permute-start.10 = (bf16[72,512]{1,0:T(8,128)(2,1)S(1)}, bf16[72,512]{1,0:T(8,128)(2,1)S(1)}, u32[]{:S(2)}, u32[]{:S(2)}) collective-permute-start(bf16[72,512]{1,0:T(8,128)(2,1)S(1)} %get-tuple-element.46), channel_id=1, source_target_pairs={{0,4},{1,5},{2,6},{3,7},{4,0},{5,1},{6,2},{7,3},{8,12},{9,13},{10,... | collective-permute-start | bytes 221192 | tf_op jit(solution)/shard_map/ppermute | solution.py:251
  34.7 1.4 %collective-permute-start.11 = (bf16[72,512]{1,0:T(8,128)(2,1)S(1)}, bf16[72,512]{1,0:T(8,128)(2,1)S(1)}, u32[]{:S(2)}, u32[]{:S(2)}) collective-permute-start(bf16[72,512]{1,0:T(8,128)(2,1)S(1)} %get-tuple-element.47), channel_id=1, source_target_pairs={{0,5},{1,4},{2,7},{3,6},{4,1},{5,0},{6,3},{7,2},{8,13},{9,12},{10,... | collective-permute-start | bytes 221192 | tf_op jit(solution)/shard_map/ppermute | solution.py:251
  36.1 1.4 %collective-permute-done.21.refs_5_ = bf16[72,512]{1,0:T(8,128)(2,1)S(1)} collective-permute-done((bf16[72,512]{1,0:T(8,128)(2,1)S(1)}, bf16[72,512]{1,0:T(8,128)(2,1)S(1)}, u32[]{:S(2)}, u32[]{:S(2)}) %collective-permute-start.21) | collective-permute-done | bytes 73760 | tf_op jit(solution)/shard_map/ppermute | solution.py:251
  37.5 1.1 %collective-permute-start.12 = (bf16[72,512]{1,0:T(8,128)(2,1)S(1)}, bf16[72,512]{1,0:T(8,128)(2,1)S(1)}, u32[]{:S(2)}, u32[]{:S(2)}) collective-permute-start(bf16[72,512]{1,0:T(8,128)(2,1)S(1)} %get-tuple-element.48), channel_id=1, source_target_pairs={{0,6},{1,7},{2,4},{3,5},{4,2},{5,3},{6,0},{7,1},{8,14},{9,15},{10,... | collective-permute-start | bytes 221192 | tf_op jit(solution)/shard_map/ppermute | solution.py:251
  38.6 0.0 collective-permute-done.22.refs_6_
  38.6 1.7 %collective-permute-start.13 = (bf16[72,512]{1,0:T(8,128)(2,1)S(1)}, bf16[72,512]{1,0:T(8,128)(2,1)S(1)}, u32[]{:S(2)}, u32[]{:S(2)}) collective-permute-start(bf16[72,512]{1,0:T(8,128)(2,1)S(1)} %get-tuple-element.49), channel_id=1, source_target_pairs={{0,7},{1,6},{2,5},{3,4},{4,3},{5,2},{6,1},{7,0},{8,15},{9,14},{10,... | collective-permute-start | bytes 221192 | tf_op jit(solution)/shard_map/ppermute | solution.py:251
  40.4 0.0 collective-permute-done.23.refs_7_
  40.4 0.2 collective-permute-start.7
  40.6 1.8 %collective-permute-start.8 = (bf16[72,512]{1,0:T(8,128)(2,1)S(1)}, bf16[72,512]{1,0:T(8,128)(2,1)S(1)}, u32[]{:S(2)}, u32[]{:S(2)}) collective-permute-start(bf16[72,512]{1,0:T(8,128)(2,1)S(1)} %get-tuple-element.44), channel_id=1, source_target_pairs={{0,2},{1,3},{2,0},{3,1},{4,6},{5,7},{6,4},{7,5},{8,10},{9,11},{10,... | collective-permute-start | bytes 221192 | tf_op jit(solution)/shard_map/ppermute | solution.py:251
  42.4 0.0 collective-permute-done.11.refs_5_
  42.4 0.0 collective-permute-start.9
  42.4 0.7 shard_map.51.refs_1_
  43.1 0.5 collective-permute-done.12.refs_6_
  43.6 1.6 %collective-permute-start.24 = (bf16[4,72,512]{2,1,0:T(8,128)(2,1)S(1)}, bf16[4,72,512]{2,1,0:T(8,128)(2,1)S(1)}, u32[]{:S(2)}, u32[]{:S(2)}) collective-permute-start(bf16[4,72,512]{2,1,0:T(8,128)(2,1)S(1)} %shard_map.51.refs_1_), channel_id=1, source_target_pairs={{0,8},{1,9},{2,10},{3,11},{4,12},{5,13},{6,14},{7,15},{8,0},{9,1},... | collective-permute-start | bytes 884744 | tf_op jit(solution)/shard_map/ppermute | solution.py:320
  45.2 1.4 %collective-permute-done.8.refs_2_ = bf16[72,512]{1,0:T(8,128)(2,1)S(1)} collective-permute-done((bf16[72,512]{1,0:T(8,128)(2,1)S(1)}, bf16[72,512]{1,0:T(8,128)(2,1)S(1)}, u32[]{:S(2)}, u32[]{:S(2)}) %collective-permute-start.8) | collective-permute-done | bytes 73760 | tf_op jit(solution)/shard_map/ppermute | solution.py:251
  46.6 1.2 %collective-permute-done.9.refs_3_ = bf16[72,512]{1,0:T(8,128)(2,1)S(1)} collective-permute-done((bf16[72,512]{1,0:T(8,128)(2,1)S(1)}, bf16[72,512]{1,0:T(8,128)(2,1)S(1)}, u32[]{:S(2)}, u32[]{:S(2)}) %collective-permute-start.9) | collective-permute-done | bytes 73760 | tf_op jit(solution)/shard_map/ppermute | solution.py:251
  47.8 0.7 shard_map.50.refs_0_
  48.5 1.6 %collective-permute-start.14 = (bf16[4,72,512]{2,1,0:T(8,128)(2,1)S(1)}, bf16[4,72,512]{2,1,0:T(8,128)(2,1)S(1)}, u32[]{:S(2)}, u32[]{:S(2)}) collective-permute-start(bf16[4,72,512]{2,1,0:T(8,128)(2,1)S(1)} %shard_map.50.refs_0_), channel_id=1, source_target_pairs={{0,8},{1,9},{2,10},{3,11},{4,12},{5,13},{6,14},{7,15},{8,0},{9,1},... | collective-permute-start | bytes 884744 | tf_op jit(solution)/shard_map/ppermute | solution.py:320
  50.1 0.0 collective-permute-start.28
  50.1 0.5 collective-permute-start.27
  50.6 1.5 %collective-permute-done.24.refs_3_ = bf16[4,72,512]{2,1,0:T(8,128)(2,1)S(1)} collective-permute-done((bf16[4,72,512]{2,1,0:T(8,128)(2,1)S(1)}, bf16[4,72,512]{2,1,0:T(8,128)(2,1)S(1)}, u32[]{:S(2)}, u32[]{:S(2)}) %collective-permute-start.24) | collective-permute-done | bytes 294944 | tf_op jit(solution)/shard_map/ppermute | solution.py:320
  52.1 2.7 %collective-permute-start.25 = (bf16[4,72,512]{2,1,0:T(8,128)(2,1)S(1)}, bf16[4,72,512]{2,1,0:T(8,128)(2,1)S(1)}, u32[]{:S(2)}, u32[]{:S(2)}) collective-permute-start(bf16[4,72,512]{2,1,0:T(8,128)(2,1)S(1)} %collective-permute-done.24.refs_3_), channel_id=1, source_target_pairs={{0,1},{1,0},{2,3},{3,2},{4,5},{5,4},{6,7},{7,6},{8,16},{9,17},{10,... | collective-permute-start | bytes 884744 | tf_op jit(solution)/shard_map/ppermute | solution.py:320
  54.9 3.6 %collective-permute-done.14.refs_2_ = bf16[4,72,512]{2,1,0:T(8,128)(2,1)S(1)} collective-permute-done((bf16[4,72,512]{2,1,0:T(8,128)(2,1)S(1)}, bf16[4,72,512]{2,1,0:T(8,128)(2,1)S(1)}, u32[]{:S(2)}, u32[]{:S(2)}) %collective-permute-start.14) | collective-permute-done | bytes 294944 | tf_op jit(solution)/shard_map/ppermute | solution.py:320
  58.5 1.1 %collective-permute-start.15 = (bf16[4,72,512]{2,1,0:T(8,128)(2,1)S(1)}, bf16[4,72,512]{2,1,0:T(8,128)(2,1)S(1)}, u32[]{:S(2)}, u32[]{:S(2)}) collective-permute-start(bf16[4,72,512]{2,1,0:T(8,128)(2,1)S(1)} %collective-permute-done.14.refs_2_), channel_id=1, source_target_pairs={{0,1},{1,0},{2,3},{3,2},{4,5},{5,4},{6,7},{7,6},{8,16},{9,17},{10,... | collective-permute-start | bytes 884744 | tf_op jit(solution)/shard_map/ppermute | solution.py:320
  59.6 0.0 collective-permute-done.28.refs_5_
  59.6 2.0 %collective-permute-start.30 = (bf16[4,72,512]{2,1,0:T(8,128)(2,1)S(1)}, bf16[4,72,512]{2,1,0:T(8,128)(2,1)S(1)}, u32[]{:S(2)}, u32[]{:S(2)}) collective-permute-start(bf16[4,72,512]{2,1,0:T(8,128)(2,1)S(1)} %collective-permute-done.28.refs_5_), channel_id=1, source_target_pairs={{0,8},{1,9},{2,10},{3,11},{4,12},{5,13},{6,14},{7,15},{8,0},{9,1},... | collective-permute-start | bytes 884744 | tf_op jit(solution)/shard_map/ppermute | solution.py:320
  61.6 0.0 collective-permute-done.27.refs_4_
  61.6 5.8 %collective-permute-start.29 = (bf16[4,72,512]{2,1,0:T(8,128)(2,1)S(1)}, bf16[4,72,512]{2,1,0:T(8,128)(2,1)S(1)}, u32[]{:S(2)}, u32[]{:S(2)}) collective-permute-start(bf16[4,72,512]{2,1,0:T(8,128)(2,1)S(1)} %collective-permute-done.27.refs_4_), channel_id=1, source_target_pairs={{0,8},{1,9},{2,10},{3,11},{4,12},{5,13},{6,14},{7,15},{8,0},{9,1},... | collective-permute-start | bytes 884744 | tf_op jit(solution)/shard_map/ppermute | solution.py:320
  67.5 0.0 collective-permute-done.25.refs_7_
  67.5 6.3 %collective-permute-start.26 = (bf16[4,72,512]{2,1,0:T(8,128)(2,1)S(1)}, bf16[4,72,512]{2,1,0:T(8,128)(2,1)S(1)}, u32[]{:S(2)}, u32[]{:S(2)}) collective-permute-start(bf16[4,72,512]{2,1,0:T(8,128)(2,1)S(1)} %collective-permute-done.25.refs_7_), channel_id=1, source_target_pairs={{0,8},{1,9},{2,10},{3,11},{4,12},{5,13},{6,14},{7,15},{8,0},{9,1},... | collective-permute-start | bytes 884744 | tf_op jit(solution)/shard_map/ppermute | solution.py:320
  73.8 0.0 collective-permute-done.15.refs_6_
  73.8 5.6 %collective-permute-start.16 = (bf16[4,72,512]{2,1,0:T(8,128)(2,1)S(1)}, bf16[4,72,512]{2,1,0:T(8,128)(2,1)S(1)}, u32[]{:S(2)}, u32[]{:S(2)}) collective-permute-start(bf16[4,72,512]{2,1,0:T(8,128)(2,1)S(1)} %collective-permute-done.15.refs_6_), channel_id=1, source_target_pairs={{0,8},{1,9},{2,10},{3,11},{4,12},{5,13},{6,14},{7,15},{8,0},{9,1},... | collective-permute-start | bytes 884744 | tf_op jit(solution)/shard_map/ppermute | solution.py:320
  79.4 0.0 collective-permute-done.30.refs_9_
  79.4 0.0 collective-permute-done.29.refs_8_
  79.4 1.3 %shard_map.52.refs_2_ = bf16[16,72,1024]{2,1,0:T(8,128)(2,1)} custom-call(bf16[4,72,512]{2,1,0:T(8,128)(2,1)S(1)} %shard_map.50.refs_0_, bf16[4,72,512]{2,1,0:T(8,128)(2,1)S(1)} %shard_map.51.refs_1_, bf16[4,72,512]{2,1,0:T(8,128)(2,1)S(1)} %collective-permute-done.14.refs_2_, bf16[4,72,512]{2,1,0:T(8,128)(2,1)S(1)} %collective-permute-done.24.refs_3_, ...), custom_call_target="tpu_custom_call" | custom-call | tf_op jit(solution)/shard_map/pallas_call | solution.py:231
  80.7 0.9 %collective-permute-done.26.refs_1_ = bf16[4,72,512]{2,1,0:T(8,128)(2,1)S(1)} collective-permute-done((bf16[4,72,512]{2,1,0:T(8,128)(2,1)S(1)}, bf16[4,72,512]{2,1,0:T(8,128)(2,1)S(1)}, u32[]{:S(2)}, u32[]{:S(2)}) %collective-permute-start.26) | collective-permute-done | bytes 294944 | tf_op jit(solution)/shard_map/ppermute | solution.py:320
  81.7 6.3 %collective-permute-done.16.refs_0_ = bf16[4,72,512]{2,1,0:T(8,128)(2,1)S(1)} collective-permute-done((bf16[4,72,512]{2,1,0:T(8,128)(2,1)S(1)}, bf16[4,72,512]{2,1,0:T(8,128)(2,1)S(1)}, u32[]{:S(2)}, u32[]{:S(2)}) %collective-permute-start.16) | collective-permute-done | bytes 294944 | tf_op jit(solution)/shard_map/ppermute | solution.py:320
  88.0 0.8 shard_map.53
  (9 shorter events, 0.0 us)
Async XLA Ops:
  0.6 13.1 %copy-start = (bf16[1,576,1024]{2,1,0:T(8,128)(2,1)S(1)}, bf16[1,576,1024]{2,1,0:T(8,128)(2,1)}, u32[]{:S(2)}) copy-start(bf16[1,576,1024]{2,1,0:T(8,128)(2,1)} %param.4) | copy-start | bytes 3538948
  2.2 7.3 %collective-permute-start.4 = (bf16[72,1024]{1,0:T(8,128)(2,1)S(1)}, bf16[72,1024]{1,0:T(8,128)(2,1)S(1)}, u32[]{:S(2)}, u32[]{:S(2)}) collective-permute-start(bf16[72,1024]{1,0:T(8,128)(2,1)S(1)} %get-tuple-element.35), channel_id=1, source_target_pairs={{0,1},{1,0},{2,3},{3,2},{4,5},{5,4},{6,7},{7,6},{8,9},{9,8},{10,11... | collective-permute-start | bytes 442376 | tf_op jit(solution)/shard_map/ppermute | solution.py:251
  2.8 8.2 %collective-permute-start.5 = (bf16[72,1024]{1,0:T(8,128)(2,1)S(1)}, bf16[72,1024]{1,0:T(8,128)(2,1)S(1)}, u32[]{:S(2)}, u32[]{:S(2)}) collective-permute-start(bf16[72,1024]{1,0:T(8,128)(2,1)S(1)} %get-tuple-element.36), channel_id=1, source_target_pairs={{0,6},{1,7},{2,4},{3,5},{4,2},{5,3},{6,0},{7,1},{8,14},{9,15},{10,... | collective-permute-start | bytes 442376 | tf_op jit(solution)/shard_map/ppermute | solution.py:251
  6.3 7.4 %collective-permute-start.6 = (bf16[72,1024]{1,0:T(8,128)(2,1)S(1)}, bf16[72,1024]{1,0:T(8,128)(2,1)S(1)}, u32[]{:S(2)}, u32[]{:S(2)}) collective-permute-start(bf16[72,1024]{1,0:T(8,128)(2,1)S(1)} %get-tuple-element.37), channel_id=1, source_target_pairs={{0,7},{1,6},{2,5},{3,4},{4,3},{5,2},{6,1},{7,0},{8,15},{9,14},{10,... | collective-permute-start | bytes 442376 | tf_op jit(solution)/shard_map/ppermute | solution.py:251
  6.3 11.6 %collective-permute-start = (bf16[72,1024]{1,0:T(8,128)(2,1)S(1)}, bf16[72,1024]{1,0:T(8,128)(2,1)S(1)}, u32[]{:S(2)}, u32[]{:S(2)}) collective-permute-start(bf16[72,1024]{1,0:T(8,128)(2,1)S(1)} %get-tuple-element.30), channel_id=1, source_target_pairs={{0,2},{1,3},{2,0},{3,1},{4,6},{5,7},{6,4},{7,5},{8,10},{9,11},{10,... | collective-permute-start | bytes 442376 | tf_op jit(solution)/shard_map/ppermute | solution.py:251
  8.0 9.9 %collective-permute-start.1 = (bf16[72,1024]{1,0:T(8,128)(2,1)S(1)}, bf16[72,1024]{1,0:T(8,128)(2,1)S(1)}, u32[]{:S(2)}, u32[]{:S(2)}) collective-permute-start(bf16[72,1024]{1,0:T(8,128)(2,1)S(1)} %get-tuple-element.31), channel_id=1, source_target_pairs={{0,4},{1,5},{2,6},{3,7},{4,0},{5,1},{6,2},{7,3},{8,12},{9,13},{10,... | collective-permute-start | bytes 442376 | tf_op jit(solution)/shard_map/ppermute | solution.py:251
  9.5 10.4 %collective-permute-start.2 = (bf16[72,1024]{1,0:T(8,128)(2,1)S(1)}, bf16[72,1024]{1,0:T(8,128)(2,1)S(1)}, u32[]{:S(2)}, u32[]{:S(2)}) collective-permute-start(bf16[72,1024]{1,0:T(8,128)(2,1)S(1)} %get-tuple-element.32), channel_id=1, source_target_pairs={{0,3},{1,2},{2,1},{3,0},{4,7},{5,6},{6,5},{7,4},{8,11},{9,10},{10,... | collective-permute-start | bytes 442376 | tf_op jit(solution)/shard_map/ppermute | solution.py:251
  11.0 9.1 %collective-permute-start.3 = (bf16[72,1024]{1,0:T(8,128)(2,1)S(1)}, bf16[72,1024]{1,0:T(8,128)(2,1)S(1)}, u32[]{:S(2)}, u32[]{:S(2)}) collective-permute-start(bf16[72,1024]{1,0:T(8,128)(2,1)S(1)} %get-tuple-element.33), channel_id=1, source_target_pairs={{0,5},{1,4},{2,7},{3,6},{4,1},{5,0},{6,3},{7,2},{8,13},{9,12},{10,... | collective-permute-start | bytes 442376 | tf_op jit(solution)/shard_map/ppermute | solution.py:251
  20.1 22.3 %copy-start.1 = (s32[4,8]{1,0:T(4,128)S(1)}, s32[4,8]{1,0:T(4,128)}, u32[]{:S(2)}) copy-start(s32[4,8]{1,0:T(4,128)} %table.3) | copy-start | bytes 388
  26.7 3.8 %collective-permute-start.17 = (bf16[72,512]{1,0:T(8,128)(2,1)S(1)}, bf16[72,512]{1,0:T(8,128)(2,1)S(1)}, u32[]{:S(2)}, u32[]{:S(2)}) collective-permute-start(bf16[72,512]{1,0:T(8,128)(2,1)S(1)} %get-tuple-element.51), channel_id=1, source_target_pairs={{0,1},{1,0},{2,3},{3,2},{4,5},{5,4},{6,7},{7,6},{8,9},{9,8},{10,11... | collective-permute-start | bytes 221192 | tf_op jit(solution)/shard_map/ppermute | solution.py:251
  26.9 6.1 %collective-permute-start.18 = (bf16[72,512]{1,0:T(8,128)(2,1)S(1)}, bf16[72,512]{1,0:T(8,128)(2,1)S(1)}, u32[]{:S(2)}, u32[]{:S(2)}) collective-permute-start(bf16[72,512]{1,0:T(8,128)(2,1)S(1)} %get-tuple-element.52), channel_id=1, source_target_pairs={{0,2},{1,3},{2,0},{3,1},{4,6},{5,7},{6,4},{7,5},{8,10},{9,11},{10,... | collective-permute-start | bytes 221192 | tf_op jit(solution)/shard_map/ppermute | solution.py:251
  28.5 4.6 %collective-permute-start.19 = (bf16[72,512]{1,0:T(8,128)(2,1)S(1)}, bf16[72,512]{1,0:T(8,128)(2,1)S(1)}, u32[]{:S(2)}, u32[]{:S(2)}) collective-permute-start(bf16[72,512]{1,0:T(8,128)(2,1)S(1)} %get-tuple-element.53), channel_id=1, source_target_pairs={{0,3},{1,2},{2,1},{3,0},{4,7},{5,6},{6,5},{7,4},{8,11},{9,10},{10,... | collective-permute-start | bytes 221192 | tf_op jit(solution)/shard_map/ppermute | solution.py:251
  28.6 6.1 %collective-permute-start.20 = (bf16[72,512]{1,0:T(8,128)(2,1)S(1)}, bf16[72,512]{1,0:T(8,128)(2,1)S(1)}, u32[]{:S(2)}, u32[]{:S(2)}) collective-permute-start(bf16[72,512]{1,0:T(8,128)(2,1)S(1)} %get-tuple-element.54), channel_id=1, source_target_pairs={{0,4},{1,5},{2,6},{3,7},{4,0},{5,1},{6,2},{7,3},{8,12},{9,13},{10,... | collective-permute-start | bytes 221192 | tf_op jit(solution)/shard_map/ppermute | solution.py:251
  30.3 7.2 %collective-permute-start.21 = (bf16[72,512]{1,0:T(8,128)(2,1)S(1)}, bf16[72,512]{1,0:T(8,128)(2,1)S(1)}, u32[]{:S(2)}, u32[]{:S(2)}) collective-permute-start(bf16[72,512]{1,0:T(8,128)(2,1)S(1)} %get-tuple-element.55), channel_id=1, source_target_pairs={{0,5},{1,4},{2,7},{3,6},{4,1},{5,0},{6,3},{7,2},{8,13},{9,12},{10,... | collective-permute-start | bytes 221192 | tf_op jit(solution)/shard_map/ppermute | solution.py:251
  30.4 8.2 %collective-permute-start.22 = (bf16[72,512]{1,0:T(8,128)(2,1)S(1)}, bf16[72,512]{1,0:T(8,128)(2,1)S(1)}, u32[]{:S(2)}, u32[]{:S(2)}) collective-permute-start(bf16[72,512]{1,0:T(8,128)(2,1)S(1)} %get-tuple-element.56), channel_id=1, source_target_pairs={{0,6},{1,7},{2,4},{3,5},{4,2},{5,3},{6,0},{7,1},{8,14},{9,15},{10,... | collective-permute-start | bytes 221192 | tf_op jit(solution)/shard_map/ppermute | solution.py:251
  33.0 7.4 %collective-permute-start.23 = (bf16[72,512]{1,0:T(8,128)(2,1)S(1)}, bf16[72,512]{1,0:T(8,128)(2,1)S(1)}, u32[]{:S(2)}, u32[]{:S(2)}) collective-permute-start(bf16[72,512]{1,0:T(8,128)(2,1)S(1)} %get-tuple-element.57), channel_id=1, source_target_pairs={{0,7},{1,6},{2,5},{3,4},{4,3},{5,2},{6,1},{7,0},{8,15},{9,14},{10,... | collective-permute-start | bytes 221192 | tf_op jit(solution)/shard_map/ppermute | solution.py:251
  33.2 7.4 %collective-permute-start.10 = (bf16[72,512]{1,0:T(8,128)(2,1)S(1)}, bf16[72,512]{1,0:T(8,128)(2,1)S(1)}, u32[]{:S(2)}, u32[]{:S(2)}) collective-permute-start(bf16[72,512]{1,0:T(8,128)(2,1)S(1)} %get-tuple-element.46), channel_id=1, source_target_pairs={{0,4},{1,5},{2,6},{3,7},{4,0},{5,1},{6,2},{7,3},{8,12},{9,13},{10,... | collective-permute-start | bytes 221192 | tf_op jit(solution)/shard_map/ppermute | solution.py:251
  34.7 7.7 %collective-permute-start.11 = (bf16[72,512]{1,0:T(8,128)(2,1)S(1)}, bf16[72,512]{1,0:T(8,128)(2,1)S(1)}, u32[]{:S(2)}, u32[]{:S(2)}) collective-permute-start(bf16[72,512]{1,0:T(8,128)(2,1)S(1)} %get-tuple-element.47), channel_id=1, source_target_pairs={{0,5},{1,4},{2,7},{3,6},{4,1},{5,0},{6,3},{7,2},{8,13},{9,12},{10,... | collective-permute-start | bytes 221192 | tf_op jit(solution)/shard_map/ppermute | solution.py:251
  37.5 6.0 %collective-permute-start.12 = (bf16[72,512]{1,0:T(8,128)(2,1)S(1)}, bf16[72,512]{1,0:T(8,128)(2,1)S(1)}, u32[]{:S(2)}, u32[]{:S(2)}) collective-permute-start(bf16[72,512]{1,0:T(8,128)(2,1)S(1)} %get-tuple-element.48), channel_id=1, source_target_pairs={{0,6},{1,7},{2,4},{3,5},{4,2},{5,3},{6,0},{7,1},{8,14},{9,15},{10,... | collective-permute-start | bytes 221192 | tf_op jit(solution)/shard_map/ppermute | solution.py:251
  38.6 6.5 %collective-permute-start.13 = (bf16[72,512]{1,0:T(8,128)(2,1)S(1)}, bf16[72,512]{1,0:T(8,128)(2,1)S(1)}, u32[]{:S(2)}, u32[]{:S(2)}) collective-permute-start(bf16[72,512]{1,0:T(8,128)(2,1)S(1)} %get-tuple-element.49), channel_id=1, source_target_pairs={{0,7},{1,6},{2,5},{3,4},{4,3},{5,2},{6,1},{7,0},{8,15},{9,14},{10,... | collective-permute-start | bytes 221192 | tf_op jit(solution)/shard_map/ppermute | solution.py:251
  40.4 4.8 %collective-permute-start.7 = (bf16[72,512]{1,0:T(8,128)(2,1)S(1)}, bf16[72,512]{1,0:T(8,128)(2,1)S(1)}, u32[]{:S(2)}, u32[]{:S(2)}) collective-permute-start(bf16[72,512]{1,0:T(8,128)(2,1)S(1)} %get-tuple-element.43), channel_id=1, source_target_pairs={{0,1},{1,0},{2,3},{3,2},{4,5},{5,4},{6,7},{7,6},{8,9},{9,8},{10,11... | collective-permute-start | bytes 221192 | tf_op jit(solution)/shard_map/ppermute | solution.py:251
  40.6 6.0 %collective-permute-start.8 = (bf16[72,512]{1,0:T(8,128)(2,1)S(1)}, bf16[72,512]{1,0:T(8,128)(2,1)S(1)}, u32[]{:S(2)}, u32[]{:S(2)}) collective-permute-start(bf16[72,512]{1,0:T(8,128)(2,1)S(1)} %get-tuple-element.44), channel_id=1, source_target_pairs={{0,2},{1,3},{2,0},{3,1},{4,6},{5,7},{6,4},{7,5},{8,10},{9,11},{10,... | collective-permute-start | bytes 221192 | tf_op jit(solution)/shard_map/ppermute | solution.py:251
  42.4 5.4 %collective-permute-start.9 = (bf16[72,512]{1,0:T(8,128)(2,1)S(1)}, bf16[72,512]{1,0:T(8,128)(2,1)S(1)}, u32[]{:S(2)}, u32[]{:S(2)}) collective-permute-start(bf16[72,512]{1,0:T(8,128)(2,1)S(1)} %get-tuple-element.45), channel_id=1, source_target_pairs={{0,3},{1,2},{2,1},{3,0},{4,7},{5,6},{6,5},{7,4},{8,11},{9,10},{10,... | collective-permute-start | bytes 221192 | tf_op jit(solution)/shard_map/ppermute | solution.py:251
  43.6 8.6 %collective-permute-start.24 = (bf16[4,72,512]{2,1,0:T(8,128)(2,1)S(1)}, bf16[4,72,512]{2,1,0:T(8,128)(2,1)S(1)}, u32[]{:S(2)}, u32[]{:S(2)}) collective-permute-start(bf16[4,72,512]{2,1,0:T(8,128)(2,1)S(1)} %shard_map.51.refs_1_), channel_id=1, source_target_pairs={{0,8},{1,9},{2,10},{3,11},{4,12},{5,13},{6,14},{7,15},{8,0},{9,1},... | collective-permute-start | bytes 884744 | tf_op jit(solution)/shard_map/ppermute | solution.py:320
  48.5 10.0 %collective-permute-start.14 = (bf16[4,72,512]{2,1,0:T(8,128)(2,1)S(1)}, bf16[4,72,512]{2,1,0:T(8,128)(2,1)S(1)}, u32[]{:S(2)}, u32[]{:S(2)}) collective-permute-start(bf16[4,72,512]{2,1,0:T(8,128)(2,1)S(1)} %shard_map.50.refs_0_), channel_id=1, source_target_pairs={{0,8},{1,9},{2,10},{3,11},{4,12},{5,13},{6,14},{7,15},{8,0},{9,1},... | collective-permute-start | bytes 884744 | tf_op jit(solution)/shard_map/ppermute | solution.py:320
  50.1 9.5 %collective-permute-start.28 = (bf16[4,72,512]{2,1,0:T(8,128)(2,1)S(1)}, bf16[4,72,512]{2,1,0:T(8,128)(2,1)S(1)}, u32[]{:S(2)}, u32[]{:S(2)}) collective-permute-start(bf16[4,72,512]{2,1,0:T(8,128)(2,1)S(1)} %shard_map.51.refs_1_), channel_id=1, source_target_pairs={{0,1},{1,0},{2,3},{3,2},{4,5},{5,4},{6,7},{7,6},{8,16},{9,17},{10,... | collective-permute-start | bytes 884744 | tf_op jit(solution)/shard_map/ppermute | solution.py:320
  50.1 11.5 %collective-permute-start.27 = (bf16[4,72,512]{2,1,0:T(8,128)(2,1)S(1)}, bf16[4,72,512]{2,1,0:T(8,128)(2,1)S(1)}, u32[]{:S(2)}, u32[]{:S(2)}) collective-permute-start(bf16[4,72,512]{2,1,0:T(8,128)(2,1)S(1)} %shard_map.50.refs_0_), channel_id=1, source_target_pairs={{0,1},{1,0},{2,3},{3,2},{4,5},{5,4},{6,7},{7,6},{8,16},{9,17},{10,... | collective-permute-start | bytes 884744 | tf_op jit(solution)/shard_map/ppermute | solution.py:320
  52.1 15.3 %collective-permute-start.25 = (bf16[4,72,512]{2,1,0:T(8,128)(2,1)S(1)}, bf16[4,72,512]{2,1,0:T(8,128)(2,1)S(1)}, u32[]{:S(2)}, u32[]{:S(2)}) collective-permute-start(bf16[4,72,512]{2,1,0:T(8,128)(2,1)S(1)} %collective-permute-done.24.refs_3_), channel_id=1, source_target_pairs={{0,1},{1,0},{2,3},{3,2},{4,5},{5,4},{6,7},{7,6},{8,16},{9,17},{10,... | collective-permute-start | bytes 884744 | tf_op jit(solution)/shard_map/ppermute | solution.py:320
  58.5 15.3 %collective-permute-start.15 = (bf16[4,72,512]{2,1,0:T(8,128)(2,1)S(1)}, bf16[4,72,512]{2,1,0:T(8,128)(2,1)S(1)}, u32[]{:S(2)}, u32[]{:S(2)}) collective-permute-start(bf16[4,72,512]{2,1,0:T(8,128)(2,1)S(1)} %collective-permute-done.14.refs_2_), channel_id=1, source_target_pairs={{0,1},{1,0},{2,3},{3,2},{4,5},{5,4},{6,7},{7,6},{8,16},{9,17},{10,... | collective-permute-start | bytes 884744 | tf_op jit(solution)/shard_map/ppermute | solution.py:320
  59.6 19.8 %collective-permute-start.30 = (bf16[4,72,512]{2,1,0:T(8,128)(2,1)S(1)}, bf16[4,72,512]{2,1,0:T(8,128)(2,1)S(1)}, u32[]{:S(2)}, u32[]{:S(2)}) collective-permute-start(bf16[4,72,512]{2,1,0:T(8,128)(2,1)S(1)} %collective-permute-done.28.refs_5_), channel_id=1, source_target_pairs={{0,8},{1,9},{2,10},{3,11},{4,12},{5,13},{6,14},{7,15},{8,0},{9,1},... | collective-permute-start | bytes 884744 | tf_op jit(solution)/shard_map/ppermute | solution.py:320
  61.6 17.8 %collective-permute-start.29 = (bf16[4,72,512]{2,1,0:T(8,128)(2,1)S(1)}, bf16[4,72,512]{2,1,0:T(8,128)(2,1)S(1)}, u32[]{:S(2)}, u32[]{:S(2)}) collective-permute-start(bf16[4,72,512]{2,1,0:T(8,128)(2,1)S(1)} %collective-permute-done.27.refs_4_), channel_id=1, source_target_pairs={{0,8},{1,9},{2,10},{3,11},{4,12},{5,13},{6,14},{7,15},{8,0},{9,1},... | collective-permute-start | bytes 884744 | tf_op jit(solution)/shard_map/ppermute | solution.py:320
  67.5 14.2 %collective-permute-start.26 = (bf16[4,72,512]{2,1,0:T(8,128)(2,1)S(1)}, bf16[4,72,512]{2,1,0:T(8,128)(2,1)S(1)}, u32[]{:S(2)}, u32[]{:S(2)}) collective-permute-start(bf16[4,72,512]{2,1,0:T(8,128)(2,1)S(1)} %collective-permute-done.25.refs_7_), channel_id=1, source_target_pairs={{0,8},{1,9},{2,10},{3,11},{4,12},{5,13},{6,14},{7,15},{8,0},{9,1},... | collective-permute-start | bytes 884744 | tf_op jit(solution)/shard_map/ppermute | solution.py:320
  73.8 14.2 %collective-permute-start.16 = (bf16[4,72,512]{2,1,0:T(8,128)(2,1)S(1)}, bf16[4,72,512]{2,1,0:T(8,128)(2,1)S(1)}, u32[]{:S(2)}, u32[]{:S(2)}) collective-permute-start(bf16[4,72,512]{2,1,0:T(8,128)(2,1)S(1)} %collective-permute-done.15.refs_6_), channel_id=1, source_target_pairs={{0,8},{1,9},{2,10},{3,11},{4,12},{5,13},{6,14},{7,15},{8,0},{9,1},... | collective-permute-start | bytes 884744 | tf_op jit(solution)/shard_map/ppermute | solution.py:320

commit v2 on v1

--- a/solution.py
+++ b/solution.py
@@ -10,7 +10,10 @@
 
 
 ITERS = 2
-CHUNKS = 2
+EDGES = (0, 4, 8)
+CHUNKS = len(EDGES) - 1
+SOON = 1
+PAIRED = ((6,), (2, 4))
 
 DECAY = 0.95
 COEF_A = 3.4445
@@ -18,6 +21,8 @@
 COEF_C = 2.0315
 EPSILON = 1e-07
 
+ORDER = (6, 7, 2, 4, 3, 5, 1)
+
 
 VMEM = pl.BlockSpec(memory_space=pltpu.VMEM)
 SMEM = pl.BlockSpec(memory_space=pltpu.SMEM)
@@ -26,6 +31,11 @@
 
 def limit(mib):
     return pltpu.CompilerParams(vmem_limit_bytes=mib * 2**20)
+
+
+def spans(columns):
+    unit = columns // EDGES[-1]
+    return [(unit * a, unit * b) for a, b in zip(EDGES, EDGES[1:])]
 
 
 def near(x):
@@ -76,9 +86,11 @@
 
 
 def send_order(own):
-    if own == 8:
-        return [6, 7, 2, 4, 3, 5, 1]
-    return list(range(own - 1, 0, -1))
+    return [d for d in ORDER if d < own]
+
+
+def parcels(own, chunks):
+    return [(c, d) for c in chunks for d in range(own) if d & -2 == d or d & -2 not in PAIRED[c]]
 
 
 def partner(kind, z, reps):
@@ -142,14 +154,16 @@
     return jnp.sum((mix * mix).reshape(rows // 8, 8, columns), axis=0), flight
 
 
-def mix_kernel(order, *refs):
-    blocks, momentum = refs[: len(order)], refs[len(order)]
-    new_momentum, blend, squares = refs[len(order) + 1 : len(order) + 4]
-    staged, sems = refs[-2:]
+def mix_kernel(order, first, last, *refs):
+    blocks, momentum = refs[: last - first], refs[last - first]
+    new_momentum, blend, squares, staged, sems = refs[-5:]
+    before = refs[last - first + 3] if first else None
     me = lax.axis_index("own")
-    total, flights = jnp.zeros(squares.shape, jnp.float32), []
-    for i, d in enumerate(order):
-        part, flight = mix_block(me, d, i, blocks[i], momentum, staged, i, new_momentum, sems.at[i], blend)
+    total, flights = (before[...] if first else jnp.zeros(squares.shape, jnp.float32)), []
+    for i in range(last - first):
+        part, flight = mix_block(
+            me, order[first + i], first + i, blocks[i], momentum, staged, i, new_momentum, sems.at[i], blend
+        )
         total += part
         flights.append(flight)
     squares[...] = total
@@ -157,23 +171,36 @@
         flight.wait()
 
 
-def update_kernel(order, first, chunks, *refs):
+def finish_chunks(order, chunks, poly, y, at, outs):
+    me = lax.axis_index("own")
+    rows, edges = y.shape[0] // len(order), spans(y.shape[1])
+    factor = 0.2 * math.sqrt(max(y.shape))
+    for c in chunks:
+        part = y[:, edges[c][0] : edges[c][1]]
+        mixed = COEF_A * part.astype(jnp.float32) + jnp.dot(poly, part, preferred_element_type=jnp.float32)
+        scaled = (factor * mixed).astype(jnp.bfloat16)
+        for i, d in enumerate(order):
+            piece = scaled[i * rows : (i + 1) * rows, :]
+            if d & -2 in PAIRED[c]:
+                outs[at[c, d & -2]][(me ^ d) & 1] = piece
+            else:
+                outs[at[c, d]][...] = piece
+
+
+def update_kernel(order, first, *refs):
     late = order[first:]
     blocks, refs = refs[: len(late)], refs[len(late) :]
     momentum, squares = refs[0], refs[3]
-    new_momentum, blend = refs[4:6]
-    outs = refs[6 : 6 + len(order) * chunks]
-    iterate, staged, sems = refs[-3:]
+    new_momentum, blend, iterate = refs[4:7]
+    outs = refs[7 + (SOON < CHUNKS) : -2]
+    staged, sems = refs[-2:]
     me = lax.axis_index("own")
-    rows, columns = blocks[0].shape
-    width = columns // chunks
     sums, flights = squares[...], []
     for i, d in enumerate(late):
         part, flight = mix_block(me, d, first + i, blocks[i], momentum, staged, i, new_momentum, sems.at[i], blend)
         sums += part
         flights.append(flight)
     scale = 1.0 / (jnp.sqrt(jnp.sum(sums, keepdims=True)) + EPSILON)
-    factor = 0.2 * math.sqrt(max(rows * len(order), columns))
     for turn in range(ITERS):
         y = blend[...] if turn == 0 else iterate[...]
         gram32 = lax.dot_general(y, y, (((1,), (1,)), ((), ())), preferred_element_type=jnp.float32)
@@ -182,43 +209,50 @@
         gram = gram32.astype(jnp.bfloat16)
         square = jnp.dot(gram, gram, preferred_element_type=jnp.float32)
         poly = (COEF_B * gram.astype(jnp.float32) + COEF_C * square).astype(jnp.bfloat16)
-        final = turn + 1 == ITERS
-        for c in range(chunks):
-            part = y[:, c * width : (c + 1) * width]
-            mixed = COEF_A * part.astype(jnp.float32) + jnp.dot(poly, part, preferred_element_type=jnp.float32)
-            if turn == 0:
-                mixed = mixed * scale
-            if final:
-                scaled = (factor * mixed).astype(jnp.bfloat16)
-                for i, d in enumerate(order):
-                    outs[c * len(order) + d][...] = scaled[i * rows : (i + 1) * rows, :]
-            else:
-                iterate[:, c * width : (c + 1) * width] = mixed.astype(jnp.bfloat16)
+        if turn + 1 < ITERS:
+            for start, stop in spans(y.shape[1]):
+                part = y[:, start:stop]
+                mixed = COEF_A * part.astype(jnp.float32) + jnp.dot(poly, part, preferred_element_type=jnp.float32)
+                if turn == 0:
+                    mixed = mixed * scale
+                iterate[:, start:stop] = mixed.astype(jnp.bfloat16)
+    if SOON < CHUNKS:
+        refs[7][...] = poly
+    soon = range(SOON)
+    finish_chunks(order, soon, poly, iterate, {key: i for i, key in enumerate(parcels(len(order), soon))}, outs)
     for flight in flights:
         flight.wait()
 
 
-def group_kernel(own, table, *refs):
-    parts, out = refs[:own], refs[own]
+def rest_kernel(order, poly, iterate, *outs):
+    chunks = range(SOON, CHUNKS)
+    at = {key: i for i, key in enumerate(parcels(len(order), chunks))}
+    finish_chunks(order, chunks, poly[...], iterate, at, outs)
+
+
+def group_kernel(table, *refs):
+    *parts, out = refs
     group, me = lax.axis_index("rep"), lax.axis_index("own")
-    for d in range(own):
+    for d, part in enumerate(parts):
         matrix = table[group, me ^ d]
 
         @pl.when(matrix < out.shape[0])
         def _():
-            out[matrix] = parts[d][...]
+            out[matrix] = part[me & 1] if len(part.shape) == 3 else part[...]
 
 
 def place_kernel(reps, where, *refs):
     parts, out, sems = refs[: len(where)], refs[-2], refs[-1]
     group = lax.axis_index("rep")
-    count, _, width = parts[0].shape
+    count = parts[0].shape[0]
+    at_columns = spans(out.shape[2])
     flights = []
     for i, (c, stream, step) in enumerate(where):
         source = group + step * (1 - 2 * lax.rem(group + stream + step + 1, 2))
         here = (source >= 0) & (source < reps)
         at = jnp.clip(source, 0, reps - 1) * count
-        to = out.at[pl.ds(at, count), :, pl.ds(c * width, width)]
+        start, stop = at_columns[c]
+        to = out.at[pl.ds(at, count), :, pl.ds(start, stop - start)]
         flights.append((here, pltpu.make_async_copy(parts[i], to, sems.at[i])))
     for here, copy in flights:
         pl.when(here)(copy.start)
@@ -241,11 +275,11 @@
 
 def chunked_body(own, reps, grads, momentum, owner_table):
     count, rows, columns = grads.shape
-    width = columns // CHUNKS
+    widths = [b - a for a, b in spans(columns)]
     half = jnp.bfloat16
     order = send_order(own)
     arrival = [0, order[-1]] + order[:-1]
-    first = own // 2
+    stages = [0, own // 2, own - 2] if own > 4 else [0, own - 2]
 
     def swap(x, d):
         return lax.ppermute(x, "own", [(i, i ^ d) for i in range(own)])
@@ -268,48 +302,69 @@
     for d in order:
         incoming[d] = swap(outgoing[d], d)
     slots = near(momentum.reshape(own, rows, columns))
-    new_momentum, blend, squares = pl.pallas_call(
-        functools.partial(mix_kernel, arrival[:first]),
-        in_specs=[VMEM] * (first + 1),
-        out_specs=[ANY, VMEM, VMEM],
+    state = []
+    for first, last in zip(stages, stages[1:]):
+        aliases = {last - first + 1: 0, last - first + 2: 1} if first else {}
+        state = pl.pallas_call(
+            functools.partial(mix_kernel, arrival, first, last),
+            in_specs=[VMEM] * (last - first + 1) + ([ANY, VMEM, VMEM] if first else []),
+            out_specs=[ANY, VMEM, VMEM],
+            out_shape=[
+                jax.ShapeDtypeStruct((own, rows, columns), half),
+                pltpu.VMEM((own * rows, columns), half),
+                pltpu.VMEM((8, columns), jnp.float32),
+            ],
+            input_output_aliases=aliases,
+            scratch_shapes=[pltpu.VMEM((last - first, rows, columns), half), pltpu.SemaphoreType.DMA((last - first,))],
+            compiler_params=limit(8),
+        )(*[near(incoming[d]) for d in arrival[first:last]], slots, *state)
+        state = [state[0], near(state[1]), near(state[2])]
+    first = stages[-1]
+    late = own - first
+    shapes = {
+        (c, d): pltpu.VMEM((2,) * (d in PAIRED[c]) + (rows, widths[c]), half) for c, d in parcels(own, range(CHUNKS))
+    }
+    now, rest = parcels(own, range(SOON)), parcels(own, range(SOON, CHUNKS))
+    new_momentum, _, iterate, *parts = pl.pallas_call(
+        functools.partial(update_kernel, arrival, first),
+        in_specs=[VMEM] * (late + 1) + [ANY, VMEM, VMEM],
+        out_specs=[ANY] + [VMEM] * (2 + bool(rest) + len(now)),
         out_shape=[
             jax.ShapeDtypeStruct((own, rows, columns), half),
             pltpu.VMEM((own * rows, columns), half),
-            pltpu.VMEM((8, columns), jnp.float32),
-        ],
-        scratch_shapes=[pltpu.VMEM((first, rows, columns), half), pltpu.SemaphoreType.DMA((first,))],
-        compiler_params=limit(8),
-        name="mix",
-    )(*[near(incoming[d]) for d in arrival[:first]], slots)
-    late = own - first
-    new_momentum, _, *parts = pl.pallas_call(
-        functools.partial(update_kernel, arrival, first, CHUNKS),
-        in_specs=[VMEM] * (late + 1) + [ANY, VMEM, VMEM],
-        out_specs=[ANY] + [VMEM] * (1 + own * CHUNKS),
-        out_shape=[
-            jax.ShapeDtypeStruct((own, rows, columns), half),
             pltpu.VMEM((own * rows, columns), half),
         ]
-        + [pltpu.VMEM((rows, width), half)] * (own * CHUNKS),
+        + [pltpu.VMEM((own * rows, own * rows), half)] * bool(rest)
+        + [shapes[key] for key in now],
         input_output_aliases={late + 1: 0, late + 2: 1},
-        scratch_shapes=[
-            pltpu.VMEM((own * rows, columns), half),
-            pltpu.VMEM((late, rows, columns), half),
-            pltpu.SemaphoreType.DMA((late,)),
-        ],
+        scratch_shapes=[pltpu.VMEM((late, rows, columns), half), pltpu.SemaphoreType.DMA((late,))],
         compiler_params=limit(24),
         name="update",
-    )(*[near(incoming[d]) for d in arrival[first:]], slots, new_momentum, near(blend), near(squares))
+    )(*[near(incoming[d]) for d in arrival[first:]], slots, *state)
+    poly = parts[: bool(rest)]
+    sent = dict(zip(now, parts[bool(rest) :]))
+    if rest:
+        parts = pl.pallas_call(
+            functools.partial(rest_kernel, arrival),
+            in_specs=[VMEM, VMEM],
+            out_specs=[VMEM] * len(rest),
+            out_shape=[shapes[key] for key in rest],
+            compiler_params=limit(16),
+            name="rest",
+        )(near(poly[0]), near(iterate))
+        sent.update(zip(rest, parts))
     held = {}
     for c in range(CHUNKS):
-        back = [parts[c * own]] + [None] * (own - 1)
-        for d in order:
-            back[d] = swap(parts[c * own + d], d)
+        back = [None] * own
+        for k, d in parcels(own, [c]):
+            back[d] = swap(sent[k, d], d) if d else sent[k, d]
+        for d in PAIRED[c]:
+            back[d + 1] = swap(back[d], 1)
         held[c, 0, 0] = pl.pallas_call(
-            functools.partial(group_kernel, own),
+            group_kernel,
             in_specs=[SMEM] + [VMEM] * own,
             out_specs=VMEM,
-            out_shape=pltpu.VMEM((count, rows, width), half),
+            out_shape=pltpu.VMEM((count, rows, widths[c]), half),
             compiler_params=limit(4),
         )(owner_table, *map(near, back))
     pairs = [line_pairs(kind, reps, own) for kind in (0, 1)]
@@ -333,8 +388,8 @@
 
     def step(grads, momentum, owner_table):
         _, total_rows, columns = grads.shape
-        tiled = total_rows % (8 * own) == 0 and columns % (128 * CHUNKS) == 0
-        if not tiled or own & (own - 1) or not 4 <= own <= 8 or reps < 2:
+        tiled = total_rows % (8 * own) == 0 and columns % (128 * EDGES[-1]) == 0
+        if not tiled or own != len(ORDER) + 1 or reps < 3:
             return jax.shard_map(general_body, mesh=mesh, in_specs=in_specs, out_specs=out_specs, check_vma=False)(
                 grads, momentum, owner_table
             )

time: 89 us -> 91.8 us (1.031)
  waiting for transfers between devices: 26 us -> 35.5 us
  starting transfers between devices: 49.6 us -> 42.2 us
    ppermute x21, waiting for transfers between devices: 13.6 us -> 20.3 us  [swap(): return lax.ppermute(x, 'own', [(i, i ^ d) for i in range(own)])]
    ppermute x21, starting transfers between devices: 22.2 us -> 18.2 us  [swap(): return lax.ppermute(x, 'own', [(i, i ^ d) for i in range(own)])]
    ppermute x10, starting transfers between devices: 27.4 us -> 24 us  [chunked_body(): lax.ppermute(behind, ('rep', 'own'), pairs[(stream + step + 1) % 2])]
    ppermute x10, waiting for transfers between devices: 12.4 us -> 15.2 us  [chunked_body(): lax.ppermute(behind, ('rep', 'own'), pairs[(stream + step + 1) % 2])]
    pallas_call x4 -> x6, Pallas kernels: 8.78 us -> 9.51 us  [the longest x1 5.86 us: chunked_body(): pl.pallas_call(functools.partial(update_kernel, arrival, first), in_specs...]
  transfers between devices with their start and end apart: 31 -> 31, of which waited for: 13 -> 15; matrix products, arithmetic and copies ran while one was open for 0% -> 0% of each run, Pallas kernels for 4% -> 5%
where the time goes in v2:
time: 91.8 us; the launch traced here: 91.7 us
  starting transfers between devices  42.2 us (46%)
  waiting for transfers between devices  35.5 us (39%)
  Pallas kernels  13.2 us (14%)
    ppermute x10, starting transfers between devices, chunked_body(): lax.ppermute(behind, ('rep', 'own'), pairs[(stream + step + 1) % 2])  24 us
    ppermute x21, waiting for transfers between devices, swap(): return lax.ppermute(x, 'own', [(i, i ^ d) for i in range(own)])  20.3 us
    ppermute x21, starting transfers between devices, swap(): return lax.ppermute(x, 'own', [(i, i ^ d) for i in range(own)])  18.2 us
    ppermute x10, waiting for transfers between devices, chunked_body(): lax.ppermute(behind, ('rep', 'own'), pairs[(stream + step + 1) % 2])  15.2 us
    pallas_call x1, Pallas kernels, chunked_body(): pl.pallas_call(functools.partial(update_kernel, arrival, first), in_specs...  5.86 us
    pallas_call x2, Pallas kernels, place(): pl.pallas_call(functools.partial(place_kernel, reps, where), in_specs=[VM...  2.11 us
  transfers between devices with their start and end apart: 31, of which 15 were waited for; matrix products, arithmetic and copies ran while one was open for 0% of the time, Pallas kernels for 5%

profile of v2, /device:TPU:0, one launch (start us, length us, event | category | flops | bytes accessed | tf_op | source)
XLA Modules:
  0.0 91.7 jit_solution(15082109356196937088)
XLA Ops:
  0.6 1.6 %pack.1 = (bf16[72,1024]{1,0:T(8,128)(2,1)S(1)}, bf16[72,1024]{1,0:T(8,128)(2,1)S(1)}, bf16[72,1024]{1,0:T(8,128)(2,1)S(1)}, bf16[72,1024]{1,0:T(8,128)(2,1)S(1)...) custom-call(s32[4,8]{1,0:T(4,128)} %table.3, ...), custom_call_target="tpu_custom_call" | custom-call | tf_op jit(solution)/shard_map/pack/pallas_call | solution.py:287
  2.2 0.6 collective-permute-start.4
  2.8 3.5 %collective-permute-start.5 = (bf16[72,1024]{1,0:T(8,128)(2,1)S(1)}, bf16[72,1024]{1,0:T(8,128)(2,1)S(1)}, u32[]{:S(2)}, u32[]{:S(2)}) collective-permute-start(bf16[72,1024]{1,0:T(8,128)(2,1)S(1)} %get-tuple-element.38), channel_id=1, source_target_pairs={{0,6},{1,7},{2,4},{3,5},{4,2},{5,3},{6,0},{7,1},{8,14},{9,15},{10,... | collective-permute-start | bytes 442376 | tf_op jit(solution)/shard_map/ppermute | solution.py:285
  6.3 0.0 collective-permute-start.6
  6.3 1.7 %collective-permute-start.2 = (bf16[72,1024]{1,0:T(8,128)(2,1)S(1)}, bf16[72,1024]{1,0:T(8,128)(2,1)S(1)}, u32[]{:S(2)}, u32[]{:S(2)}) collective-permute-start(bf16[72,1024]{1,0:T(8,128)(2,1)S(1)} %get-tuple-element.34), channel_id=1, source_target_pairs={{0,2},{1,3},{2,0},{3,1},{4,6},{5,7},{6,4},{7,5},{8,10},{9,11},{10,... | collective-permute-start | bytes 442376 | tf_op jit(solution)/shard_map/ppermute | solution.py:285
  8.0 1.5 %collective-permute-start.3 = (bf16[72,1024]{1,0:T(8,128)(2,1)S(1)}, bf16[72,1024]{1,0:T(8,128)(2,1)S(1)}, u32[]{:S(2)}, u32[]{:S(2)}) collective-permute-start(bf16[72,1024]{1,0:T(8,128)(2,1)S(1)} %get-tuple-element.35), channel_id=1, source_target_pairs={{0,4},{1,5},{2,6},{3,7},{4,0},{5,1},{6,2},{7,3},{8,12},{9,13},{10,... | collective-permute-start | bytes 442376 | tf_op jit(solution)/shard_map/ppermute | solution.py:285
  9.5 1.5 %collective-permute-done.5.refs_2_ = bf16[72,1024]{1,0:T(8,128)(2,1)S(1)} collective-permute-done((bf16[72,1024]{1,0:T(8,128)(2,1)S(1)}, bf16[72,1024]{1,0:T(8,128)(2,1)S(1)}, u32[]{:S(2)}, u32[]{:S(2)}) %collective-permute-start.5) | collective-permute-done | bytes 147488 | tf_op jit(solution)/shard_map/ppermute | solution.py:285
  11.0 0.6 collective-permute-start.1
  11.6 2.1 %collective-permute-done.6.refs_3_ = bf16[72,1024]{1,0:T(8,128)(2,1)S(1)} collective-permute-done((bf16[72,1024]{1,0:T(8,128)(2,1)S(1)}, bf16[72,1024]{1,0:T(8,128)(2,1)S(1)}, u32[]{:S(2)}, u32[]{:S(2)}) %collective-permute-start.6) | collective-permute-done | bytes 147488 | tf_op jit(solution)/shard_map/ppermute | solution.py:285
  13.7 0.9 shard_map.50
  14.6 3.2 %collective-permute-done.2.refs_0_ = bf16[72,1024]{1,0:T(8,128)(2,1)S(1)} collective-permute-done((bf16[72,1024]{1,0:T(8,128)(2,1)S(1)}, bf16[72,1024]{1,0:T(8,128)(2,1)S(1)}, u32[]{:S(2)}, u32[]{:S(2)}) %collective-permute-start.2) | collective-permute-done | bytes 147488 | tf_op jit(solution)/shard_map/ppermute | solution.py:285
  17.9 0.0 collective-permute-done.3.refs_1_
  17.9 0.8 shard_map.51
  18.7 1.3 %collective-permute-done.refs_0_ = bf16[72,1024]{1,0:T(8,128)(2,1)S(1)} collective-permute-done((bf16[72,1024]{1,0:T(8,128)(2,1)S(1)}, bf16[72,1024]{1,0:T(8,128)(2,1)S(1)}, u32[]{:S(2)}, u32[]{:S(2)}) %collective-permute-start) | collective-permute-done | bytes 147488 | tf_op jit(solution)/shard_map/ppermute | solution.py:285
  20.0 0.2 collective-permute-done.1.refs_1_
  20.1 5.9 %update.1 = (bf16[8,72,1024]{2,1,0:T(8,128)(2,1)}, bf16[576,1024]{1,0:T(8,128)(2,1)S(1)}, bf16[576,1024]{1,0:T(8,128)(2,1)S(1)}, bf16[576,576]{1,0:T(8,128)(2,1)...) custom-call(bf16[72,1024]{1,0:T(8,128)(2,1)S(1)} %collective-permute, ...), custom_call_target="tpu_custom_call", output_to_operand_aliasing={{0}: (3, {}), {1}: (4, {})} | custom-call | tf_op jit(solution)/shard_map/update/pallas_call | solution.py:328
  26.0 0.0 copy-start.1
  26.0 2.7 %collective-permute-start.12 = (bf16[2,72,512]{2,1,0:T(8,128)(2,1)S(1)}, bf16[2,72,512]{2,1,0:T(8,128)(2,1)S(1)}, u32[]{:S(2)}, u32[]{:S(2)}) collective-permute-start(bf16[2,72,512]{2,1,0:T(8,128)(2,1)S(1)} %get-tuple-element.53), channel_id=1, source_target_pairs={{0,6},{1,7},{2,4},{3,5},{4,2},{5,3},{6,0},{7,1},{8,14},{9,15},{10,... | collective-permute-start | bytes 442376 | tf_op jit(solution)/shard_map/ppermute | solution.py:285
  28.7 0.0 collective-permute-start.7
  28.7 0.6 rest.1
  29.3 0.6 collective-permute-start.18
  29.9 0.3 collective-permute-start.20
  30.2 1.7 %collective-permute-start.8 = (bf16[72,512]{1,0:T(8,128)(2,1)S(1)}, bf16[72,512]{1,0:T(8,128)(2,1)S(1)}, u32[]{:S(2)}, u32[]{:S(2)}) collective-permute-start(bf16[72,512]{1,0:T(8,128)(2,1)S(1)} %get-tuple-element.49), channel_id=1, source_target_pairs={{0,2},{1,3},{2,0},{3,1},{4,6},{5,7},{6,4},{7,5},{8,10},{9,11},{10,... | collective-permute-start | bytes 221192 | tf_op jit(solution)/shard_map/ppermute | solution.py:285
  31.9 0.0 collective-permute-done.7.refs_1_
  31.9 0.0 collective-permute-start.9
  31.9 1.5 %collective-permute-done.12.refs_6_ = bf16[2,72,512]{2,1,0:T(8,128)(2,1)S(1)} collective-permute-done((bf16[2,72,512]{2,1,0:T(8,128)(2,1)S(1)}, bf16[2,72,512]{2,1,0:T(8,128)(2,1)S(1)}, u32[]{:S(2)}, u32[]{:S(2)}) %collective-permute-start.12) | collective-permute-done | bytes 147488 | tf_op jit(solution)/shard_map/ppermute | solution.py:285
  33.4 0.0 collective-permute-start.13
  33.4 5.0 %collective-permute-done.8.refs_2_ = bf16[72,512]{1,0:T(8,128)(2,1)S(1)} collective-permute-done((bf16[72,512]{1,0:T(8,128)(2,1)S(1)}, bf16[72,512]{1,0:T(8,128)(2,1)S(1)}, u32[]{:S(2)}, u32[]{:S(2)}) %collective-permute-start.8) | collective-permute-done | bytes 73760 | tf_op jit(solution)/shard_map/ppermute | solution.py:285
  38.4 0.3 collective-permute-start.10
  38.7 0.1 collective-permute-done.9.refs_3_
  38.8 0.4 collective-permute-start.11
  39.2 0.0 collective-permute-done.18.refs_2_
  39.2 1.3 %collective-permute-start.19 = (bf16[2,72,512]{2,1,0:T(8,128)(2,1)S(1)}, bf16[2,72,512]{2,1,0:T(8,128)(2,1)S(1)}, u32[]{:S(2)}, u32[]{:S(2)}) collective-permute-start(bf16[2,72,512]{2,1,0:T(8,128)(2,1)S(1)} %collective-permute-done.18.refs_2_), channel_id=1, source_target_pairs={{0,1},{1,0},{2,3},{3,2},{4,5},{5,4},{6,7},{7,6},{8,9},{9,8},{10,11... | collective-permute-start | bytes 442376 | tf_op jit(solution)/shard_map/ppermute | solution.py:285
  40.5 0.1 collective-permute-start.21
  40.6 2.8 %collective-permute-done.10.refs_4_ = bf16[72,512]{1,0:T(8,128)(2,1)S(1)} collective-permute-done((bf16[72,512]{1,0:T(8,128)(2,1)S(1)}, bf16[72,512]{1,0:T(8,128)(2,1)S(1)}, u32[]{:S(2)}, u32[]{:S(2)}) %collective-permute-start.10) | collective-permute-done | bytes 73760 | tf_op jit(solution)/shard_map/ppermute | solution.py:285
  43.4 0.0 collective-permute-start.17
  43.4 0.0 collective-permute-done.11.refs_5_
  43.4 2.6 %collective-permute-start.22 = (bf16[72,512]{1,0:T(8,128)(2,1)S(1)}, bf16[72,512]{1,0:T(8,128)(2,1)S(1)}, u32[]{:S(2)}, u32[]{:S(2)}) collective-permute-start(bf16[72,512]{1,0:T(8,128)(2,1)S(1)} %get-tuple-element.60), channel_id=1, source_target_pairs={{0,6},{1,7},{2,4},{3,5},{4,2},{5,3},{6,0},{7,1},{8,14},{9,15},{10,... | collective-permute-start | bytes 221192 | tf_op jit(solution)/shard_map/ppermute | solution.py:285
  46.0 0.0 collective-permute-done.13.refs_7_
  46.0 0.3 collective-permute-start.23
  46.2 0.7 shard_map.52.refs_0_
  46.9 1.7 %collective-permute-start.14 = (bf16[4,72,512]{2,1,0:T(8,128)(2,1)S(1)}, bf16[4,72,512]{2,1,0:T(8,128)(2,1)S(1)}, u32[]{:S(2)}, u32[]{:S(2)}) collective-permute-start(bf16[4,72,512]{2,1,0:T(8,128)(2,1)S(1)} %shard_map.52.refs_0_), channel_id=1, source_target_pairs={{0,8},{1,9},{2,10},{3,11},{4,12},{5,13},{6,14},{7,15},{8,0},{9,1},... | collective-permute-start | bytes 884744 | tf_op jit(solution)/shard_map/ppermute | solution.py:375
  48.7 0.4 collective-permute-done.22.refs_6_
  49.1 2.2 %collective-permute-done.23.refs_7_ = bf16[72,512]{1,0:T(8,128)(2,1)S(1)} collective-permute-done((bf16[72,512]{1,0:T(8,128)(2,1)S(1)}, bf16[72,512]{1,0:T(8,128)(2,1)S(1)}, u32[]{:S(2)}, u32[]{:S(2)}) %collective-permute-start.23) | collective-permute-done | bytes 73760 | tf_op jit(solution)/shard_map/ppermute | solution.py:285
  51.3 0.0 collective-permute-done.19.refs_3_
  51.3 0.0 collective-permute-done.21.refs_5_
  51.3 0.7 shard_map.53.refs_1_
  52.0 1.6 %collective-permute-start.24 = (bf16[4,72,512]{2,1,0:T(8,128)(2,1)S(1)}, bf16[4,72,512]{2,1,0:T(8,128)(2,1)S(1)}, u32[]{:S(2)}, u32[]{:S(2)}) collective-permute-start(bf16[4,72,512]{2,1,0:T(8,128)(2,1)S(1)} %shard_map.53.refs_1_), channel_id=1, source_target_pairs={{0,8},{1,9},{2,10},{3,11},{4,12},{5,13},{6,14},{7,15},{8,0},{9,1},... | collective-permute-start | bytes 884744 | tf_op jit(solution)/shard_map/ppermute | solution.py:375
  53.6 0.5 collective-permute-start.28
  54.1 2.7 %collective-permute-done.14.refs_2_ = bf16[4,72,512]{2,1,0:T(8,128)(2,1)S(1)} collective-permute-done((bf16[4,72,512]{2,1,0:T(8,128)(2,1)S(1)}, bf16[4,72,512]{2,1,0:T(8,128)(2,1)S(1)}, u32[]{:S(2)}, u32[]{:S(2)}) %collective-permute-start.14) | collective-permute-done | bytes 294944 | tf_op jit(solution)/shard_map/ppermute | solution.py:375
  56.9 0.0 collective-permute-start.15
  56.9 5.5 %collective-permute-done.24.refs_3_ = bf16[4,72,512]{2,1,0:T(8,128)(2,1)S(1)} collective-permute-done((bf16[4,72,512]{2,1,0:T(8,128)(2,1)S(1)}, bf16[4,72,512]{2,1,0:T(8,128)(2,1)S(1)}, u32[]{:S(2)}, u32[]{:S(2)}) %collective-permute-start.24) | collective-permute-done | bytes 294944 | tf_op jit(solution)/shard_map/ppermute | solution.py:375
  62.4 0.0 collective-permute-start.25
  62.4 3.2 %collective-permute-start.29 = (bf16[4,72,512]{2,1,0:T(8,128)(2,1)S(1)}, bf16[4,72,512]{2,1,0:T(8,128)(2,1)S(1)}, u32[]{:S(2)}, u32[]{:S(2)}) collective-permute-start(bf16[4,72,512]{2,1,0:T(8,128)(2,1)S(1)} %collective-permute-done.27.refs_4_), channel_id=1, source_target_pairs={{0,8},{1,9},{2,10},{3,11},{4,12},{5,13},{6,14},{7,15},{8,0},{9,1},... | collective-permute-start | bytes 884744 | tf_op jit(solution)/shard_map/ppermute | solution.py:375
  65.7 0.0 collective-permute-done.28.refs_5_
  65.7 5.3 %collective-permute-start.30 = (bf16[4,72,512]{2,1,0:T(8,128)(2,1)S(1)}, bf16[4,72,512]{2,1,0:T(8,128)(2,1)S(1)}, u32[]{:S(2)}, u32[]{:S(2)}) collective-permute-start(bf16[4,72,512]{2,1,0:T(8,128)(2,1)S(1)} %collective-permute-done.28.refs_5_), channel_id=1, source_target_pairs={{0,8},{1,9},{2,10},{3,11},{4,12},{5,13},{6,14},{7,15},{8,0},{9,1},... | collective-permute-start | bytes 884744 | tf_op jit(solution)/shard_map/ppermute | solution.py:375
  71.0 6.3 %collective-permute-start.16 = (bf16[4,72,512]{2,1,0:T(8,128)(2,1)S(1)}, bf16[4,72,512]{2,1,0:T(8,128)(2,1)S(1)}, u32[]{:S(2)}, u32[]{:S(2)}) collective-permute-start(bf16[4,72,512]{2,1,0:T(8,128)(2,1)S(1)} %collective-permute-done.15.refs_6_), channel_id=1, source_target_pairs={{0,8},{1,9},{2,10},{3,11},{4,12},{5,13},{6,14},{7,15},{8,0},{9,1},... | collective-permute-start | bytes 884744 | tf_op jit(solution)/shard_map/ppermute | solution.py:375
  77.3 5.3 %collective-permute-start.26 = (bf16[4,72,512]{2,1,0:T(8,128)(2,1)S(1)}, bf16[4,72,512]{2,1,0:T(8,128)(2,1)S(1)}, u32[]{:S(2)}, u32[]{:S(2)}) collective-permute-start(bf16[4,72,512]{2,1,0:T(8,128)(2,1)S(1)} %collective-permute-done.25.refs_7_), channel_id=1, source_target_pairs={{0,8},{1,9},{2,10},{3,11},{4,12},{5,13},{6,14},{7,15},{8,0},{9,1},... | collective-permute-start | bytes 884744 | tf_op jit(solution)/shard_map/ppermute | solution.py:375
  82.6 0.0 collective-permute-done.29.refs_8_
  82.6 0.0 collective-permute-done.30.refs_9_
  82.6 1.3 %shard_map.54.refs_2_ = bf16[16,72,1024]{2,1,0:T(8,128)(2,1)} custom-call(bf16[4,72,512]{2,1,0:T(8,128)(2,1)S(1)} %shard_map.52.refs_0_, bf16[4,72,512]{2,1,0:T(8,128)(2,1)S(1)} %shard_map.53.refs_1_, bf16[4,72,512]{2,1,0:T(8,128)(2,1)S(1)} %collective-permute-done.14.refs_2_, bf16[4,72,512]{2,1,0:T(8,128)(2,1)S(1)} %collective-permute-done.24.refs_3_, ...), custom_call_target="tpu_custom_call" | custom-call | tf_op jit(solution)/shard_map/pallas_call | solution.py:265
  83.9 2.3 %collective-permute-done.16.refs_0_ = bf16[4,72,512]{2,1,0:T(8,128)(2,1)S(1)} collective-permute-done((bf16[4,72,512]{2,1,0:T(8,128)(2,1)S(1)}, bf16[4,72,512]{2,1,0:T(8,128)(2,1)S(1)}, u32[]{:S(2)}, u32[]{:S(2)}) %collective-permute-start.16) | collective-permute-done | bytes 294944 | tf_op jit(solution)/shard_map/ppermute | solution.py:375
  86.2 4.7 %collective-permute-done.26.refs_1_ = bf16[4,72,512]{2,1,0:T(8,128)(2,1)S(1)} collective-permute-done((bf16[4,72,512]{2,1,0:T(8,128)(2,1)S(1)}, bf16[4,72,512]{2,1,0:T(8,128)(2,1)S(1)}, u32[]{:S(2)}, u32[]{:S(2)}) %collective-permute-start.26) | collective-permute-done | bytes 294944 | tf_op jit(solution)/shard_map/ppermute | solution.py:375
  90.8 0.8 shard_map.55
  (11 shorter events, 0.0 us)
Async XLA Ops:
  0.6 13.1 %copy-start = (bf16[1,576,1024]{2,1,0:T(8,128)(2,1)S(1)}, bf16[1,576,1024]{2,1,0:T(8,128)(2,1)}, u32[]{:S(2)}) copy-start(bf16[1,576,1024]{2,1,0:T(8,128)(2,1)} %param.4) | copy-start | bytes 3538948
  2.2 7.3 %collective-permute-start.4 = (bf16[72,1024]{1,0:T(8,128)(2,1)S(1)}, bf16[72,1024]{1,0:T(8,128)(2,1)S(1)}, u32[]{:S(2)}, u32[]{:S(2)}) collective-permute-start(bf16[72,1024]{1,0:T(8,128)(2,1)S(1)} %get-tuple-element.37), channel_id=1, source_target_pairs={{0,1},{1,0},{2,3},{3,2},{4,5},{5,4},{6,7},{7,6},{8,9},{9,8},{10,11... | collective-permute-start | bytes 442376 | tf_op jit(solution)/shard_map/ppermute | solution.py:285
  2.8 8.2 %collective-permute-start.5 = (bf16[72,1024]{1,0:T(8,128)(2,1)S(1)}, bf16[72,1024]{1,0:T(8,128)(2,1)S(1)}, u32[]{:S(2)}, u32[]{:S(2)}) collective-permute-start(bf16[72,1024]{1,0:T(8,128)(2,1)S(1)} %get-tuple-element.38), channel_id=1, source_target_pairs={{0,6},{1,7},{2,4},{3,5},{4,2},{5,3},{6,0},{7,1},{8,14},{9,15},{10,... | collective-permute-start | bytes 442376 | tf_op jit(solution)/shard_map/ppermute | solution.py:285
  6.3 7.4 %collective-permute-start.6 = (bf16[72,1024]{1,0:T(8,128)(2,1)S(1)}, bf16[72,1024]{1,0:T(8,128)(2,1)S(1)}, u32[]{:S(2)}, u32[]{:S(2)}) collective-permute-start(bf16[72,1024]{1,0:T(8,128)(2,1)S(1)} %get-tuple-element.39), channel_id=1, source_target_pairs={{0,7},{1,6},{2,5},{3,4},{4,3},{5,2},{6,1},{7,0},{8,15},{9,14},{10,... | collective-permute-start | bytes 442376 | tf_op jit(solution)/shard_map/ppermute | solution.py:285
  6.3 11.6 %collective-permute-start.2 = (bf16[72,1024]{1,0:T(8,128)(2,1)S(1)}, bf16[72,1024]{1,0:T(8,128)(2,1)S(1)}, u32[]{:S(2)}, u32[]{:S(2)}) collective-permute-start(bf16[72,1024]{1,0:T(8,128)(2,1)S(1)} %get-tuple-element.34), channel_id=1, source_target_pairs={{0,2},{1,3},{2,0},{3,1},{4,6},{5,7},{6,4},{7,5},{8,10},{9,11},{10,... | collective-permute-start | bytes 442376 | tf_op jit(solution)/shard_map/ppermute | solution.py:285
  8.0 9.9 %collective-permute-start.3 = (bf16[72,1024]{1,0:T(8,128)(2,1)S(1)}, bf16[72,1024]{1,0:T(8,128)(2,1)S(1)}, u32[]{:S(2)}, u32[]{:S(2)}) collective-permute-start(bf16[72,1024]{1,0:T(8,128)(2,1)S(1)} %get-tuple-element.35), channel_id=1, source_target_pairs={{0,4},{1,5},{2,6},{3,7},{4,0},{5,1},{6,2},{7,3},{8,12},{9,13},{10,... | collective-permute-start | bytes 442376 | tf_op jit(solution)/shard_map/ppermute | solution.py:285
  9.5 10.4 %collective-permute-start = (bf16[72,1024]{1,0:T(8,128)(2,1)S(1)}, bf16[72,1024]{1,0:T(8,128)(2,1)S(1)}, u32[]{:S(2)}, u32[]{:S(2)}) collective-permute-start(bf16[72,1024]{1,0:T(8,128)(2,1)S(1)} %get-tuple-element.32), channel_id=1, source_target_pairs={{0,3},{1,2},{2,1},{3,0},{4,7},{5,6},{6,5},{7,4},{8,11},{9,10},{10,... | collective-permute-start | bytes 442376 | tf_op jit(solution)/shard_map/ppermute | solution.py:285
  11.0 9.1 %collective-permute-start.1 = (bf16[72,1024]{1,0:T(8,128)(2,1)S(1)}, bf16[72,1024]{1,0:T(8,128)(2,1)S(1)}, u32[]{:S(2)}, u32[]{:S(2)}) collective-permute-start(bf16[72,1024]{1,0:T(8,128)(2,1)S(1)} %get-tuple-element.33), channel_id=1, source_target_pairs={{0,5},{1,4},{2,7},{3,6},{4,1},{5,0},{6,3},{7,2},{8,13},{9,12},{10,... | collective-permute-start | bytes 442376 | tf_op jit(solution)/shard_map/ppermute | solution.py:285
  26.0 20.3 %copy-start.1 = (s32[4,8]{1,0:T(4,128)S(1)}, s32[4,8]{1,0:T(4,128)}, u32[]{:S(2)}) copy-start(s32[4,8]{1,0:T(4,128)} %table.3) | copy-start | bytes 388
  26.0 7.4 %collective-permute-start.12 = (bf16[2,72,512]{2,1,0:T(8,128)(2,1)S(1)}, bf16[2,72,512]{2,1,0:T(8,128)(2,1)S(1)}, u32[]{:S(2)}, u32[]{:S(2)}) collective-permute-start(bf16[2,72,512]{2,1,0:T(8,128)(2,1)S(1)} %get-tuple-element.53), channel_id=1, source_target_pairs={{0,6},{1,7},{2,4},{3,5},{4,2},{5,3},{6,0},{7,1},{8,14},{9,15},{10,... | collective-permute-start | bytes 442376 | tf_op jit(solution)/shard_map/ppermute | solution.py:285
  28.7 3.2 %collective-permute-start.7 = (bf16[72,512]{1,0:T(8,128)(2,1)S(1)}, bf16[72,512]{1,0:T(8,128)(2,1)S(1)}, u32[]{:S(2)}, u32[]{:S(2)}) collective-permute-start(bf16[72,512]{1,0:T(8,128)(2,1)S(1)} %get-tuple-element.48), channel_id=1, source_target_pairs={{0,1},{1,0},{2,3},{3,2},{4,5},{5,4},{6,7},{7,6},{8,9},{9,8},{10,11... | collective-permute-start | bytes 221192 | tf_op jit(solution)/shard_map/ppermute | solution.py:285
  29.3 9.9 %collective-permute-start.18 = (bf16[2,72,512]{2,1,0:T(8,128)(2,1)S(1)}, bf16[2,72,512]{2,1,0:T(8,128)(2,1)S(1)}, u32[]{:S(2)}, u32[]{:S(2)}) collective-permute-start(bf16[2,72,512]{2,1,0:T(8,128)(2,1)S(1)} %get-tuple-element.58), channel_id=1, source_target_pairs={{0,2},{1,3},{2,0},{3,1},{4,6},{5,7},{6,4},{7,5},{8,10},{9,11},{10,... | collective-permute-start | bytes 442376 | tf_op jit(solution)/shard_map/ppermute | solution.py:285
  29.9 10.6 %collective-permute-start.20 = (bf16[2,72,512]{2,1,0:T(8,128)(2,1)S(1)}, bf16[2,72,512]{2,1,0:T(8,128)(2,1)S(1)}, u32[]{:S(2)}, u32[]{:S(2)}) collective-permute-start(bf16[2,72,512]{2,1,0:T(8,128)(2,1)S(1)} %get-tuple-element.59), channel_id=1, source_target_pairs={{0,4},{1,5},{2,6},{3,7},{4,0},{5,1},{6,2},{7,3},{8,12},{9,13},{10,... | collective-permute-start | bytes 442376 | tf_op jit(solution)/shard_map/ppermute | solution.py:285
  30.2 8.1 %collective-permute-start.8 = (bf16[72,512]{1,0:T(8,128)(2,1)S(1)}, bf16[72,512]{1,0:T(8,128)(2,1)S(1)}, u32[]{:S(2)}, u32[]{:S(2)}) collective-permute-start(bf16[72,512]{1,0:T(8,128)(2,1)S(1)} %get-tuple-element.49), channel_id=1, source_target_pairs={{0,2},{1,3},{2,0},{3,1},{4,6},{5,7},{6,4},{7,5},{8,10},{9,11},{10,... | collective-permute-start | bytes 221192 | tf_op jit(solution)/shard_map/ppermute | solution.py:285
  31.9 6.9 %collective-permute-start.9 = (bf16[72,512]{1,0:T(8,128)(2,1)S(1)}, bf16[72,512]{1,0:T(8,128)(2,1)S(1)}, u32[]{:S(2)}, u32[]{:S(2)}) collective-permute-start(bf16[72,512]{1,0:T(8,128)(2,1)S(1)} %get-tuple-element.50), channel_id=1, source_target_pairs={{0,3},{1,2},{2,1},{3,0},{4,7},{5,6},{6,5},{7,4},{8,11},{9,10},{10,... | collective-permute-start | bytes 221192 | tf_op jit(solution)/shard_map/ppermute | solution.py:285
  33.4 12.6 %collective-permute-start.13 = (bf16[2,72,512]{2,1,0:T(8,128)(2,1)S(1)}, bf16[2,72,512]{2,1,0:T(8,128)(2,1)S(1)}, u32[]{:S(2)}, u32[]{:S(2)}) collective-permute-start(bf16[2,72,512]{2,1,0:T(8,128)(2,1)S(1)} %collective-permute-done.12.refs_6_), channel_id=1, source_target_pairs={{0,1},{1,0},{2,3},{3,2},{4,5},{5,4},{6,7},{7,6},{8,9},{9,8},{10,11... | collective-permute-start | bytes 442376 | tf_op jit(solution)/shard_map/ppermute | solution.py:285
  38.4 5.0 %collective-permute-start.10 = (bf16[72,512]{1,0:T(8,128)(2,1)S(1)}, bf16[72,512]{1,0:T(8,128)(2,1)S(1)}, u32[]{:S(2)}, u32[]{:S(2)}) collective-permute-start(bf16[72,512]{1,0:T(8,128)(2,1)S(1)} %get-tuple-element.51), channel_id=1, source_target_pairs={{0,4},{1,5},{2,6},{3,7},{4,0},{5,1},{6,2},{7,3},{8,12},{9,13},{10,... | collective-permute-start | bytes 221192 | tf_op jit(solution)/shard_map/ppermute | solution.py:285
  38.8 4.6 %collective-permute-start.11 = (bf16[72,512]{1,0:T(8,128)(2,1)S(1)}, bf16[72,512]{1,0:T(8,128)(2,1)S(1)}, u32[]{:S(2)}, u32[]{:S(2)}) collective-permute-start(bf16[72,512]{1,0:T(8,128)(2,1)S(1)} %get-tuple-element.52), channel_id=1, source_target_pairs={{0,5},{1,4},{2,7},{3,6},{4,1},{5,0},{6,3},{7,2},{8,13},{9,12},{10,... | collective-permute-start | bytes 221192 | tf_op jit(solution)/shard_map/ppermute | solution.py:285
  39.2 12.1 %collective-permute-start.19 = (bf16[2,72,512]{2,1,0:T(8,128)(2,1)S(1)}, bf16[2,72,512]{2,1,0:T(8,128)(2,1)S(1)}, u32[]{:S(2)}, u32[]{:S(2)}) collective-permute-start(bf16[2,72,512]{2,1,0:T(8,128)(2,1)S(1)} %collective-permute-done.18.refs_2_), channel_id=1, source_target_pairs={{0,1},{1,0},{2,3},{3,2},{4,5},{5,4},{6,7},{7,6},{8,9},{9,8},{10,11... | collective-permute-start | bytes 442376 | tf_op jit(solution)/shard_map/ppermute | solution.py:285
  40.5 10.8 %collective-permute-start.21 = (bf16[2,72,512]{2,1,0:T(8,128)(2,1)S(1)}, bf16[2,72,512]{2,1,0:T(8,128)(2,1)S(1)}, u32[]{:S(2)}, u32[]{:S(2)}) collective-permute-start(bf16[2,72,512]{2,1,0:T(8,128)(2,1)S(1)} %collective-permute-done.20.refs_4_), channel_id=1, source_target_pairs={{0,1},{1,0},{2,3},{3,2},{4,5},{5,4},{6,7},{7,6},{8,9},{9,8},{10,11... | collective-permute-start | bytes 442376 | tf_op jit(solution)/shard_map/ppermute | solution.py:285
  43.4 3.5 %collective-permute-start.17 = (bf16[72,512]{1,0:T(8,128)(2,1)S(1)}, bf16[72,512]{1,0:T(8,128)(2,1)S(1)}, u32[]{:S(2)}, u32[]{:S(2)}) collective-permute-start(bf16[72,512]{1,0:T(8,128)(2,1)S(1)} %get-tuple-element.57), channel_id=1, source_target_pairs={{0,1},{1,0},{2,3},{3,2},{4,5},{5,4},{6,7},{7,6},{8,9},{9,8},{10,11... | collective-permute-start | bytes 221192 | tf_op jit(solution)/shard_map/ppermute | solution.py:285
  43.4 5.7 %collective-permute-start.22 = (bf16[72,512]{1,0:T(8,128)(2,1)S(1)}, bf16[72,512]{1,0:T(8,128)(2,1)S(1)}, u32[]{:S(2)}, u32[]{:S(2)}) collective-permute-start(bf16[72,512]{1,0:T(8,128)(2,1)S(1)} %get-tuple-element.60), channel_id=1, source_target_pairs={{0,6},{1,7},{2,4},{3,5},{4,2},{5,3},{6,0},{7,1},{8,14},{9,15},{10,... | collective-permute-start | bytes 221192 | tf_op jit(solution)/shard_map/ppermute | solution.py:285
  46.0 5.3 %collective-permute-start.23 = (bf16[72,512]{1,0:T(8,128)(2,1)S(1)}, bf16[72,512]{1,0:T(8,128)(2,1)S(1)}, u32[]{:S(2)}, u32[]{:S(2)}) collective-permute-start(bf16[72,512]{1,0:T(8,128)(2,1)S(1)} %get-tuple-element.61), channel_id=1, source_target_pairs={{0,7},{1,6},{2,5},{3,4},{4,3},{5,2},{6,1},{7,0},{8,15},{9,14},{10,... | collective-permute-start | bytes 221192 | tf_op jit(solution)/shard_map/ppermute | solution.py:285
  46.9 9.9 %collective-permute-start.14 = (bf16[4,72,512]{2,1,0:T(8,128)(2,1)S(1)}, bf16[4,72,512]{2,1,0:T(8,128)(2,1)S(1)}, u32[]{:S(2)}, u32[]{:S(2)}) collective-permute-start(bf16[4,72,512]{2,1,0:T(8,128)(2,1)S(1)} %shard_map.52.refs_0_), channel_id=1, source_target_pairs={{0,8},{1,9},{2,10},{3,11},{4,12},{5,13},{6,14},{7,15},{8,0},{9,1},... | collective-permute-start | bytes 884744 | tf_op jit(solution)/shard_map/ppermute | solution.py:375
  52.0 10.4 %collective-permute-start.24 = (bf16[4,72,512]{2,1,0:T(8,128)(2,1)S(1)}, bf16[4,72,512]{2,1,0:T(8,128)(2,1)S(1)}, u32[]{:S(2)}, u32[]{:S(2)}) collective-permute-start(bf16[4,72,512]{2,1,0:T(8,128)(2,1)S(1)} %shard_map.53.refs_1_), channel_id=1, source_target_pairs={{0,8},{1,9},{2,10},{3,11},{4,12},{5,13},{6,14},{7,15},{8,0},{9,1},... | collective-permute-start | bytes 884744 | tf_op jit(solution)/shard_map/ppermute | solution.py:375
  53.6 8.8 %collective-permute-start.27 = (bf16[4,72,512]{2,1,0:T(8,128)(2,1)S(1)}, bf16[4,72,512]{2,1,0:T(8,128)(2,1)S(1)}, u32[]{:S(2)}, u32[]{:S(2)}) collective-permute-start(bf16[4,72,512]{2,1,0:T(8,128)(2,1)S(1)} %shard_map.52.refs_0_), channel_id=1, source_target_pairs={{0,1},{1,0},{2,3},{3,2},{4,5},{5,4},{6,7},{7,6},{8,16},{9,17},{10,... | collective-permute-start | bytes 884744 | tf_op jit(solution)/shard_map/ppermute | solution.py:375
  53.6 12.0 %collective-permute-start.28 = (bf16[4,72,512]{2,1,0:T(8,128)(2,1)S(1)}, bf16[4,72,512]{2,1,0:T(8,128)(2,1)S(1)}, u32[]{:S(2)}, u32[]{:S(2)}) collective-permute-start(bf16[4,72,512]{2,1,0:T(8,128)(2,1)S(1)} %shard_map.53.refs_1_), channel_id=1, source_target_pairs={{0,1},{1,0},{2,3},{3,2},{4,5},{5,4},{6,7},{7,6},{8,16},{9,17},{10,... | collective-permute-start | bytes 884744 | tf_op jit(solution)/shard_map/ppermute | solution.py:375
  56.9 14.1 %collective-permute-start.15 = (bf16[4,72,512]{2,1,0:T(8,128)(2,1)S(1)}, bf16[4,72,512]{2,1,0:T(8,128)(2,1)S(1)}, u32[]{:S(2)}, u32[]{:S(2)}) collective-permute-start(bf16[4,72,512]{2,1,0:T(8,128)(2,1)S(1)} %collective-permute-done.14.refs_2_), channel_id=1, source_target_pairs={{0,1},{1,0},{2,3},{3,2},{4,5},{5,4},{6,7},{7,6},{8,16},{9,17},{10,... | collective-permute-start | bytes 884744 | tf_op jit(solution)/shard_map/ppermute | solution.py:375
  62.4 14.9 %collective-permute-start.25 = (bf16[4,72,512]{2,1,0:T(8,128)(2,1)S(1)}, bf16[4,72,512]{2,1,0:T(8,128)(2,1)S(1)}, u32[]{:S(2)}, u32[]{:S(2)}) collective-permute-start(bf16[4,72,512]{2,1,0:T(8,128)(2,1)S(1)} %collective-permute-done.24.refs_3_), channel_id=1, source_target_pairs={{0,1},{1,0},{2,3},{3,2},{4,5},{5,4},{6,7},{7,6},{8,16},{9,17},{10,... | collective-permute-start | bytes 884744 | tf_op jit(solution)/shard_map/ppermute | solution.py:375
  62.4 20.2 %collective-permute-start.29 = (bf16[4,72,512]{2,1,0:T(8,128)(2,1)S(1)}, bf16[4,72,512]{2,1,0:T(8,128)(2,1)S(1)}, u32[]{:S(2)}, u32[]{:S(2)}) collective-permute-start(bf16[4,72,512]{2,1,0:T(8,128)(2,1)S(1)} %collective-permute-done.27.refs_4_), channel_id=1, source_target_pairs={{0,8},{1,9},{2,10},{3,11},{4,12},{5,13},{6,14},{7,15},{8,0},{9,1},... | collective-permute-start | bytes 884744 | tf_op jit(solution)/shard_map/ppermute | solution.py:375
  65.7 16.9 %collective-permute-start.30 = (bf16[4,72,512]{2,1,0:T(8,128)(2,1)S(1)}, bf16[4,72,512]{2,1,0:T(8,128)(2,1)S(1)}, u32[]{:S(2)}, u32[]{:S(2)}) collective-permute-start(bf16[4,72,512]{2,1,0:T(8,128)(2,1)S(1)} %collective-permute-done.28.refs_5_), channel_id=1, source_target_pairs={{0,8},{1,9},{2,10},{3,11},{4,12},{5,13},{6,14},{7,15},{8,0},{9,1},... | collective-permute-start | bytes 884744 | tf_op jit(solution)/shard_map/ppermute | solution.py:375
  71.0 15.2 %collective-permute-start.16 = (bf16[4,72,512]{2,1,0:T(8,128)(2,1)S(1)}, bf16[4,72,512]{2,1,0:T(8,128)(2,1)S(1)}, u32[]{:S(2)}, u32[]{:S(2)}) collective-permute-start(bf16[4,72,512]{2,1,0:T(8,128)(2,1)S(1)} %collective-permute-done.15.refs_6_), channel_id=1, source_target_pairs={{0,8},{1,9},{2,10},{3,11},{4,12},{5,13},{6,14},{7,15},{8,0},{9,1},... | collective-permute-start | bytes 884744 | tf_op jit(solution)/shard_map/ppermute | solution.py:375
  77.3 13.6 %collective-permute-start.26 = (bf16[4,72,512]{2,1,0:T(8,128)(2,1)S(1)}, bf16[4,72,512]{2,1,0:T(8,128)(2,1)S(1)}, u32[]{:S(2)}, u32[]{:S(2)}) collective-permute-start(bf16[4,72,512]{2,1,0:T(8,128)(2,1)S(1)} %collective-permute-done.25.refs_7_), channel_id=1, source_target_pairs={{0,8},{1,9},{2,10},{3,11},{4,12},{5,13},{6,14},{7,15},{8,0},{9,1},... | collective-permute-start | bytes 884744 | tf_op jit(solution)/shard_map/ppermute | solution.py:375

commit v3 on v2

--- a/solution.py
+++ b/solution.py
@@ -128,18 +128,21 @@
     flights += [pltpu.make_async_copy(grads_hbm.at[k], grads.at[k], sems.at[k]) for k in range(count)]
     for flight in flights:
         flight.start()
-    for flight in flights:
-        flight.wait()
-    for d, out in enumerate(outs):
-        matrix = table[group, me ^ d]
-
-        @pl.when(matrix < count)
-        def _():
-            out[...] = grads[jnp.minimum(matrix, count - 1)].astype(jnp.bfloat16)
+    flights[0].wait()
+    held = [table[group, me ^ d] for d in range(len(outs))]
+    for matrix, out in zip(held, outs):
 
         @pl.when(matrix >= count)
         def _():
             out[...] = jnp.zeros(out.shape, out.dtype)
+
+    for k in range(count):
+        flights[k + 1].wait()
+        for matrix, out in zip(held, outs):
+
+            @pl.when(matrix == k)
+            def _():
+                out[...] = grads[k].astype(jnp.bfloat16)
 
 
 def mix_block(me, d, at, block, momentum, staged, stage_at, new_momentum, sem, blend):

time: 91.8 us -> 91.7 us (level)
  no operation moved by 1% of the time
where the time goes in v3:
time: 91.7 us; the launch traced here: 91.5 us
  starting transfers between devices  42.1 us (46%)
  waiting for transfers between devices  35.7 us (39%)
  Pallas kernels  13 us (14%)
    ppermute x10, starting transfers between devices, chunked_body(): lax.ppermute(behind, ('rep', 'own'), pairs[(stream + step + 1) % 2])  23.9 us
    ppermute x21, waiting for transfers between devices, swap(): return lax.ppermute(x, 'own', [(i, i ^ d) for i in range(own)])  20.3 us
    ppermute x21, starting transfers between devices, swap(): return lax.ppermute(x, 'own', [(i, i ^ d) for i in range(own)])  18.2 us
    ppermute x10, waiting for transfers between devices, chunked_body(): lax.ppermute(behind, ('rep', 'own'), pairs[(stream + step + 1) % 2])  15.3 us
    pallas_call x1, Pallas kernels, chunked_body(): pl.pallas_call(functools.partial(update_kernel, arrival, first), in_specs...  5.86 us
    pallas_call x2, Pallas kernels, place(): pl.pallas_call(functools.partial(place_kernel, reps, where), in_specs=[VM...  2.11 us
  transfers between devices with their start and end apart: 31, of which 15 were waited for; matrix products, arithmetic and copies ran while one was open for 0% of the time, Pallas kernels for 5%

profile of v3, /device:TPU:0, one launch (start us, length us, event | category | flops | bytes accessed | tf_op | source)
XLA Modules:
  0.0 91.5 jit_solution(14692350412338695356)
XLA Ops:
  0.6 1.4 %pack.1 = (bf16[72,1024]{1,0:T(8,128)(2,1)S(1)}, bf16[72,1024]{1,0:T(8,128)(2,1)S(1)}, bf16[72,1024]{1,0:T(8,128)(2,1)S(1)}, bf16[72,1024]{1,0:T(8,128)(2,1)S(1)...) custom-call(s32[4,8]{1,0:T(4,128)} %table.3, ...), custom_call_target="tpu_custom_call" | custom-call | tf_op jit(solution)/shard_map/pack/pallas_call | solution.py:290
  2.0 0.6 collective-permute-start.4
  2.6 3.5 %collective-permute-start.5 = (bf16[72,1024]{1,0:T(8,128)(2,1)S(1)}, bf16[72,1024]{1,0:T(8,128)(2,1)S(1)}, u32[]{:S(2)}, u32[]{:S(2)}) collective-permute-start(bf16[72,1024]{1,0:T(8,128)(2,1)S(1)} %get-tuple-element.38), channel_id=1, source_target_pairs={{0,6},{1,7},{2,4},{3,5},{4,2},{5,3},{6,0},{7,1},{8,14},{9,15},{10,... | collective-permute-start | bytes 442376 | tf_op jit(solution)/shard_map/ppermute | solution.py:288
  6.1 0.0 collective-permute-start.6
  6.2 1.7 %collective-permute-start.2 = (bf16[72,1024]{1,0:T(8,128)(2,1)S(1)}, bf16[72,1024]{1,0:T(8,128)(2,1)S(1)}, u32[]{:S(2)}, u32[]{:S(2)}) collective-permute-start(bf16[72,1024]{1,0:T(8,128)(2,1)S(1)} %get-tuple-element.34), channel_id=1, source_target_pairs={{0,2},{1,3},{2,0},{3,1},{4,6},{5,7},{6,4},{7,5},{8,10},{9,11},{10,... | collective-permute-start | bytes 442376 | tf_op jit(solution)/shard_map/ppermute | solution.py:288
  7.8 1.5 %collective-permute-start.3 = (bf16[72,1024]{1,0:T(8,128)(2,1)S(1)}, bf16[72,1024]{1,0:T(8,128)(2,1)S(1)}, u32[]{:S(2)}, u32[]{:S(2)}) collective-permute-start(bf16[72,1024]{1,0:T(8,128)(2,1)S(1)} %get-tuple-element.35), channel_id=1, source_target_pairs={{0,4},{1,5},{2,6},{3,7},{4,0},{5,1},{6,2},{7,3},{8,12},{9,13},{10,... | collective-permute-start | bytes 442376 | tf_op jit(solution)/shard_map/ppermute | solution.py:288
  9.4 0.0 collective-permute-done.4.refs_1_
  9.4 0.0 collective-permute-start
  9.4 1.5 %collective-permute-done.5.refs_2_ = bf16[72,1024]{1,0:T(8,128)(2,1)S(1)} collective-permute-done((bf16[72,1024]{1,0:T(8,128)(2,1)S(1)}, bf16[72,1024]{1,0:T(8,128)(2,1)S(1)}, u32[]{:S(2)}, u32[]{:S(2)}) %collective-permute-start.5) | collective-permute-done | bytes 147488 | tf_op jit(solution)/shard_map/ppermute | solution.py:288
  10.9 0.6 collective-permute-start.1
  11.5 2.1 %collective-permute-done.6.refs_3_ = bf16[72,1024]{1,0:T(8,128)(2,1)S(1)} collective-permute-done((bf16[72,1024]{1,0:T(8,128)(2,1)S(1)}, bf16[72,1024]{1,0:T(8,128)(2,1)S(1)}, u32[]{:S(2)}, u32[]{:S(2)}) %collective-permute-start.6) | collective-permute-done | bytes 147488 | tf_op jit(solution)/shard_map/ppermute | solution.py:288
  13.6 0.9 shard_map.50
  14.5 3.2 %collective-permute-done.2.refs_0_ = bf16[72,1024]{1,0:T(8,128)(2,1)S(1)} collective-permute-done((bf16[72,1024]{1,0:T(8,128)(2,1)S(1)}, bf16[72,1024]{1,0:T(8,128)(2,1)S(1)}, u32[]{:S(2)}, u32[]{:S(2)}) %collective-permute-start.2) | collective-permute-done | bytes 147488 | tf_op jit(solution)/shard_map/ppermute | solution.py:288
  17.7 0.0 collective-permute-done.3.refs_1_
  17.7 0.8 shard_map.51
  18.5 1.3 %collective-permute-done.refs_0_ = bf16[72,1024]{1,0:T(8,128)(2,1)S(1)} collective-permute-done((bf16[72,1024]{1,0:T(8,128)(2,1)S(1)}, bf16[72,1024]{1,0:T(8,128)(2,1)S(1)}, u32[]{:S(2)}, u32[]{:S(2)}) %collective-permute-start) | collective-permute-done | bytes 147488 | tf_op jit(solution)/shard_map/ppermute | solution.py:288
  19.8 0.2 collective-permute-done.1.refs_1_
  20.0 5.9 %update.1 = (bf16[8,72,1024]{2,1,0:T(8,128)(2,1)}, bf16[576,1024]{1,0:T(8,128)(2,1)S(1)}, bf16[576,1024]{1,0:T(8,128)(2,1)S(1)}, bf16[576,576]{1,0:T(8,128)(2,1)...) custom-call(bf16[72,1024]{1,0:T(8,128)(2,1)S(1)} %collective-permute, ...), custom_call_target="tpu_custom_call", output_to_operand_aliasing={{0}: (3, {}), {1}: (4, {})} | custom-call | tf_op jit(solution)/shard_map/update/pallas_call | solution.py:331
  25.8 0.0 copy-start.1
  25.8 2.7 %collective-permute-start.12 = (bf16[2,72,512]{2,1,0:T(8,128)(2,1)S(1)}, bf16[2,72,512]{2,1,0:T(8,128)(2,1)S(1)}, u32[]{:S(2)}, u32[]{:S(2)}) collective-permute-start(bf16[2,72,512]{2,1,0:T(8,128)(2,1)S(1)} %get-tuple-element.53), channel_id=1, source_target_pairs={{0,6},{1,7},{2,4},{3,5},{4,2},{5,3},{6,0},{7,1},{8,14},{9,15},{10,... | collective-permute-start | bytes 442376 | tf_op jit(solution)/shard_map/ppermute | solution.py:288
  28.5 0.0 collective-permute-start.7
  28.5 0.6 rest.1
  29.2 0.6 collective-permute-start.18
  29.8 0.3 collective-permute-start.20
  30.1 1.7 %collective-permute-start.8 = (bf16[72,512]{1,0:T(8,128)(2,1)S(1)}, bf16[72,512]{1,0:T(8,128)(2,1)S(1)}, u32[]{:S(2)}, u32[]{:S(2)}) collective-permute-start(bf16[72,512]{1,0:T(8,128)(2,1)S(1)} %get-tuple-element.49), channel_id=1, source_target_pairs={{0,2},{1,3},{2,0},{3,1},{4,6},{5,7},{6,4},{7,5},{8,10},{9,11},{10,... | collective-permute-start | bytes 221192 | tf_op jit(solution)/shard_map/ppermute | solution.py:288
  31.8 0.0 collective-permute-done.7.refs_1_
  31.8 0.0 collective-permute-start.9
  31.8 1.5 %collective-permute-done.12.refs_6_ = bf16[2,72,512]{2,1,0:T(8,128)(2,1)S(1)} collective-permute-done((bf16[2,72,512]{2,1,0:T(8,128)(2,1)S(1)}, bf16[2,72,512]{2,1,0:T(8,128)(2,1)S(1)}, u32[]{:S(2)}, u32[]{:S(2)}) %collective-permute-start.12) | collective-permute-done | bytes 147488 | tf_op jit(solution)/shard_map/ppermute | solution.py:288
  33.2 5.0 %collective-permute-done.8.refs_2_ = bf16[72,512]{1,0:T(8,128)(2,1)S(1)} collective-permute-done((bf16[72,512]{1,0:T(8,128)(2,1)S(1)}, bf16[72,512]{1,0:T(8,128)(2,1)S(1)}, u32[]{:S(2)}, u32[]{:S(2)}) %collective-permute-start.8) | collective-permute-done | bytes 73760 | tf_op jit(solution)/shard_map/ppermute | solution.py:288
  38.2 0.3 collective-permute-start.10
  38.5 0.1 collective-permute-done.9.refs_3_
  38.7 0.4 collective-permute-start.11
  39.1 0.0 collective-permute-done.18.refs_2_
  39.1 1.3 %collective-permute-start.19 = (bf16[2,72,512]{2,1,0:T(8,128)(2,1)S(1)}, bf16[2,72,512]{2,1,0:T(8,128)(2,1)S(1)}, u32[]{:S(2)}, u32[]{:S(2)}) collective-permute-start(bf16[2,72,512]{2,1,0:T(8,128)(2,1)S(1)} %collective-permute-done.18.refs_2_), channel_id=1, source_target_pairs={{0,1},{1,0},{2,3},{3,2},{4,5},{5,4},{6,7},{7,6},{8,9},{9,8},{10,11... | collective-permute-start | bytes 442376 | tf_op jit(solution)/shard_map/ppermute | solution.py:288
  40.4 0.1 collective-permute-start.21
  40.4 2.8 %collective-permute-done.10.refs_4_ = bf16[72,512]{1,0:T(8,128)(2,1)S(1)} collective-permute-done((bf16[72,512]{1,0:T(8,128)(2,1)S(1)}, bf16[72,512]{1,0:T(8,128)(2,1)S(1)}, u32[]{:S(2)}, u32[]{:S(2)}) %collective-permute-start.10) | collective-permute-done | bytes 73760 | tf_op jit(solution)/shard_map/ppermute | solution.py:288
  43.2 2.6 %collective-permute-start.22 = (bf16[72,512]{1,0:T(8,128)(2,1)S(1)}, bf16[72,512]{1,0:T(8,128)(2,1)S(1)}, u32[]{:S(2)}, u32[]{:S(2)}) collective-permute-start(bf16[72,512]{1,0:T(8,128)(2,1)S(1)} %get-tuple-element.60), channel_id=1, source_target_pairs={{0,6},{1,7},{2,4},{3,5},{4,2},{5,3},{6,0},{7,1},{8,14},{9,15},{10,... | collective-permute-start | bytes 221192 | tf_op jit(solution)/shard_map/ppermute | solution.py:288
  45.8 0.3 collective-permute-start.23
  46.1 0.7 shard_map.52.refs_0_
  46.8 0.0 collective-permute-done.17.refs_1_
  46.8 1.7 %collective-permute-start.14 = (bf16[4,72,512]{2,1,0:T(8,128)(2,1)S(1)}, bf16[4,72,512]{2,1,0:T(8,128)(2,1)S(1)}, u32[]{:S(2)}, u32[]{:S(2)}) collective-permute-start(bf16[4,72,512]{2,1,0:T(8,128)(2,1)S(1)} %shard_map.52.refs_0_), channel_id=1, source_target_pairs={{0,8},{1,9},{2,10},{3,11},{4,12},{5,13},{6,14},{7,15},{8,0},{9,1},... | collective-permute-start | bytes 884744 | tf_op jit(solution)/shard_map/ppermute | solution.py:378
  48.5 0.4 collective-permute-done.22.refs_6_
  48.9 2.2 %collective-permute-done.23.refs_7_ = bf16[72,512]{1,0:T(8,128)(2,1)S(1)} collective-permute-done((bf16[72,512]{1,0:T(8,128)(2,1)S(1)}, bf16[72,512]{1,0:T(8,128)(2,1)S(1)}, u32[]{:S(2)}, u32[]{:S(2)}) %collective-permute-start.23) | collective-permute-done | bytes 73760 | tf_op jit(solution)/shard_map/ppermute | solution.py:288
  51.1 0.0 collective-permute-done.19.refs_3_
  51.1 0.0 collective-permute-done.21.refs_5_
  51.1 0.7 shard_map.53.refs_1_
  51.8 1.6 %collective-permute-start.24 = (bf16[4,72,512]{2,1,0:T(8,128)(2,1)S(1)}, bf16[4,72,512]{2,1,0:T(8,128)(2,1)S(1)}, u32[]{:S(2)}, u32[]{:S(2)}) collective-permute-start(bf16[4,72,512]{2,1,0:T(8,128)(2,1)S(1)} %shard_map.53.refs_1_), channel_id=1, source_target_pairs={{0,8},{1,9},{2,10},{3,11},{4,12},{5,13},{6,14},{7,15},{8,0},{9,1},... | collective-permute-start | bytes 884744 | tf_op jit(solution)/shard_map/ppermute | solution.py:378
  53.4 0.0 collective-permute-start.27
  53.4 0.5 collective-permute-start.28
  54.0 2.8 %collective-permute-done.14.refs_2_ = bf16[4,72,512]{2,1,0:T(8,128)(2,1)S(1)} collective-permute-done((bf16[4,72,512]{2,1,0:T(8,128)(2,1)S(1)}, bf16[4,72,512]{2,1,0:T(8,128)(2,1)S(1)}, u32[]{:S(2)}, u32[]{:S(2)}) %collective-permute-start.14) | collective-permute-done | bytes 294944 | tf_op jit(solution)/shard_map/ppermute | solution.py:378
  56.7 0.0 collective-permute-start.15
  56.7 5.5 %collective-permute-done.24.refs_3_ = bf16[4,72,512]{2,1,0:T(8,128)(2,1)S(1)} collective-permute-done((bf16[4,72,512]{2,1,0:T(8,128)(2,1)S(1)}, bf16[4,72,512]{2,1,0:T(8,128)(2,1)S(1)}, u32[]{:S(2)}, u32[]{:S(2)}) %collective-permute-start.24) | collective-permute-done | bytes 294944 | tf_op jit(solution)/shard_map/ppermute | solution.py:378
  62.3 0.0 collective-permute-done.27.refs_4_
  62.3 3.2 %collective-permute-start.29 = (bf16[4,72,512]{2,1,0:T(8,128)(2,1)S(1)}, bf16[4,72,512]{2,1,0:T(8,128)(2,1)S(1)}, u32[]{:S(2)}, u32[]{:S(2)}) collective-permute-start(bf16[4,72,512]{2,1,0:T(8,128)(2,1)S(1)} %collective-permute-done.27.refs_4_), channel_id=1, source_target_pairs={{0,8},{1,9},{2,10},{3,11},{4,12},{5,13},{6,14},{7,15},{8,0},{9,1},... | collective-permute-start | bytes 884744 | tf_op jit(solution)/shard_map/ppermute | solution.py:378
  65.5 0.0 collective-permute-done.28.refs_5_
  65.5 5.3 %collective-permute-start.30 = (bf16[4,72,512]{2,1,0:T(8,128)(2,1)S(1)}, bf16[4,72,512]{2,1,0:T(8,128)(2,1)S(1)}, u32[]{:S(2)}, u32[]{:S(2)}) collective-permute-start(bf16[4,72,512]{2,1,0:T(8,128)(2,1)S(1)} %collective-permute-done.28.refs_5_), channel_id=1, source_target_pairs={{0,8},{1,9},{2,10},{3,11},{4,12},{5,13},{6,14},{7,15},{8,0},{9,1},... | collective-permute-start | bytes 884744 | tf_op jit(solution)/shard_map/ppermute | solution.py:378
  70.8 6.3 %collective-permute-start.16 = (bf16[4,72,512]{2,1,0:T(8,128)(2,1)S(1)}, bf16[4,72,512]{2,1,0:T(8,128)(2,1)S(1)}, u32[]{:S(2)}, u32[]{:S(2)}) collective-permute-start(bf16[4,72,512]{2,1,0:T(8,128)(2,1)S(1)} %collective-permute-done.15.refs_6_), channel_id=1, source_target_pairs={{0,8},{1,9},{2,10},{3,11},{4,12},{5,13},{6,14},{7,15},{8,0},{9,1},... | collective-permute-start | bytes 884744 | tf_op jit(solution)/shard_map/ppermute | solution.py:378
  77.1 5.3 %collective-permute-start.26 = (bf16[4,72,512]{2,1,0:T(8,128)(2,1)S(1)}, bf16[4,72,512]{2,1,0:T(8,128)(2,1)S(1)}, u32[]{:S(2)}, u32[]{:S(2)}) collective-permute-start(bf16[4,72,512]{2,1,0:T(8,128)(2,1)S(1)} %collective-permute-done.25.refs_7_), channel_id=1, source_target_pairs={{0,8},{1,9},{2,10},{3,11},{4,12},{5,13},{6,14},{7,15},{8,0},{9,1},... | collective-permute-start | bytes 884744 | tf_op jit(solution)/shard_map/ppermute | solution.py:378
  82.4 0.0 collective-permute-done.29.refs_8_
  82.4 0.0 collective-permute-done.30.refs_9_
  82.4 1.3 %shard_map.54.refs_2_ = bf16[16,72,1024]{2,1,0:T(8,128)(2,1)} custom-call(bf16[4,72,512]{2,1,0:T(8,128)(2,1)S(1)} %shard_map.52.refs_0_, bf16[4,72,512]{2,1,0:T(8,128)(2,1)S(1)} %shard_map.53.refs_1_, bf16[4,72,512]{2,1,0:T(8,128)(2,1)S(1)} %collective-permute-done.14.refs_2_, bf16[4,72,512]{2,1,0:T(8,128)(2,1)S(1)} %collective-permute-done.24.refs_3_, ...), custom_call_target="tpu_custom_call" | custom-call | tf_op jit(solution)/shard_map/pallas_call | solution.py:268
  83.7 2.3 %collective-permute-done.16.refs_0_ = bf16[4,72,512]{2,1,0:T(8,128)(2,1)S(1)} collective-permute-done((bf16[4,72,512]{2,1,0:T(8,128)(2,1)S(1)}, bf16[4,72,512]{2,1,0:T(8,128)(2,1)S(1)}, u32[]{:S(2)}, u32[]{:S(2)}) %collective-permute-start.16) | collective-permute-done | bytes 294944 | tf_op jit(solution)/shard_map/ppermute | solution.py:378
  86.0 4.7 %collective-permute-done.26.refs_1_ = bf16[4,72,512]{2,1,0:T(8,128)(2,1)S(1)} collective-permute-done((bf16[4,72,512]{2,1,0:T(8,128)(2,1)S(1)}, bf16[4,72,512]{2,1,0:T(8,128)(2,1)S(1)}, u32[]{:S(2)}, u32[]{:S(2)}) %collective-permute-start.26) | collective-permute-done | bytes 294944 | tf_op jit(solution)/shard_map/ppermute | solution.py:378
  90.7 0.8 shard_map.55
  (11 shorter events, 0.0 us)
Async XLA Ops:
  0.6 12.9 %copy-start = (bf16[1,576,1024]{2,1,0:T(8,128)(2,1)S(1)}, bf16[1,576,1024]{2,1,0:T(8,128)(2,1)}, u32[]{:S(2)}) copy-start(bf16[1,576,1024]{2,1,0:T(8,128)(2,1)} %param.4) | copy-start | bytes 3538948
  2.0 7.3 %collective-permute-start.4 = (bf16[72,1024]{1,0:T(8,128)(2,1)S(1)}, bf16[72,1024]{1,0:T(8,128)(2,1)S(1)}, u32[]{:S(2)}, u32[]{:S(2)}) collective-permute-start(bf16[72,1024]{1,0:T(8,128)(2,1)S(1)} %get-tuple-element.37), channel_id=1, source_target_pairs={{0,1},{1,0},{2,3},{3,2},{4,5},{5,4},{6,7},{7,6},{8,9},{9,8},{10,11... | collective-permute-start | bytes 442376 | tf_op jit(solution)/shard_map/ppermute | solution.py:288
  2.6 8.3 %collective-permute-start.5 = (bf16[72,1024]{1,0:T(8,128)(2,1)S(1)}, bf16[72,1024]{1,0:T(8,128)(2,1)S(1)}, u32[]{:S(2)}, u32[]{:S(2)}) collective-permute-start(bf16[72,1024]{1,0:T(8,128)(2,1)S(1)} %get-tuple-element.38), channel_id=1, source_target_pairs={{0,6},{1,7},{2,4},{3,5},{4,2},{5,3},{6,0},{7,1},{8,14},{9,15},{10,... | collective-permute-start | bytes 442376 | tf_op jit(solution)/shard_map/ppermute | solution.py:288
  6.1 7.4 %collective-permute-start.6 = (bf16[72,1024]{1,0:T(8,128)(2,1)S(1)}, bf16[72,1024]{1,0:T(8,128)(2,1)S(1)}, u32[]{:S(2)}, u32[]{:S(2)}) collective-permute-start(bf16[72,1024]{1,0:T(8,128)(2,1)S(1)} %get-tuple-element.39), channel_id=1, source_target_pairs={{0,7},{1,6},{2,5},{3,4},{4,3},{5,2},{6,1},{7,0},{8,15},{9,14},{10,... | collective-permute-start | bytes 442376 | tf_op jit(solution)/shard_map/ppermute | solution.py:288
  6.2 11.5 %collective-permute-start.2 = (bf16[72,1024]{1,0:T(8,128)(2,1)S(1)}, bf16[72,1024]{1,0:T(8,128)(2,1)S(1)}, u32[]{:S(2)}, u32[]{:S(2)}) collective-permute-start(bf16[72,1024]{1,0:T(8,128)(2,1)S(1)} %get-tuple-element.34), channel_id=1, source_target_pairs={{0,2},{1,3},{2,0},{3,1},{4,6},{5,7},{6,4},{7,5},{8,10},{9,11},{10,... | collective-permute-start | bytes 442376 | tf_op jit(solution)/shard_map/ppermute | solution.py:288
  7.8 9.9 %collective-permute-start.3 = (bf16[72,1024]{1,0:T(8,128)(2,1)S(1)}, bf16[72,1024]{1,0:T(8,128)(2,1)S(1)}, u32[]{:S(2)}, u32[]{:S(2)}) collective-permute-start(bf16[72,1024]{1,0:T(8,128)(2,1)S(1)} %get-tuple-element.35), channel_id=1, source_target_pairs={{0,4},{1,5},{2,6},{3,7},{4,0},{5,1},{6,2},{7,3},{8,12},{9,13},{10,... | collective-permute-start | bytes 442376 | tf_op jit(solution)/shard_map/ppermute | solution.py:288
  9.4 10.4 %collective-permute-start = (bf16[72,1024]{1,0:T(8,128)(2,1)S(1)}, bf16[72,1024]{1,0:T(8,128)(2,1)S(1)}, u32[]{:S(2)}, u32[]{:S(2)}) collective-permute-start(bf16[72,1024]{1,0:T(8,128)(2,1)S(1)} %get-tuple-element.32), channel_id=1, source_target_pairs={{0,3},{1,2},{2,1},{3,0},{4,7},{5,6},{6,5},{7,4},{8,11},{9,10},{10,... | collective-permute-start | bytes 442376 | tf_op jit(solution)/shard_map/ppermute | solution.py:288
  10.9 9.1 %collective-permute-start.1 = (bf16[72,1024]{1,0:T(8,128)(2,1)S(1)}, bf16[72,1024]{1,0:T(8,128)(2,1)S(1)}, u32[]{:S(2)}, u32[]{:S(2)}) collective-permute-start(bf16[72,1024]{1,0:T(8,128)(2,1)S(1)} %get-tuple-element.33), channel_id=1, source_target_pairs={{0,5},{1,4},{2,7},{3,6},{4,1},{5,0},{6,3},{7,2},{8,13},{9,12},{10,... | collective-permute-start | bytes 442376 | tf_op jit(solution)/shard_map/ppermute | solution.py:288
  25.8 20.3 %copy-start.1 = (s32[4,8]{1,0:T(4,128)S(1)}, s32[4,8]{1,0:T(4,128)}, u32[]{:S(2)}) copy-start(s32[4,8]{1,0:T(4,128)} %table.3) | copy-start | bytes 388
  25.8 7.4 %collective-permute-start.12 = (bf16[2,72,512]{2,1,0:T(8,128)(2,1)S(1)}, bf16[2,72,512]{2,1,0:T(8,128)(2,1)S(1)}, u32[]{:S(2)}, u32[]{:S(2)}) collective-permute-start(bf16[2,72,512]{2,1,0:T(8,128)(2,1)S(1)} %get-tuple-element.53), channel_id=1, source_target_pairs={{0,6},{1,7},{2,4},{3,5},{4,2},{5,3},{6,0},{7,1},{8,14},{9,15},{10,... | collective-permute-start | bytes 442376 | tf_op jit(solution)/shard_map/ppermute | solution.py:288
  28.5 3.2 %collective-permute-start.7 = (bf16[72,512]{1,0:T(8,128)(2,1)S(1)}, bf16[72,512]{1,0:T(8,128)(2,1)S(1)}, u32[]{:S(2)}, u32[]{:S(2)}) collective-permute-start(bf16[72,512]{1,0:T(8,128)(2,1)S(1)} %get-tuple-element.48), channel_id=1, source_target_pairs={{0,1},{1,0},{2,3},{3,2},{4,5},{5,4},{6,7},{7,6},{8,9},{9,8},{10,11... | collective-permute-start | bytes 221192 | tf_op jit(solution)/shard_map/ppermute | solution.py:288
  29.2 9.9 %collective-permute-start.18 = (bf16[2,72,512]{2,1,0:T(8,128)(2,1)S(1)}, bf16[2,72,512]{2,1,0:T(8,128)(2,1)S(1)}, u32[]{:S(2)}, u32[]{:S(2)}) collective-permute-start(bf16[2,72,512]{2,1,0:T(8,128)(2,1)S(1)} %get-tuple-element.58), channel_id=1, source_target_pairs={{0,2},{1,3},{2,0},{3,1},{4,6},{5,7},{6,4},{7,5},{8,10},{9,11},{10,... | collective-permute-start | bytes 442376 | tf_op jit(solution)/shard_map/ppermute | solution.py:288
  29.8 10.6 %collective-permute-start.20 = (bf16[2,72,512]{2,1,0:T(8,128)(2,1)S(1)}, bf16[2,72,512]{2,1,0:T(8,128)(2,1)S(1)}, u32[]{:S(2)}, u32[]{:S(2)}) collective-permute-start(bf16[2,72,512]{2,1,0:T(8,128)(2,1)S(1)} %get-tuple-element.59), channel_id=1, source_target_pairs={{0,4},{1,5},{2,6},{3,7},{4,0},{5,1},{6,2},{7,3},{8,12},{9,13},{10,... | collective-permute-start | bytes 442376 | tf_op jit(solution)/shard_map/ppermute | solution.py:288
  30.1 8.1 %collective-permute-start.8 = (bf16[72,512]{1,0:T(8,128)(2,1)S(1)}, bf16[72,512]{1,0:T(8,128)(2,1)S(1)}, u32[]{:S(2)}, u32[]{:S(2)}) collective-permute-start(bf16[72,512]{1,0:T(8,128)(2,1)S(1)} %get-tuple-element.49), channel_id=1, source_target_pairs={{0,2},{1,3},{2,0},{3,1},{4,6},{5,7},{6,4},{7,5},{8,10},{9,11},{10,... | collective-permute-start | bytes 221192 | tf_op jit(solution)/shard_map/ppermute | solution.py:288
  31.8 6.9 %collective-permute-start.9 = (bf16[72,512]{1,0:T(8,128)(2,1)S(1)}, bf16[72,512]{1,0:T(8,128)(2,1)S(1)}, u32[]{:S(2)}, u32[]{:S(2)}) collective-permute-start(bf16[72,512]{1,0:T(8,128)(2,1)S(1)} %get-tuple-element.50), channel_id=1, source_target_pairs={{0,3},{1,2},{2,1},{3,0},{4,7},{5,6},{6,5},{7,4},{8,11},{9,10},{10,... | collective-permute-start | bytes 221192 | tf_op jit(solution)/shard_map/ppermute | solution.py:288
  33.2 12.6 %collective-permute-start.13 = (bf16[2,72,512]{2,1,0:T(8,128)(2,1)S(1)}, bf16[2,72,512]{2,1,0:T(8,128)(2,1)S(1)}, u32[]{:S(2)}, u32[]{:S(2)}) collective-permute-start(bf16[2,72,512]{2,1,0:T(8,128)(2,1)S(1)} %collective-permute-done.12.refs_6_), channel_id=1, source_target_pairs={{0,1},{1,0},{2,3},{3,2},{4,5},{5,4},{6,7},{7,6},{8,9},{9,8},{10,11... | collective-permute-start | bytes 442376 | tf_op jit(solution)/shard_map/ppermute | solution.py:288
  38.2 5.0 %collective-permute-start.10 = (bf16[72,512]{1,0:T(8,128)(2,1)S(1)}, bf16[72,512]{1,0:T(8,128)(2,1)S(1)}, u32[]{:S(2)}, u32[]{:S(2)}) collective-permute-start(bf16[72,512]{1,0:T(8,128)(2,1)S(1)} %get-tuple-element.51), channel_id=1, source_target_pairs={{0,4},{1,5},{2,6},{3,7},{4,0},{5,1},{6,2},{7,3},{8,12},{9,13},{10,... | collective-permute-start | bytes 221192 | tf_op jit(solution)/shard_map/ppermute | solution.py:288
  38.7 4.6 %collective-permute-start.11 = (bf16[72,512]{1,0:T(8,128)(2,1)S(1)}, bf16[72,512]{1,0:T(8,128)(2,1)S(1)}, u32[]{:S(2)}, u32[]{:S(2)}) collective-permute-start(bf16[72,512]{1,0:T(8,128)(2,1)S(1)} %get-tuple-element.52), channel_id=1, source_target_pairs={{0,5},{1,4},{2,7},{3,6},{4,1},{5,0},{6,3},{7,2},{8,13},{9,12},{10,... | collective-permute-start | bytes 221192 | tf_op jit(solution)/shard_map/ppermute | solution.py:288
  39.1 12.0 %collective-permute-start.19 = (bf16[2,72,512]{2,1,0:T(8,128)(2,1)S(1)}, bf16[2,72,512]{2,1,0:T(8,128)(2,1)S(1)}, u32[]{:S(2)}, u32[]{:S(2)}) collective-permute-start(bf16[2,72,512]{2,1,0:T(8,128)(2,1)S(1)} %collective-permute-done.18.refs_2_), channel_id=1, source_target_pairs={{0,1},{1,0},{2,3},{3,2},{4,5},{5,4},{6,7},{7,6},{8,9},{9,8},{10,11... | collective-permute-start | bytes 442376 | tf_op jit(solution)/shard_map/ppermute | solution.py:288
  40.4 10.8 %collective-permute-start.21 = (bf16[2,72,512]{2,1,0:T(8,128)(2,1)S(1)}, bf16[2,72,512]{2,1,0:T(8,128)(2,1)S(1)}, u32[]{:S(2)}, u32[]{:S(2)}) collective-permute-start(bf16[2,72,512]{2,1,0:T(8,128)(2,1)S(1)} %collective-permute-done.20.refs_4_), channel_id=1, source_target_pairs={{0,1},{1,0},{2,3},{3,2},{4,5},{5,4},{6,7},{7,6},{8,9},{9,8},{10,11... | collective-permute-start | bytes 442376 | tf_op jit(solution)/shard_map/ppermute | solution.py:288
  43.2 3.5 %collective-permute-start.17 = (bf16[72,512]{1,0:T(8,128)(2,1)S(1)}, bf16[72,512]{1,0:T(8,128)(2,1)S(1)}, u32[]{:S(2)}, u32[]{:S(2)}) collective-permute-start(bf16[72,512]{1,0:T(8,128)(2,1)S(1)} %get-tuple-element.57), channel_id=1, source_target_pairs={{0,1},{1,0},{2,3},{3,2},{4,5},{5,4},{6,7},{7,6},{8,9},{9,8},{10,11... | collective-permute-start | bytes 221192 | tf_op jit(solution)/shard_map/ppermute | solution.py:288
  43.2 5.7 %collective-permute-start.22 = (bf16[72,512]{1,0:T(8,128)(2,1)S(1)}, bf16[72,512]{1,0:T(8,128)(2,1)S(1)}, u32[]{:S(2)}, u32[]{:S(2)}) collective-permute-start(bf16[72,512]{1,0:T(8,128)(2,1)S(1)} %get-tuple-element.60), channel_id=1, source_target_pairs={{0,6},{1,7},{2,4},{3,5},{4,2},{5,3},{6,0},{7,1},{8,14},{9,15},{10,... | collective-permute-start | bytes 221192 | tf_op jit(solution)/shard_map/ppermute | solution.py:288
  45.8 5.3 %collective-permute-start.23 = (bf16[72,512]{1,0:T(8,128)(2,1)S(1)}, bf16[72,512]{1,0:T(8,128)(2,1)S(1)}, u32[]{:S(2)}, u32[]{:S(2)}) collective-permute-start(bf16[72,512]{1,0:T(8,128)(2,1)S(1)} %get-tuple-element.61), channel_id=1, source_target_pairs={{0,7},{1,6},{2,5},{3,4},{4,3},{5,2},{6,1},{7,0},{8,15},{9,14},{10,... | collective-permute-start | bytes 221192 | tf_op jit(solution)/shard_map/ppermute | solution.py:288
  46.8 9.9 %collective-permute-start.14 = (bf16[4,72,512]{2,1,0:T(8,128)(2,1)S(1)}, bf16[4,72,512]{2,1,0:T(8,128)(2,1)S(1)}, u32[]{:S(2)}, u32[]{:S(2)}) collective-permute-start(bf16[4,72,512]{2,1,0:T(8,128)(2,1)S(1)} %shard_map.52.refs_0_), channel_id=1, source_target_pairs={{0,8},{1,9},{2,10},{3,11},{4,12},{5,13},{6,14},{7,15},{8,0},{9,1},... | collective-permute-start | bytes 884744 | tf_op jit(solution)/shard_map/ppermute | solution.py:378
  51.8 10.5 %collective-permute-start.24 = (bf16[4,72,512]{2,1,0:T(8,128)(2,1)S(1)}, bf16[4,72,512]{2,1,0:T(8,128)(2,1)S(1)}, u32[]{:S(2)}, u32[]{:S(2)}) collective-permute-start(bf16[4,72,512]{2,1,0:T(8,128)(2,1)S(1)} %shard_map.53.refs_1_), channel_id=1, source_target_pairs={{0,8},{1,9},{2,10},{3,11},{4,12},{5,13},{6,14},{7,15},{8,0},{9,1},... | collective-permute-start | bytes 884744 | tf_op jit(solution)/shard_map/ppermute | solution.py:378
  53.4 8.8 %collective-permute-start.27 = (bf16[4,72,512]{2,1,0:T(8,128)(2,1)S(1)}, bf16[4,72,512]{2,1,0:T(8,128)(2,1)S(1)}, u32[]{:S(2)}, u32[]{:S(2)}) collective-permute-start(bf16[4,72,512]{2,1,0:T(8,128)(2,1)S(1)} %shard_map.52.refs_0_), channel_id=1, source_target_pairs={{0,1},{1,0},{2,3},{3,2},{4,5},{5,4},{6,7},{7,6},{8,16},{9,17},{10,... | collective-permute-start | bytes 884744 | tf_op jit(solution)/shard_map/ppermute | solution.py:378
  53.4 12.1 %collective-permute-start.28 = (bf16[4,72,512]{2,1,0:T(8,128)(2,1)S(1)}, bf16[4,72,512]{2,1,0:T(8,128)(2,1)S(1)}, u32[]{:S(2)}, u32[]{:S(2)}) collective-permute-start(bf16[4,72,512]{2,1,0:T(8,128)(2,1)S(1)} %shard_map.53.refs_1_), channel_id=1, source_target_pairs={{0,1},{1,0},{2,3},{3,2},{4,5},{5,4},{6,7},{7,6},{8,16},{9,17},{10,... | collective-permute-start | bytes 884744 | tf_op jit(solution)/shard_map/ppermute | solution.py:378
  56.7 14.0 %collective-permute-start.15 = (bf16[4,72,512]{2,1,0:T(8,128)(2,1)S(1)}, bf16[4,72,512]{2,1,0:T(8,128)(2,1)S(1)}, u32[]{:S(2)}, u32[]{:S(2)}) collective-permute-start(bf16[4,72,512]{2,1,0:T(8,128)(2,1)S(1)} %collective-permute-done.14.refs_2_), channel_id=1, source_target_pairs={{0,1},{1,0},{2,3},{3,2},{4,5},{5,4},{6,7},{7,6},{8,16},{9,17},{10,... | collective-permute-start | bytes 884744 | tf_op jit(solution)/shard_map/ppermute | solution.py:378
  62.3 14.8 %collective-permute-start.25 = (bf16[4,72,512]{2,1,0:T(8,128)(2,1)S(1)}, bf16[4,72,512]{2,1,0:T(8,128)(2,1)S(1)}, u32[]{:S(2)}, u32[]{:S(2)}) collective-permute-start(bf16[4,72,512]{2,1,0:T(8,128)(2,1)S(1)} %collective-permute-done.24.refs_3_), channel_id=1, source_target_pairs={{0,1},{1,0},{2,3},{3,2},{4,5},{5,4},{6,7},{7,6},{8,16},{9,17},{10,... | collective-permute-start | bytes 884744 | tf_op jit(solution)/shard_map/ppermute | solution.py:378
  62.3 20.1 %collective-permute-start.29 = (bf16[4,72,512]{2,1,0:T(8,128)(2,1)S(1)}, bf16[4,72,512]{2,1,0:T(8,128)(2,1)S(1)}, u32[]{:S(2)}, u32[]{:S(2)}) collective-permute-start(bf16[4,72,512]{2,1,0:T(8,128)(2,1)S(1)} %collective-permute-done.27.refs_4_), channel_id=1, source_target_pairs={{0,8},{1,9},{2,10},{3,11},{4,12},{5,13},{6,14},{7,15},{8,0},{9,1},... | collective-permute-start | bytes 884744 | tf_op jit(solution)/shard_map/ppermute | solution.py:378
  65.5 16.9 %collective-permute-start.30 = (bf16[4,72,512]{2,1,0:T(8,128)(2,1)S(1)}, bf16[4,72,512]{2,1,0:T(8,128)(2,1)S(1)}, u32[]{:S(2)}, u32[]{:S(2)}) collective-permute-start(bf16[4,72,512]{2,1,0:T(8,128)(2,1)S(1)} %collective-permute-done.28.refs_5_), channel_id=1, source_target_pairs={{0,8},{1,9},{2,10},{3,11},{4,12},{5,13},{6,14},{7,15},{8,0},{9,1},... | collective-permute-start | bytes 884744 | tf_op jit(solution)/shard_map/ppermute | solution.py:378
  70.8 15.2 %collective-permute-start.16 = (bf16[4,72,512]{2,1,0:T(8,128)(2,1)S(1)}, bf16[4,72,512]{2,1,0:T(8,128)(2,1)S(1)}, u32[]{:S(2)}, u32[]{:S(2)}) collective-permute-start(bf16[4,72,512]{2,1,0:T(8,128)(2,1)S(1)} %collective-permute-done.15.refs_6_), channel_id=1, source_target_pairs={{0,8},{1,9},{2,10},{3,11},{4,12},{5,13},{6,14},{7,15},{8,0},{9,1},... | collective-permute-start | bytes 884744 | tf_op jit(solution)/shard_map/ppermute | solution.py:378
  77.1 13.6 %collective-permute-start.26 = (bf16[4,72,512]{2,1,0:T(8,128)(2,1)S(1)}, bf16[4,72,512]{2,1,0:T(8,128)(2,1)S(1)}, u32[]{:S(2)}, u32[]{:S(2)}) collective-permute-start(bf16[4,72,512]{2,1,0:T(8,128)(2,1)S(1)} %collective-permute-done.25.refs_7_), channel_id=1, source_target_pairs={{0,8},{1,9},{2,10},{3,11},{4,12},{5,13},{6,14},{7,15},{8,0},{9,1},... | collective-permute-start | bytes 884744 | tf_op jit(solution)/shard_map/ppermute | solution.py:378

commit v4 on v3

--- a/solution.py
+++ b/solution.py
@@ -21,7 +21,7 @@
 COEF_C = 2.0315
 EPSILON = 1e-07
 
-ORDER = (6, 7, 2, 4, 3, 5, 1)
+ORDER = (6, 7, 4, 2, 5, 3, 1)
 
 
 VMEM = pl.BlockSpec(memory_space=pltpu.VMEM)
@@ -380,7 +380,8 @@
     last = [key for key in held if key[1:] == steps[-1]]
     soon = [key for key in held if key not in last]
     updates = place(reps, soon, [held[key] for key in soon], shape, None)
-    updates = place(reps, last, [held[key] for key in last], shape, updates)
+    for key in last:
+        updates = place(reps, [key], [held[key]], shape, updates)
     return (new_momentum.reshape(1, own * rows, columns), updates)
 
 

time: 91.7 us -> 91.6 us (level)
    pallas_call x2 -> x3, Pallas kernels: 2.11 us -> 2.73 us  [place(): pl.pallas_call(functools.partial(place_kernel, reps, where), in_specs=[VM...]
  transfers between devices with their start and end apart: 31 -> 31, of which waited for: 15 -> 15; matrix products, arithmetic and copies ran while one was open for 0% -> 0% of each run, Pallas kernels for 5% -> 6%
where the time goes in v4:
time: 91.6 us; the launch traced here: 91.4 us
  starting transfers between devices  41.9 us (46%)
  waiting for transfers between devices  35.1 us (38%)
  Pallas kernels  13.6 us (15%)
    ppermute x10, starting transfers between devices, chunked_body(): lax.ppermute(behind, ('rep', 'own'), pairs[(stream + step + 1) % 2])  23.9 us
    ppermute x21, waiting for transfers between devices, swap(): return lax.ppermute(x, 'own', [(i, i ^ d) for i in range(own)])  20.5 us
    ppermute x21, starting transfers between devices, swap(): return lax.ppermute(x, 'own', [(i, i ^ d) for i in range(own)])  18 us
    ppermute x10, waiting for transfers between devices, chunked_body(): lax.ppermute(behind, ('rep', 'own'), pairs[(stream + step + 1) % 2])  14.6 us
    pallas_call x1, Pallas kernels, chunked_body(): pl.pallas_call(functools.partial(update_kernel, arrival, first), in_specs...  5.85 us
    pallas_call x3, Pallas kernels, place(): pl.pallas_call(functools.partial(place_kernel, reps, where), in_specs=[VM...  2.73 us
  transfers between devices with their start and end apart: 31, of which 15 were waited for; matrix products, arithmetic and copies ran while one was open for 0% of the time, Pallas kernels for 6%

profile of v4, /device:TPU:0, one launch (start us, length us, event | category | flops | bytes accessed | tf_op | source)
XLA Modules:
  0.0 91.4 jit_solution(12031903742706492381)
XLA Ops:
  0.6 1.4 %pack.1 = (bf16[72,1024]{1,0:T(8,128)(2,1)S(1)}, bf16[72,1024]{1,0:T(8,128)(2,1)S(1)}, bf16[72,1024]{1,0:T(8,128)(2,1)S(1)}, bf16[72,1024]{1,0:T(8,128)(2,1)S(1)...) custom-call(s32[4,8]{1,0:T(4,128)} %table.3, ...), custom_call_target="tpu_custom_call" | custom-call | tf_op jit(solution)/shard_map/pack/pallas_call | solution.py:290
  2.0 0.6 collective-permute-start.4
  2.6 3.5 %collective-permute-start.5 = (bf16[72,1024]{1,0:T(8,128)(2,1)S(1)}, bf16[72,1024]{1,0:T(8,128)(2,1)S(1)}, u32[]{:S(2)}, u32[]{:S(2)}) collective-permute-start(bf16[72,1024]{1,0:T(8,128)(2,1)S(1)} %get-tuple-element.38), channel_id=1, source_target_pairs={{0,6},{1,7},{2,4},{3,5},{4,2},{5,3},{6,0},{7,1},{8,14},{9,15},{10,... | collective-permute-start | bytes 442376 | tf_op jit(solution)/shard_map/ppermute | solution.py:288
  6.1 0.0 collective-permute-start.6
  6.2 1.7 %collective-permute-start.2 = (bf16[72,1024]{1,0:T(8,128)(2,1)S(1)}, bf16[72,1024]{1,0:T(8,128)(2,1)S(1)}, u32[]{:S(2)}, u32[]{:S(2)}) collective-permute-start(bf16[72,1024]{1,0:T(8,128)(2,1)S(1)} %get-tuple-element.34), channel_id=1, source_target_pairs={{0,4},{1,5},{2,6},{3,7},{4,0},{5,1},{6,2},{7,3},{8,12},{9,13},{10,... | collective-permute-start | bytes 442376 | tf_op jit(solution)/shard_map/ppermute | solution.py:288
  7.9 1.5 %collective-permute-start.3 = (bf16[72,1024]{1,0:T(8,128)(2,1)S(1)}, bf16[72,1024]{1,0:T(8,128)(2,1)S(1)}, u32[]{:S(2)}, u32[]{:S(2)}) collective-permute-start(bf16[72,1024]{1,0:T(8,128)(2,1)S(1)} %get-tuple-element.35), channel_id=1, source_target_pairs={{0,2},{1,3},{2,0},{3,1},{4,6},{5,7},{6,4},{7,5},{8,10},{9,11},{10,... | collective-permute-start | bytes 442376 | tf_op jit(solution)/shard_map/ppermute | solution.py:288
  9.4 0.0 collective-permute-done.4.refs_1_
  9.4 1.5 %collective-permute-done.5.refs_2_ = bf16[72,1024]{1,0:T(8,128)(2,1)S(1)} collective-permute-done((bf16[72,1024]{1,0:T(8,128)(2,1)S(1)}, bf16[72,1024]{1,0:T(8,128)(2,1)S(1)}, u32[]{:S(2)}, u32[]{:S(2)}) %collective-permute-start.5) | collective-permute-done | bytes 147488 | tf_op jit(solution)/shard_map/ppermute | solution.py:288
  10.9 0.5 collective-permute-start.1
  11.4 2.2 %collective-permute-done.6.refs_3_ = bf16[72,1024]{1,0:T(8,128)(2,1)S(1)} collective-permute-done((bf16[72,1024]{1,0:T(8,128)(2,1)S(1)}, bf16[72,1024]{1,0:T(8,128)(2,1)S(1)}, u32[]{:S(2)}, u32[]{:S(2)}) %collective-permute-start.6) | collective-permute-done | bytes 147488 | tf_op jit(solution)/shard_map/ppermute | solution.py:288
  13.6 0.9 shard_map.50
  14.5 2.5 %collective-permute-done.2.refs_0_ = bf16[72,1024]{1,0:T(8,128)(2,1)S(1)} collective-permute-done((bf16[72,1024]{1,0:T(8,128)(2,1)S(1)}, bf16[72,1024]{1,0:T(8,128)(2,1)S(1)}, u32[]{:S(2)}, u32[]{:S(2)}) %collective-permute-start.2) | collective-permute-done | bytes 147488 | tf_op jit(solution)/shard_map/ppermute | solution.py:288
  16.9 0.8 collective-permute-done.3.refs_1_
  17.7 0.8 shard_map.51
  18.5 1.5 %collective-permute-done.refs_0_ = bf16[72,1024]{1,0:T(8,128)(2,1)S(1)} collective-permute-done((bf16[72,1024]{1,0:T(8,128)(2,1)S(1)}, bf16[72,1024]{1,0:T(8,128)(2,1)S(1)}, u32[]{:S(2)}, u32[]{:S(2)}) %collective-permute-start) | collective-permute-done | bytes 147488 | tf_op jit(solution)/shard_map/ppermute | solution.py:288
  20.0 5.8 %update.1 = (bf16[8,72,1024]{2,1,0:T(8,128)(2,1)}, bf16[576,1024]{1,0:T(8,128)(2,1)S(1)}, bf16[576,1024]{1,0:T(8,128)(2,1)S(1)}, bf16[576,576]{1,0:T(8,128)(2,1)...) custom-call(bf16[72,1024]{1,0:T(8,128)(2,1)S(1)} %collective-permute, ...), custom_call_target="tpu_custom_call", output_to_operand_aliasing={{0}: (3, {}), {1}: (4, {})} | custom-call | tf_op jit(solution)/shard_map/update/pallas_call | solution.py:331
  25.8 0.0 copy-start.1
  25.9 2.7 %collective-permute-start.22 = (bf16[2,72,512]{2,1,0:T(8,128)(2,1)S(1)}, bf16[2,72,512]{2,1,0:T(8,128)(2,1)S(1)}, u32[]{:S(2)}, u32[]{:S(2)}) collective-permute-start(bf16[2,72,512]{2,1,0:T(8,128)(2,1)S(1)} %get-tuple-element.61), channel_id=1, source_target_pairs={{0,6},{1,7},{2,4},{3,5},{4,2},{5,3},{6,0},{7,1},{8,14},{9,15},{10,... | collective-permute-start | bytes 442376 | tf_op jit(solution)/shard_map/ppermute | solution.py:288
  28.6 0.0 collective-permute-start.17
  28.6 0.6 rest.1
  29.2 0.6 collective-permute-start.8
  29.8 0.3 collective-permute-start.10
  30.1 1.7 %collective-permute-start.18 = (bf16[72,512]{1,0:T(8,128)(2,1)S(1)}, bf16[72,512]{1,0:T(8,128)(2,1)S(1)}, u32[]{:S(2)}, u32[]{:S(2)}) collective-permute-start(bf16[72,512]{1,0:T(8,128)(2,1)S(1)} %get-tuple-element.57), channel_id=1, source_target_pairs={{0,2},{1,3},{2,0},{3,1},{4,6},{5,7},{6,4},{7,5},{8,10},{9,11},{10,... | collective-permute-start | bytes 221192 | tf_op jit(solution)/shard_map/ppermute | solution.py:288
  31.8 0.0 collective-permute-done.17.refs_1_
  31.8 0.0 collective-permute-start.19
  31.8 1.4 %collective-permute-done.22.refs_6_ = bf16[2,72,512]{2,1,0:T(8,128)(2,1)S(1)} collective-permute-done((bf16[2,72,512]{2,1,0:T(8,128)(2,1)S(1)}, bf16[2,72,512]{2,1,0:T(8,128)(2,1)S(1)}, u32[]{:S(2)}, u32[]{:S(2)}) %collective-permute-start.22) | collective-permute-done | bytes 147488 | tf_op jit(solution)/shard_map/ppermute | solution.py:288
  33.2 5.1 %collective-permute-done.18.refs_2_ = bf16[72,512]{1,0:T(8,128)(2,1)S(1)} collective-permute-done((bf16[72,512]{1,0:T(8,128)(2,1)S(1)}, bf16[72,512]{1,0:T(8,128)(2,1)S(1)}, u32[]{:S(2)}, u32[]{:S(2)}) %collective-permute-start.18) | collective-permute-done | bytes 73760 | tf_op jit(solution)/shard_map/ppermute | solution.py:288
  38.2 0.2 collective-permute-start.20
  38.5 0.2 collective-permute-done.19.refs_3_
  38.7 0.4 collective-permute-start.21
  39.1 0.0 collective-permute-done.8.refs_2_
  39.1 1.3 %collective-permute-start.9 = (bf16[2,72,512]{2,1,0:T(8,128)(2,1)S(1)}, bf16[2,72,512]{2,1,0:T(8,128)(2,1)S(1)}, u32[]{:S(2)}, u32[]{:S(2)}) collective-permute-start(bf16[2,72,512]{2,1,0:T(8,128)(2,1)S(1)} %collective-permute-done.8.refs_2_), channel_id=1, source_target_pairs={{0,1},{1,0},{2,3},{3,2},{4,5},{5,4},{6,7},{7,6},{8,9},{9,8},{10,11... | collective-permute-start | bytes 442376 | tf_op jit(solution)/shard_map/ppermute | solution.py:288
  40.4 0.1 collective-permute-start.11
  40.5 2.8 %collective-permute-done.20.refs_4_ = bf16[72,512]{1,0:T(8,128)(2,1)S(1)} collective-permute-done((bf16[72,512]{1,0:T(8,128)(2,1)S(1)}, bf16[72,512]{1,0:T(8,128)(2,1)S(1)}, u32[]{:S(2)}, u32[]{:S(2)}) %collective-permute-start.20) | collective-permute-done | bytes 73760 | tf_op jit(solution)/shard_map/ppermute | solution.py:288
  43.3 0.0 collective-permute-start.7
  43.3 0.0 collective-permute-done.21.refs_5_
  43.3 2.6 %collective-permute-start.12 = (bf16[72,512]{1,0:T(8,128)(2,1)S(1)}, bf16[72,512]{1,0:T(8,128)(2,1)S(1)}, u32[]{:S(2)}, u32[]{:S(2)}) collective-permute-start(bf16[72,512]{1,0:T(8,128)(2,1)S(1)} %get-tuple-element.53), channel_id=1, source_target_pairs={{0,6},{1,7},{2,4},{3,5},{4,2},{5,3},{6,0},{7,1},{8,14},{9,15},{10,... | collective-permute-start | bytes 221192 | tf_op jit(solution)/shard_map/ppermute | solution.py:288
  45.8 0.0 collective-permute-done.23.refs_7_
  45.8 0.3 collective-permute-start.13
  46.1 0.7 shard_map.53.refs_0_
  46.8 1.7 %collective-permute-start.24 = (bf16[4,72,512]{2,1,0:T(8,128)(2,1)S(1)}, bf16[4,72,512]{2,1,0:T(8,128)(2,1)S(1)}, u32[]{:S(2)}, u32[]{:S(2)}) collective-permute-start(bf16[4,72,512]{2,1,0:T(8,128)(2,1)S(1)} %shard_map.53.refs_0_), channel_id=1, source_target_pairs={{0,8},{1,9},{2,10},{3,11},{4,12},{5,13},{6,14},{7,15},{8,0},{9,1},... | collective-permute-start | bytes 884744 | tf_op jit(solution)/shard_map/ppermute | solution.py:378
  48.5 0.4 collective-permute-done.12.refs_6_
  48.9 2.2 %collective-permute-done.13.refs_7_ = bf16[72,512]{1,0:T(8,128)(2,1)S(1)} collective-permute-done((bf16[72,512]{1,0:T(8,128)(2,1)S(1)}, bf16[72,512]{1,0:T(8,128)(2,1)S(1)}, u32[]{:S(2)}, u32[]{:S(2)}) %collective-permute-start.13) | collective-permute-done | bytes 73760 | tf_op jit(solution)/shard_map/ppermute | solution.py:288
  51.1 0.0 collective-permute-done.9.refs_3_
  51.1 0.0 collective-permute-done.11.refs_5_
  51.1 0.7 shard_map.52.refs_1_
  51.8 1.6 %collective-permute-start.14 = (bf16[4,72,512]{2,1,0:T(8,128)(2,1)S(1)}, bf16[4,72,512]{2,1,0:T(8,128)(2,1)S(1)}, u32[]{:S(2)}, u32[]{:S(2)}) collective-permute-start(bf16[4,72,512]{2,1,0:T(8,128)(2,1)S(1)} %shard_map.52.refs_1_), channel_id=1, source_target_pairs={{0,8},{1,9},{2,10},{3,11},{4,12},{5,13},{6,14},{7,15},{8,0},{9,1},... | collective-permute-start | bytes 884744 | tf_op jit(solution)/shard_map/ppermute | solution.py:378
  53.5 0.0 collective-permute-start.27
  53.5 0.5 collective-permute-start.28
  54.0 2.8 %collective-permute-done.24.refs_2_ = bf16[4,72,512]{2,1,0:T(8,128)(2,1)S(1)} collective-permute-done((bf16[4,72,512]{2,1,0:T(8,128)(2,1)S(1)}, bf16[4,72,512]{2,1,0:T(8,128)(2,1)S(1)}, u32[]{:S(2)}, u32[]{:S(2)}) %collective-permute-start.24) | collective-permute-done | bytes 294944 | tf_op jit(solution)/shard_map/ppermute | solution.py:378
  56.8 5.5 %collective-permute-done.14.refs_3_ = bf16[4,72,512]{2,1,0:T(8,128)(2,1)S(1)} collective-permute-done((bf16[4,72,512]{2,1,0:T(8,128)(2,1)S(1)}, bf16[4,72,512]{2,1,0:T(8,128)(2,1)S(1)}, u32[]{:S(2)}, u32[]{:S(2)}) %collective-permute-start.14) | collective-permute-done | bytes 294944 | tf_op jit(solution)/shard_map/ppermute | solution.py:378
  62.3 0.0 collective-permute-start.15
  62.3 0.0 collective-permute-done.27.refs_4_
  62.3 3.2 %collective-permute-start.29 = (bf16[4,72,512]{2,1,0:T(8,128)(2,1)S(1)}, bf16[4,72,512]{2,1,0:T(8,128)(2,1)S(1)}, u32[]{:S(2)}, u32[]{:S(2)}) collective-permute-start(bf16[4,72,512]{2,1,0:T(8,128)(2,1)S(1)} %collective-permute-done.27.refs_4_), channel_id=1, source_target_pairs={{0,8},{1,9},{2,10},{3,11},{4,12},{5,13},{6,14},{7,15},{8,0},{9,1},... | collective-permute-start | bytes 884744 | tf_op jit(solution)/shard_map/ppermute | solution.py:378
  65.5 5.3 %collective-permute-start.30 = (bf16[4,72,512]{2,1,0:T(8,128)(2,1)S(1)}, bf16[4,72,512]{2,1,0:T(8,128)(2,1)S(1)}, u32[]{:S(2)}, u32[]{:S(2)}) collective-permute-start(bf16[4,72,512]{2,1,0:T(8,128)(2,1)S(1)} %collective-permute-done.28.refs_5_), channel_id=1, source_target_pairs={{0,8},{1,9},{2,10},{3,11},{4,12},{5,13},{6,14},{7,15},{8,0},{9,1},... | collective-permute-start | bytes 884744 | tf_op jit(solution)/shard_map/ppermute | solution.py:378
  70.8 0.0 collective-permute-done.25.refs_6_
  70.8 6.3 %collective-permute-start.26 = (bf16[4,72,512]{2,1,0:T(8,128)(2,1)S(1)}, bf16[4,72,512]{2,1,0:T(8,128)(2,1)S(1)}, u32[]{:S(2)}, u32[]{:S(2)}) collective-permute-start(bf16[4,72,512]{2,1,0:T(8,128)(2,1)S(1)} %collective-permute-done.25.refs_6_), channel_id=1, source_target_pairs={{0,8},{1,9},{2,10},{3,11},{4,12},{5,13},{6,14},{7,15},{8,0},{9,1},... | collective-permute-start | bytes 884744 | tf_op jit(solution)/shard_map/ppermute | solution.py:378
  77.1 0.0 collective-permute-done.15.refs_7_
  77.1 5.3 %collective-permute-start.16 = (bf16[4,72,512]{2,1,0:T(8,128)(2,1)S(1)}, bf16[4,72,512]{2,1,0:T(8,128)(2,1)S(1)}, u32[]{:S(2)}, u32[]{:S(2)}) collective-permute-start(bf16[4,72,512]{2,1,0:T(8,128)(2,1)S(1)} %collective-permute-done.15.refs_7_), channel_id=1, source_target_pairs={{0,8},{1,9},{2,10},{3,11},{4,12},{5,13},{6,14},{7,15},{8,0},{9,1},... | collective-permute-start | bytes 884744 | tf_op jit(solution)/shard_map/ppermute | solution.py:378
  82.4 1.3 %shard_map.54.refs_1_ = bf16[16,72,1024]{2,1,0:T(8,128)(2,1)} custom-call(bf16[4,72,512]{2,1,0:T(8,128)(2,1)S(1)} %shard_map.53.refs_0_, bf16[4,72,512]{2,1,0:T(8,128)(2,1)S(1)} %shard_map.52.refs_1_, bf16[4,72,512]{2,1,0:T(8,128)(2,1)S(1)} %collective-permute-done.24.refs_2_, bf16[4,72,512]{2,1,0:T(8,128)(2,1)S(1)} %collective-permute-done.14.refs_3_, ...), custom_call_target="tpu_custom_call" | custom-call | tf_op jit(solution)/shard_map/pallas_call | solution.py:268
  83.7 2.3 %collective-permute-done.26.refs_0_ = bf16[4,72,512]{2,1,0:T(8,128)(2,1)S(1)} collective-permute-done((bf16[4,72,512]{2,1,0:T(8,128)(2,1)S(1)}, bf16[4,72,512]{2,1,0:T(8,128)(2,1)S(1)}, u32[]{:S(2)}, u32[]{:S(2)}) %collective-permute-start.26) | collective-permute-done | bytes 294944 | tf_op jit(solution)/shard_map/ppermute | solution.py:378
  86.0 0.7 shard_map.55.refs_1_
  86.7 4.0 %collective-permute-done.16.refs_0_ = bf16[4,72,512]{2,1,0:T(8,128)(2,1)S(1)} collective-permute-done((bf16[4,72,512]{2,1,0:T(8,128)(2,1)S(1)}, bf16[4,72,512]{2,1,0:T(8,128)(2,1)S(1)}, u32[]{:S(2)}, u32[]{:S(2)}) %collective-permute-start.16) | collective-permute-done | bytes 294944 | tf_op jit(solution)/shard_map/ppermute | solution.py:378
  90.7 0.7 shard_map.56
  (12 shorter events, 0.0 us)
Async XLA Ops:
  0.6 12.9 %copy-start = (bf16[1,576,1024]{2,1,0:T(8,128)(2,1)S(1)}, bf16[1,576,1024]{2,1,0:T(8,128)(2,1)}, u32[]{:S(2)}) copy-start(bf16[1,576,1024]{2,1,0:T(8,128)(2,1)} %param.4) | copy-start | bytes 3538948
  2.0 7.3 %collective-permute-start.4 = (bf16[72,1024]{1,0:T(8,128)(2,1)S(1)}, bf16[72,1024]{1,0:T(8,128)(2,1)S(1)}, u32[]{:S(2)}, u32[]{:S(2)}) collective-permute-start(bf16[72,1024]{1,0:T(8,128)(2,1)S(1)} %get-tuple-element.37), channel_id=1, source_target_pairs={{0,1},{1,0},{2,3},{3,2},{4,5},{5,4},{6,7},{7,6},{8,9},{9,8},{10,11... | collective-permute-start | bytes 442376 | tf_op jit(solution)/shard_map/ppermute | solution.py:288
  2.6 8.3 %collective-permute-start.5 = (bf16[72,1024]{1,0:T(8,128)(2,1)S(1)}, bf16[72,1024]{1,0:T(8,128)(2,1)S(1)}, u32[]{:S(2)}, u32[]{:S(2)}) collective-permute-start(bf16[72,1024]{1,0:T(8,128)(2,1)S(1)} %get-tuple-element.38), channel_id=1, source_target_pairs={{0,6},{1,7},{2,4},{3,5},{4,2},{5,3},{6,0},{7,1},{8,14},{9,15},{10,... | collective-permute-start | bytes 442376 | tf_op jit(solution)/shard_map/ppermute | solution.py:288
  6.1 7.4 %collective-permute-start.6 = (bf16[72,1024]{1,0:T(8,128)(2,1)S(1)}, bf16[72,1024]{1,0:T(8,128)(2,1)S(1)}, u32[]{:S(2)}, u32[]{:S(2)}) collective-permute-start(bf16[72,1024]{1,0:T(8,128)(2,1)S(1)} %get-tuple-element.39), channel_id=1, source_target_pairs={{0,7},{1,6},{2,5},{3,4},{4,3},{5,2},{6,1},{7,0},{8,15},{9,14},{10,... | collective-permute-start | bytes 442376 | tf_op jit(solution)/shard_map/ppermute | solution.py:288
  6.2 10.8 %collective-permute-start.2 = (bf16[72,1024]{1,0:T(8,128)(2,1)S(1)}, bf16[72,1024]{1,0:T(8,128)(2,1)S(1)}, u32[]{:S(2)}, u32[]{:S(2)}) collective-permute-start(bf16[72,1024]{1,0:T(8,128)(2,1)S(1)} %get-tuple-element.34), channel_id=1, source_target_pairs={{0,4},{1,5},{2,6},{3,7},{4,0},{5,1},{6,2},{7,3},{8,12},{9,13},{10,... | collective-permute-start | bytes 442376 | tf_op jit(solution)/shard_map/ppermute | solution.py:288
  7.9 9.8 %collective-permute-start.3 = (bf16[72,1024]{1,0:T(8,128)(2,1)S(1)}, bf16[72,1024]{1,0:T(8,128)(2,1)S(1)}, u32[]{:S(2)}, u32[]{:S(2)}) collective-permute-start(bf16[72,1024]{1,0:T(8,128)(2,1)S(1)} %get-tuple-element.35), channel_id=1, source_target_pairs={{0,2},{1,3},{2,0},{3,1},{4,6},{5,7},{6,4},{7,5},{8,10},{9,11},{10,... | collective-permute-start | bytes 442376 | tf_op jit(solution)/shard_map/ppermute | solution.py:288
  9.4 10.6 %collective-permute-start = (bf16[72,1024]{1,0:T(8,128)(2,1)S(1)}, bf16[72,1024]{1,0:T(8,128)(2,1)S(1)}, u32[]{:S(2)}, u32[]{:S(2)}) collective-permute-start(bf16[72,1024]{1,0:T(8,128)(2,1)S(1)} %get-tuple-element.32), channel_id=1, source_target_pairs={{0,5},{1,4},{2,7},{3,6},{4,1},{5,0},{6,3},{7,2},{8,13},{9,12},{10,... | collective-permute-start | bytes 442376 | tf_op jit(solution)/shard_map/ppermute | solution.py:288
  10.9 9.1 %collective-permute-start.1 = (bf16[72,1024]{1,0:T(8,128)(2,1)S(1)}, bf16[72,1024]{1,0:T(8,128)(2,1)S(1)}, u32[]{:S(2)}, u32[]{:S(2)}) collective-permute-start(bf16[72,1024]{1,0:T(8,128)(2,1)S(1)} %get-tuple-element.33), channel_id=1, source_target_pairs={{0,3},{1,2},{2,1},{3,0},{4,7},{5,6},{6,5},{7,4},{8,11},{9,10},{10,... | collective-permute-start | bytes 442376 | tf_op jit(solution)/shard_map/ppermute | solution.py:288
  25.8 20.3 %copy-start.1 = (s32[4,8]{1,0:T(4,128)S(1)}, s32[4,8]{1,0:T(4,128)}, u32[]{:S(2)}) copy-start(s32[4,8]{1,0:T(4,128)} %table.3) | copy-start | bytes 388
  25.9 7.3 %collective-permute-start.22 = (bf16[2,72,512]{2,1,0:T(8,128)(2,1)S(1)}, bf16[2,72,512]{2,1,0:T(8,128)(2,1)S(1)}, u32[]{:S(2)}, u32[]{:S(2)}) collective-permute-start(bf16[2,72,512]{2,1,0:T(8,128)(2,1)S(1)} %get-tuple-element.61), channel_id=1, source_target_pairs={{0,6},{1,7},{2,4},{3,5},{4,2},{5,3},{6,0},{7,1},{8,14},{9,15},{10,... | collective-permute-start | bytes 442376 | tf_op jit(solution)/shard_map/ppermute | solution.py:288
  28.6 3.2 %collective-permute-start.17 = (bf16[72,512]{1,0:T(8,128)(2,1)S(1)}, bf16[72,512]{1,0:T(8,128)(2,1)S(1)}, u32[]{:S(2)}, u32[]{:S(2)}) collective-permute-start(bf16[72,512]{1,0:T(8,128)(2,1)S(1)} %get-tuple-element.56), channel_id=1, source_target_pairs={{0,1},{1,0},{2,3},{3,2},{4,5},{5,4},{6,7},{7,6},{8,9},{9,8},{10,11... | collective-permute-start | bytes 221192 | tf_op jit(solution)/shard_map/ppermute | solution.py:288
  29.2 9.8 %collective-permute-start.8 = (bf16[2,72,512]{2,1,0:T(8,128)(2,1)S(1)}, bf16[2,72,512]{2,1,0:T(8,128)(2,1)S(1)}, u32[]{:S(2)}, u32[]{:S(2)}) collective-permute-start(bf16[2,72,512]{2,1,0:T(8,128)(2,1)S(1)} %get-tuple-element.51), channel_id=1, source_target_pairs={{0,2},{1,3},{2,0},{3,1},{4,6},{5,7},{6,4},{7,5},{8,10},{9,11},{10,... | collective-permute-start | bytes 442376 | tf_op jit(solution)/shard_map/ppermute | solution.py:288
  29.8 10.6 %collective-permute-start.10 = (bf16[2,72,512]{2,1,0:T(8,128)(2,1)S(1)}, bf16[2,72,512]{2,1,0:T(8,128)(2,1)S(1)}, u32[]{:S(2)}, u32[]{:S(2)}) collective-permute-start(bf16[2,72,512]{2,1,0:T(8,128)(2,1)S(1)} %get-tuple-element.52), channel_id=1, source_target_pairs={{0,4},{1,5},{2,6},{3,7},{4,0},{5,1},{6,2},{7,3},{8,12},{9,13},{10,... | collective-permute-start | bytes 442376 | tf_op jit(solution)/shard_map/ppermute | solution.py:288
  30.1 8.1 %collective-permute-start.18 = (bf16[72,512]{1,0:T(8,128)(2,1)S(1)}, bf16[72,512]{1,0:T(8,128)(2,1)S(1)}, u32[]{:S(2)}, u32[]{:S(2)}) collective-permute-start(bf16[72,512]{1,0:T(8,128)(2,1)S(1)} %get-tuple-element.57), channel_id=1, source_target_pairs={{0,2},{1,3},{2,0},{3,1},{4,6},{5,7},{6,4},{7,5},{8,10},{9,11},{10,... | collective-permute-start | bytes 221192 | tf_op jit(solution)/shard_map/ppermute | solution.py:288
  31.8 6.9 %collective-permute-start.19 = (bf16[72,512]{1,0:T(8,128)(2,1)S(1)}, bf16[72,512]{1,0:T(8,128)(2,1)S(1)}, u32[]{:S(2)}, u32[]{:S(2)}) collective-permute-start(bf16[72,512]{1,0:T(8,128)(2,1)S(1)} %get-tuple-element.58), channel_id=1, source_target_pairs={{0,3},{1,2},{2,1},{3,0},{4,7},{5,6},{6,5},{7,4},{8,11},{9,10},{10,... | collective-permute-start | bytes 221192 | tf_op jit(solution)/shard_map/ppermute | solution.py:288
  33.2 12.6 %collective-permute-start.23 = (bf16[2,72,512]{2,1,0:T(8,128)(2,1)S(1)}, bf16[2,72,512]{2,1,0:T(8,128)(2,1)S(1)}, u32[]{:S(2)}, u32[]{:S(2)}) collective-permute-start(bf16[2,72,512]{2,1,0:T(8,128)(2,1)S(1)} %collective-permute-done.22.refs_6_), channel_id=1, source_target_pairs={{0,1},{1,0},{2,3},{3,2},{4,5},{5,4},{6,7},{7,6},{8,9},{9,8},{10,11... | collective-permute-start | bytes 442376 | tf_op jit(solution)/shard_map/ppermute | solution.py:288
  38.2 5.0 %collective-permute-start.20 = (bf16[72,512]{1,0:T(8,128)(2,1)S(1)}, bf16[72,512]{1,0:T(8,128)(2,1)S(1)}, u32[]{:S(2)}, u32[]{:S(2)}) collective-permute-start(bf16[72,512]{1,0:T(8,128)(2,1)S(1)} %get-tuple-element.59), channel_id=1, source_target_pairs={{0,4},{1,5},{2,6},{3,7},{4,0},{5,1},{6,2},{7,3},{8,12},{9,13},{10,... | collective-permute-start | bytes 221192 | tf_op jit(solution)/shard_map/ppermute | solution.py:288
  38.7 4.6 %collective-permute-start.21 = (bf16[72,512]{1,0:T(8,128)(2,1)S(1)}, bf16[72,512]{1,0:T(8,128)(2,1)S(1)}, u32[]{:S(2)}, u32[]{:S(2)}) collective-permute-start(bf16[72,512]{1,0:T(8,128)(2,1)S(1)} %get-tuple-element.60), channel_id=1, source_target_pairs={{0,5},{1,4},{2,7},{3,6},{4,1},{5,0},{6,3},{7,2},{8,13},{9,12},{10,... | collective-permute-start | bytes 221192 | tf_op jit(solution)/shard_map/ppermute | solution.py:288
  39.1 12.1 %collective-permute-start.9 = (bf16[2,72,512]{2,1,0:T(8,128)(2,1)S(1)}, bf16[2,72,512]{2,1,0:T(8,128)(2,1)S(1)}, u32[]{:S(2)}, u32[]{:S(2)}) collective-permute-start(bf16[2,72,512]{2,1,0:T(8,128)(2,1)S(1)} %collective-permute-done.8.refs_2_), channel_id=1, source_target_pairs={{0,1},{1,0},{2,3},{3,2},{4,5},{5,4},{6,7},{7,6},{8,9},{9,8},{10,11... | collective-permute-start | bytes 442376 | tf_op jit(solution)/shard_map/ppermute | solution.py:288
  40.4 10.7 %collective-permute-start.11 = (bf16[2,72,512]{2,1,0:T(8,128)(2,1)S(1)}, bf16[2,72,512]{2,1,0:T(8,128)(2,1)S(1)}, u32[]{:S(2)}, u32[]{:S(2)}) collective-permute-start(bf16[2,72,512]{2,1,0:T(8,128)(2,1)S(1)} %collective-permute-done.10.refs_4_), channel_id=1, source_target_pairs={{0,1},{1,0},{2,3},{3,2},{4,5},{5,4},{6,7},{7,6},{8,9},{9,8},{10,11... | collective-permute-start | bytes 442376 | tf_op jit(solution)/shard_map/ppermute | solution.py:288
  43.3 3.5 %collective-permute-start.7 = (bf16[72,512]{1,0:T(8,128)(2,1)S(1)}, bf16[72,512]{1,0:T(8,128)(2,1)S(1)}, u32[]{:S(2)}, u32[]{:S(2)}) collective-permute-start(bf16[72,512]{1,0:T(8,128)(2,1)S(1)} %get-tuple-element.50), channel_id=1, source_target_pairs={{0,1},{1,0},{2,3},{3,2},{4,5},{5,4},{6,7},{7,6},{8,9},{9,8},{10,11... | collective-permute-start | bytes 221192 | tf_op jit(solution)/shard_map/ppermute | solution.py:288
  43.3 5.7 %collective-permute-start.12 = (bf16[72,512]{1,0:T(8,128)(2,1)S(1)}, bf16[72,512]{1,0:T(8,128)(2,1)S(1)}, u32[]{:S(2)}, u32[]{:S(2)}) collective-permute-start(bf16[72,512]{1,0:T(8,128)(2,1)S(1)} %get-tuple-element.53), channel_id=1, source_target_pairs={{0,6},{1,7},{2,4},{3,5},{4,2},{5,3},{6,0},{7,1},{8,14},{9,15},{10,... | collective-permute-start | bytes 221192 | tf_op jit(solution)/shard_map/ppermute | solution.py:288
  45.8 5.3 %collective-permute-start.13 = (bf16[72,512]{1,0:T(8,128)(2,1)S(1)}, bf16[72,512]{1,0:T(8,128)(2,1)S(1)}, u32[]{:S(2)}, u32[]{:S(2)}) collective-permute-start(bf16[72,512]{1,0:T(8,128)(2,1)S(1)} %get-tuple-element.54), channel_id=1, source_target_pairs={{0,7},{1,6},{2,5},{3,4},{4,3},{5,2},{6,1},{7,0},{8,15},{9,14},{10,... | collective-permute-start | bytes 221192 | tf_op jit(solution)/shard_map/ppermute | solution.py:288
  46.8 9.9 %collective-permute-start.24 = (bf16[4,72,512]{2,1,0:T(8,128)(2,1)S(1)}, bf16[4,72,512]{2,1,0:T(8,128)(2,1)S(1)}, u32[]{:S(2)}, u32[]{:S(2)}) collective-permute-start(bf16[4,72,512]{2,1,0:T(8,128)(2,1)S(1)} %shard_map.53.refs_0_), channel_id=1, source_target_pairs={{0,8},{1,9},{2,10},{3,11},{4,12},{5,13},{6,14},{7,15},{8,0},{9,1},... | collective-permute-start | bytes 884744 | tf_op jit(solution)/shard_map/ppermute | solution.py:378
  51.8 10.5 %collective-permute-start.14 = (bf16[4,72,512]{2,1,0:T(8,128)(2,1)S(1)}, bf16[4,72,512]{2,1,0:T(8,128)(2,1)S(1)}, u32[]{:S(2)}, u32[]{:S(2)}) collective-permute-start(bf16[4,72,512]{2,1,0:T(8,128)(2,1)S(1)} %shard_map.52.refs_1_), channel_id=1, source_target_pairs={{0,8},{1,9},{2,10},{3,11},{4,12},{5,13},{6,14},{7,15},{8,0},{9,1},... | collective-permute-start | bytes 884744 | tf_op jit(solution)/shard_map/ppermute | solution.py:378
  53.5 8.9 %collective-permute-start.27 = (bf16[4,72,512]{2,1,0:T(8,128)(2,1)S(1)}, bf16[4,72,512]{2,1,0:T(8,128)(2,1)S(1)}, u32[]{:S(2)}, u32[]{:S(2)}) collective-permute-start(bf16[4,72,512]{2,1,0:T(8,128)(2,1)S(1)} %shard_map.53.refs_0_), channel_id=1, source_target_pairs={{0,1},{1,0},{2,3},{3,2},{4,5},{5,4},{6,7},{7,6},{8,16},{9,17},{10,... | collective-permute-start | bytes 884744 | tf_op jit(solution)/shard_map/ppermute | solution.py:378
  53.5 12.1 %collective-permute-start.28 = (bf16[4,72,512]{2,1,0:T(8,128)(2,1)S(1)}, bf16[4,72,512]{2,1,0:T(8,128)(2,1)S(1)}, u32[]{:S(2)}, u32[]{:S(2)}) collective-permute-start(bf16[4,72,512]{2,1,0:T(8,128)(2,1)S(1)} %shard_map.52.refs_1_), channel_id=1, source_target_pairs={{0,1},{1,0},{2,3},{3,2},{4,5},{5,4},{6,7},{7,6},{8,16},{9,17},{10,... | collective-permute-start | bytes 884744 | tf_op jit(solution)/shard_map/ppermute | solution.py:378
  56.8 14.0 %collective-permute-start.25 = (bf16[4,72,512]{2,1,0:T(8,128)(2,1)S(1)}, bf16[4,72,512]{2,1,0:T(8,128)(2,1)S(1)}, u32[]{:S(2)}, u32[]{:S(2)}) collective-permute-start(bf16[4,72,512]{2,1,0:T(8,128)(2,1)S(1)} %collective-permute-done.24.refs_2_), channel_id=1, source_target_pairs={{0,1},{1,0},{2,3},{3,2},{4,5},{5,4},{6,7},{7,6},{8,16},{9,17},{10,... | collective-permute-start | bytes 884744 | tf_op jit(solution)/shard_map/ppermute | solution.py:378
  62.3 14.8 %collective-permute-start.15 = (bf16[4,72,512]{2,1,0:T(8,128)(2,1)S(1)}, bf16[4,72,512]{2,1,0:T(8,128)(2,1)S(1)}, u32[]{:S(2)}, u32[]{:S(2)}) collective-permute-start(bf16[4,72,512]{2,1,0:T(8,128)(2,1)S(1)} %collective-permute-done.14.refs_3_), channel_id=1, source_target_pairs={{0,1},{1,0},{2,3},{3,2},{4,5},{5,4},{6,7},{7,6},{8,16},{9,17},{10,... | collective-permute-start | bytes 884744 | tf_op jit(solution)/shard_map/ppermute | solution.py:378
  62.3 20.1 %collective-permute-start.29 = (bf16[4,72,512]{2,1,0:T(8,128)(2,1)S(1)}, bf16[4,72,512]{2,1,0:T(8,128)(2,1)S(1)}, u32[]{:S(2)}, u32[]{:S(2)}) collective-permute-start(bf16[4,72,512]{2,1,0:T(8,128)(2,1)S(1)} %collective-permute-done.27.refs_4_), channel_id=1, source_target_pairs={{0,8},{1,9},{2,10},{3,11},{4,12},{5,13},{6,14},{7,15},{8,0},{9,1},... | collective-permute-start | bytes 884744 | tf_op jit(solution)/shard_map/ppermute | solution.py:378
  65.5 16.9 %collective-permute-start.30 = (bf16[4,72,512]{2,1,0:T(8,128)(2,1)S(1)}, bf16[4,72,512]{2,1,0:T(8,128)(2,1)S(1)}, u32[]{:S(2)}, u32[]{:S(2)}) collective-permute-start(bf16[4,72,512]{2,1,0:T(8,128)(2,1)S(1)} %collective-permute-done.28.refs_5_), channel_id=1, source_target_pairs={{0,8},{1,9},{2,10},{3,11},{4,12},{5,13},{6,14},{7,15},{8,0},{9,1},... | collective-permute-start | bytes 884744 | tf_op jit(solution)/shard_map/ppermute | solution.py:378
  70.8 15.2 %collective-permute-start.26 = (bf16[4,72,512]{2,1,0:T(8,128)(2,1)S(1)}, bf16[4,72,512]{2,1,0:T(8,128)(2,1)S(1)}, u32[]{:S(2)}, u32[]{:S(2)}) collective-permute-start(bf16[4,72,512]{2,1,0:T(8,128)(2,1)S(1)} %collective-permute-done.25.refs_6_), channel_id=1, source_target_pairs={{0,8},{1,9},{2,10},{3,11},{4,12},{5,13},{6,14},{7,15},{8,0},{9,1},... | collective-permute-start | bytes 884744 | tf_op jit(solution)/shard_map/ppermute | solution.py:378
  77.1 13.6 %collective-permute-start.16 = (bf16[4,72,512]{2,1,0:T(8,128)(2,1)S(1)}, bf16[4,72,512]{2,1,0:T(8,128)(2,1)S(1)}, u32[]{:S(2)}, u32[]{:S(2)}) collective-permute-start(bf16[4,72,512]{2,1,0:T(8,128)(2,1)S(1)} %collective-permute-done.15.refs_7_), channel_id=1, source_target_pairs={{0,8},{1,9},{2,10},{3,11},{4,12},{5,13},{6,14},{7,15},{8,0},{9,1},... | collective-permute-start | bytes 884744 | tf_op jit(solution)/shard_map/ppermute | solution.py:378
